TPU v7x, 32 devices: a whole 2x2x4 slice. The times are simulated.
32 devices in a mesh: tile: 8 (over z, y), slab: 4 (over x, core).
Axes of the slice: x: 2, y: 2, z: 4, core: 2. Of those that a mesh axis runs over, the one named last changes fastest.
Arguments:
- snapshots: float32 [64, 61440], P('tile', 'slab'), as said below
- old_basis: float32 [61440, 512], P(('slab', 'tile'))
- sing_values: float32 [512], replicated, may hold values from 2 to 8
Outputs:
- new_basis: bfloat16 [61440, 512], P(('slab', 'tile'))
Inputs may be any that keep to these rules, and one draw needn't show every extreme that they name: Each snapshot is a combination of the resident modes plus a residual part whose size differs strongly between snapshots and grows along the cells.
All inputs are finite; a program needn't handle non-finite values.
Results may differ from a plain program's by a relative error of at most 0.001.
Values sent between devices are 32-bit elements; how exact they have to be, the bound alone decides.
No kernel may reach another device: no remote copies, remote signals or barrier semaphores. Data moves between devices by JAX's collectives and lax.ppermute only.
A program may use at most 64 MiB of HBM per device.

v0:
```python
import jax
import jax.numpy as jnp
from jax import lax
from jax.experimental import pallas as pl
from jax.experimental.pallas import tpu as pltpu
from jax.sharding import PartitionSpec as P

HIGHEST = lax.Precision.HIGHEST
BLOCK = 128


def dot(left, right, contract=((1,), (0,)), precision=HIGHEST):
    return lax.dot_general(
        left, right, (contract, ((), ())), precision=precision, preferred_element_type=jnp.float32
    )


def factor_block(work):
    size = work.shape[0]
    lanes = lax.broadcasted_iota(jnp.int32, (8, size), 1)
    subs = lax.broadcasted_iota(jnp.int32, (8, size), 0)
    full = (8, size)
    for step in range(size // 8):
        base = 8 * step
        inside = (lanes >= base) & (lanes < base + 8)
        row = work[pl.ds(base, 8), :]
        cols = [jnp.broadcast_to(row[:, base + j : base + j + 1], full) for j in range(8)]
        entry = {
            (i, j): jnp.broadcast_to(cols[j][i : i + 1, :], full) for j in range(8) for i in range(j, 8)
        }
        ratio, recip = {}, []
        for j in range(8):
            recip.append(1.0 / entry[j, j])
            for k in range(j + 1, 8):
                ratio[j, k] = entry[k, j] * recip[j]
            for k in range(j + 1, 8):
                for i in range(k, 8):
                    entry[i, k] = entry[i, k] - entry[i, j] * ratio[j, k]
        pivots = entry[0, 0]
        for j in range(1, 8):
            pivots = jnp.where(subs == j, entry[j, j], pivots)
        for k in range(1, 8):
            for j in range(k):
                cols[k] = cols[k] - cols[j] * ratio[j, k]
        row = jnp.where(inside, jnp.where(lanes - base == subs, 1.0, 0.0), row)
        scaled = []
        for j in range(8):
            scaled.append(jnp.broadcast_to(row[j : j + 1, :], full) * recip[j])
            if j < 7:
                row = row - jnp.where(subs > j, cols[j], 0.0) * scaled[j]
        work[pl.ds(base, 8), :] = row * lax.rsqrt(pivots)
        for other in range(step + 1, size // 8):
            below = work[pl.ds(8 * other, 8), :]
            cols = [jnp.broadcast_to(below[:, base + j : base + j + 1], full) for j in range(8)]
            for k in range(1, 8):
                for j in range(k):
                    cols[k] = cols[k] - cols[j] * ratio[j, k]
            terms = [cols[j] * scaled[j] for j in range(8)]
            while len(terms) > 1:
                terms = [a + b for a, b in zip(terms[::2], terms[1::2])]
            work[pl.ds(8 * other, 8), :] = jnp.where(inside, 0.0, below) - terms[0]


def tril(value):
    rows = lax.broadcasted_iota(jnp.int32, value.shape, 0)
    return jnp.where(lax.broadcasted_iota(jnp.int32, value.shape, 1) <= rows, value, 0.0)


def factor_inverse(gram, work):
    size = gram.shape[0]
    count = size // BLOCK

    def step(index, carry):
        start = pl.multiple_of(index * BLOCK, BLOCK)
        here = pl.ds(start, BLOCK)
        work[...] = gram[here, here]
        factor_block(work)
        inverse = tril(work[...])
        gram[here, here] = jnp.eye(BLOCK, dtype=jnp.float32)
        for block in range(count):

            @pl.when(index == block)
            def _():
                low = BLOCK * block
                rest = size - low - BLOCK
                row = dot(inverse, gram[pl.ds(low, BLOCK), :])
                gram[pl.ds(low, BLOCK), :] = row
                if rest:
                    turned = row[:, low + BLOCK :].T
                    gram[pl.ds(low + BLOCK, rest), pl.ds(low, BLOCK)] = jnp.zeros(
                        (rest, BLOCK), jnp.float32
                    )
                    for other in range(0, rest, BLOCK):
                        rows = pl.ds(low + BLOCK + other, BLOCK)
                        gram[rows, :] = gram[rows, :] - dot(turned[other : other + BLOCK], row)

        return carry

    lax.fori_loop(0, count, step, 0)
    gram[...] = tril(gram[...])


def diagonal(value):
    rows = lax.broadcasted_iota(jnp.int32, value.shape, 0)
    cols = lax.broadcasted_iota(jnp.int32, value.shape, 1)
    return rows == cols


def half(value):
    rows = lax.broadcasted_iota(jnp.int32, value.shape, 0)
    cols = lax.broadcasted_iota(jnp.int32, value.shape, 1)
    return jnp.where(rows > cols, value, jnp.where(rows == cols, 0.5 * value, 0.0))


def dot3(left, right, contract=((1,), (0,))):
    left_top = left.astype(jnp.bfloat16)
    right_top = right.astype(jnp.bfloat16)
    left_low = (left - left_top.astype(jnp.float32)).astype(jnp.bfloat16)
    right_low = (right - right_top.astype(jnp.float32)).astype(jnp.bfloat16)
    small = dot(left_low, right_top, contract, None) + dot(left_top, right_low, contract, None)
    return dot(left_top, right_top, contract, None) + small


NT = ((1,), (1,))
STOP = 1e-5
NEAR = 0.2


def rotation_kernel(coeffs_ref, gram_ref, squares_ref, cells_ref, snaps_ref, inv_one, inv_two, upper, work):
    coeffs = coeffs_ref[...]
    modes = coeffs.shape[1]
    squares = squares_ref[...]
    coeffs_turned = coeffs.T
    square = dot(coeffs_turned, coeffs)
    upper[...] = square + jnp.where(diagonal(square), squares, 0.0)
    inv_one[...] = dot(upper[...], upper[...]) + dot(
        coeffs_turned, dot(gram_ref[...], coeffs)
    )
    factor_inverse(inv_one, work)
    stacked = dot(inv_one[...], upper[...])
    part = dot(inv_one[...], coeffs_turned)
    gram_two = dot(stacked, stacked, NT) + dot(dot(part, gram_ref[...]), part, NT)
    inv_two[...] = gram_two
    rest = gram_two - jnp.where(diagonal(gram_two), 1.0, 0.0)
    size = jnp.sum(rest * rest)
    near = size < NEAR

    @pl.when(near)
    def _():
        upper[...] = rest

        def more(carry):
            return (carry[0] >= STOP) & (carry[1] < 16)

        def newton(carry):
            rest = upper[...]
            low = half(rest)
            inv_one[...] = inv_one[...] - dot3(low, inv_one[...])
            mixed = dot3(low, rest)
            rest = dot3(low + mixed, low, NT) - mixed - mixed.T
            upper[...] = rest
            return jnp.sum(rest * rest), carry[1] + 1

        lax.while_loop(more, newton, (size, jnp.int32(0)))
        inv_one[...] = inv_one[...] - dot3(half(upper[...]), inv_one[...])

    @pl.when(jnp.logical_not(near))
    def _():
        factor_inverse(inv_two, work)
        inv_one[...] = dot(inv_two[...], inv_one[...])

    cells_ref[...] = inv_one[...] * squares
    snaps_ref[...] = dot(coeffs, inv_one[...], NT)


def rotation_of(coeffs, gram_res, squares):
    snaps, modes = coeffs.shape
    whole = pltpu.VMEM((modes, modes), jnp.float32)
    spec = pl.BlockSpec(memory_space=pltpu.VMEM)
    return pl.pallas_call(
        rotation_kernel,
        out_shape=(
            jax.ShapeDtypeStruct((modes, modes), jnp.float32),
            jax.ShapeDtypeStruct((snaps, modes), jnp.float32),
        ),
        in_specs=[spec] * 3,
        out_specs=(spec, spec),
        scratch_shapes=[whole, whole, whole, pltpu.VMEM((BLOCK, BLOCK), jnp.float32)],
    )(coeffs, gram_res, squares)


HIGH = lax.Precision.HIGH


def mat(left, right, contract, precision=HIGH):
    return lax.dot_general(
        left, right, (contract, ((), ())), precision=precision, preferred_element_type=jnp.float32
    )


def pair_rounds():
    rounds = []
    for name in ("slab", "tile"):
        size = lax.axis_size(name)
        step = 1
        while step < size:
            rounds.append((name, [(i, i ^ step) for i in range(size)]))
            step *= 2
    return rounds


def sum_all(part):
    for name, pairs in pair_rounds():
        part = part + lax.ppermute(part, name, pairs)
    return part


def sum_all_halved(part):
    rounds = pair_rounds()
    half_rows = part.shape[0] // 2
    first = lax.axis_index(rounds[0][0]) % 2 == 0
    top, low = part[:half_rows], part[half_rows:]
    kept = jnp.where(first, top, low) + lax.ppermute(jnp.where(first, low, top), *rounds[0])
    for name, pairs in rounds[1:]:
        kept = kept + lax.ppermute(kept, name, pairs)
    other = lax.ppermute(kept, *rounds[0])
    return jnp.concatenate([jnp.where(first, kept, other), jnp.where(first, other, kept)], axis=0)


def local(snapshots, old_basis, sing_values):
    snap_rows = lax.all_to_all(snapshots, "tile", split_axis=1, concat_axis=0, tiled=True)
    cell_count = old_basis.shape[0] * lax.axis_size("tile") * lax.axis_size("slab")
    weight_cell = 1.0 / cell_count
    coeffs = sum_all_halved(mat(snap_rows, old_basis, ((1,), (0,))) * weight_cell)
    resid = snap_rows - mat(coeffs, old_basis, ((1,), (1,)))
    gram_res = sum_all(mat(resid, resid, ((1,), (1,))) * weight_cell)
    squares = (sing_values * sing_values)[None, :]
    turn_cells, turn_snaps = rotation_of(coeffs, gram_res, squares)
    result = mat(old_basis, turn_cells, ((1,), (1,))) + mat(snap_rows, turn_snaps, ((0,), (0,)))
    return result.astype(jnp.bfloat16)


def solution(mesh):
    placed = (P("tile", "slab"), P(("slab", "tile"), None), P())
    return jax.shard_map(
        local, mesh=mesh, in_specs=placed, out_specs=P(("slab", "tile"), None), check_vma=False
    )
```

profile of v0, /device:TPU:0, one launch (start us, length us, event | category | flops | bytes accessed | tf_op | source)
XLA Modules:
  0.0 118.4 jit_solution(10771829278201369049)
XLA Ops:
  0.0 7.3 %all-to-all-start = ((f32[8,8,1920]{2,0,1:T(8,128)}), f32[8,8,1920]{2,0,1:T(8,128)S(1)}, u32[]{:S(2)}, u32[]{:S(2)}) async-start(f32[8,8,1920]{2,0,1:T(8,128)} %bitcast.19), calls=%async_computation | async-start | bytes 983040 | tf_op jit(solution)/shard_map/all_to_all | solution.py:231
  7.3 13.8 %all-to-all-done = f32[8,8,1920]{2,0,1:T(8,128)S(1)} async-done(((f32[8,8,1920]{2,0,1:T(8,128)}), f32[8,8,1920]{2,0,1:T(8,128)S(1)}, u32[]{:S(2)}, u32[]{:S(2)}) %all-to-all-start) | async-done | bytes 491552 | tf_op jit(solution)/shard_map/all_to_all | solution.py:231
  21.1 0.0 copy-start
  21.1 3.6 %convolution_multiply_fusion = f32[64,512]{1,0:T(8,128)S(1)} fusion(f32[1920,512]{1,0:T(8,128)} %param.4, f32[8,8,1920]{2,0,1:T(8,128)S(1)} %all-to-all-done), kind=kOutput, calls=%fused_computation.3 | convolution fusion | flops 377520128 | bytes 4554752 | tf_op jit(solution)/shard_map/dot_general | solution.py:196
  24.7 0.0 copy-start.2
  24.7 0.1 collective-permute-start
  24.8 1.2 %collective-permute-done = f32[32,512]{1,0:T(8,128)S(1)} collective-permute-done((f32[32,512]{1,0:T(8,128)S(1)}, f32[32,512]{1,0:T(8,128)S(1)}, u32[]{:S(2)}, u32[]{:S(2)}) %collective-permute-start) | collective-permute-done | bytes 65568 | tf_op jit(solution)/shard_map/ppermute | solution.py:223
  26.1 1.6 %collective-permute-start.1 = (f32[32,512]{1,0:T(8,128)S(1)}, f32[32,512]{1,0:T(8,128)S(1)}, u32[]{:S(2)}, u32[]{:S(2)}) collective-permute-start(f32[32,512]{1,0:T(8,128)S(1)} %select_add_fusion), channel_id=1, source_target_pairs={{0,2},{1,3},{2,0},{3,1},{4,6},{5,7},{6,4},{7,5},{8,10},{9,11},{10,... | collective-permute-start | bytes 196616 | tf_op jit(solution)/shard_map/ppermute | solution.py:225
  27.6 2.8 %collective-permute-done.1 = f32[32,512]{1,0:T(8,128)S(1)} collective-permute-done((f32[32,512]{1,0:T(8,128)S(1)}, f32[32,512]{1,0:T(8,128)S(1)}, u32[]{:S(2)}, u32[]{:S(2)}) %collective-permute-start.1) | collective-permute-done | bytes 65568 | tf_op jit(solution)/shard_map/ppermute | solution.py:225
  30.4 1.5 %collective-permute-start.2 = (f32[32,512]{1,0:T(8,128)S(1)}, f32[32,512]{1,0:T(8,128)S(1)}, u32[]{:S(2)}, u32[]{:S(2)}) collective-permute-start(f32[32,512]{1,0:T(8,128)S(1)} %add.40), channel_id=1, source_target_pairs={{0,4},{4,0},{8,12},{12,8},{16,20},{20,16},{24,28},{28,24},{1,5},{5... | collective-permute-start | bytes 196616 | tf_op jit(solution)/shard_map/ppermute | solution.py:225
  31.9 2.8 %collective-permute-done.2 = f32[32,512]{1,0:T(8,128)S(1)} collective-permute-done((f32[32,512]{1,0:T(8,128)S(1)}, f32[32,512]{1,0:T(8,128)S(1)}, u32[]{:S(2)}, u32[]{:S(2)}) %collective-permute-start.2) | collective-permute-done | bytes 65568 | tf_op jit(solution)/shard_map/ppermute | solution.py:225
  34.8 0.9 collective-permute-start.3
  35.6 3.5 %collective-permute-done.3 = f32[32,512]{1,0:T(8,128)S(1)} collective-permute-done((f32[32,512]{1,0:T(8,128)S(1)}, f32[32,512]{1,0:T(8,128)S(1)}, u32[]{:S(2)}, u32[]{:S(2)}) %collective-permute-start.3) | collective-permute-done | bytes 65568 | tf_op jit(solution)/shard_map/ppermute | solution.py:225
  39.1 0.3 collective-permute-start.4
  39.4 5.6 %collective-permute-done.4 = f32[32,512]{1,0:T(8,128)S(1)} collective-permute-done((f32[32,512]{1,0:T(8,128)S(1)}, f32[32,512]{1,0:T(8,128)S(1)}, u32[]{:S(2)}, u32[]{:S(2)}) %collective-permute-start.4) | collective-permute-done | bytes 65568 | tf_op jit(solution)/shard_map/ppermute | solution.py:225
  45.0 0.1 collective-permute-start.5
  45.1 1.2 %collective-permute-done.5 = f32[32,512]{1,0:T(8,128)S(1)} collective-permute-done((f32[32,512]{1,0:T(8,128)S(1)}, f32[32,512]{1,0:T(8,128)S(1)}, u32[]{:S(2)}, u32[]{:S(2)}) %collective-permute-start.5) | collective-permute-done | bytes 65568 | tf_op jit(solution)/shard_map/ppermute | solution.py:226
  46.4 0.0 copy-done
  46.4 2.0 %convolution_subtract_fusion = f32[64,1920]{1,0:T(8,128)S(1)} fusion(f32[1920,512]{1,0:T(8,128)S(1)} %copy-done, f32[8,8,1920]{2,0,1:T(8,128)S(1)} %all-to-all-done, f32[32,512]{1,0:T(8,128)S(1)} %get-tuple-element.10, f32[32,512]{1,0:T(8,128)S(1)} %get-tuple-element.9), kind=kOutput, calls=%fused_computation.2 | convolution fusion | flops 377643008 | bytes 5046272 | tf_op jit(solution)/shard_map/dot_general | solution.py:196
  48.4 0.4 convolution_multiply_fusion.1
  48.8 0.2 collective-permute-start.6
  49.0 1.0 collective-permute-done.6
  50.0 1.5 %collective-permute-start.7 = (f32[64,64]{1,0:T(8,128)S(1)}, f32[64,64]{1,0:T(8,128)S(1)}, u32[]{:S(2)}, u32[]{:S(2)}) collective-permute-start(f32[64,64]{1,0:T(8,128)S(1)} %add.44), channel_id=1, source_target_pairs={{0,2},{1,3},{2,0},{3,1},{4,6},{5,7},{6,4},{7,5},{8,10},{9,11},{10,... | collective-permute-start | bytes 49160 | tf_op jit(solution)/shard_map/ppermute | solution.py:214
  51.5 2.4 %collective-permute-done.7 = f32[64,64]{1,0:T(8,128)S(1)} collective-permute-done((f32[64,64]{1,0:T(8,128)S(1)}, f32[64,64]{1,0:T(8,128)S(1)}, u32[]{:S(2)}, u32[]{:S(2)}) %collective-permute-start.7) | collective-permute-done | bytes 16416 | tf_op jit(solution)/shard_map/ppermute | solution.py:214
  54.0 1.2 %collective-permute-start.8 = (f32[64,64]{1,0:T(8,128)S(1)}, f32[64,64]{1,0:T(8,128)S(1)}, u32[]{:S(2)}, u32[]{:S(2)}) collective-permute-start(f32[64,64]{1,0:T(8,128)S(1)} %add.45), channel_id=1, source_target_pairs={{0,4},{4,0},{8,12},{12,8},{16,20},{20,16},{24,28},{28,24},{1,5},{5... | collective-permute-start | bytes 49160 | tf_op jit(solution)/shard_map/ppermute | solution.py:214
  55.2 2.7 %collective-permute-done.8 = f32[64,64]{1,0:T(8,128)S(1)} collective-permute-done((f32[64,64]{1,0:T(8,128)S(1)}, f32[64,64]{1,0:T(8,128)S(1)}, u32[]{:S(2)}, u32[]{:S(2)}) %collective-permute-start.8) | collective-permute-done | bytes 16416 | tf_op jit(solution)/shard_map/ppermute | solution.py:214
  57.9 0.5 collective-permute-start.9
  58.4 0.0 copy-done.2
  58.4 0.6 mul.19
  59.0 2.8 %collective-permute-done.9 = f32[64,64]{1,0:T(8,128)S(1)} collective-permute-done((f32[64,64]{1,0:T(8,128)S(1)}, f32[64,64]{1,0:T(8,128)S(1)}, u32[]{:S(2)}, u32[]{:S(2)}) %collective-permute-start.9) | collective-permute-done | bytes 16416 | tf_op jit(solution)/shard_map/ppermute | solution.py:214
  61.8 0.0 collective-permute-start.10
  61.8 0.7 pad_maximum_fusion.coeffs_ref
  62.5 4.4 %collective-permute-done.10 = f32[64,64]{1,0:T(8,128)S(1)} collective-permute-done((f32[64,64]{1,0:T(8,128)S(1)}, f32[64,64]{1,0:T(8,128)S(1)}, u32[]{:S(2)}, u32[]{:S(2)}) %collective-permute-start.10) | collective-permute-done | bytes 16416 | tf_op jit(solution)/shard_map/ppermute | solution.py:214
  66.9 0.6 add.48.gram_ref
  67.5 40.7 %shard_map.37 = (f32[512,512]{1,0:T(8,128)}, f32[64,512]{1,0:T(8,128)}) custom-call(f32[64,512]{1,0:T(8,128)} %pad_maximum_fusion.coeffs_ref, f32[64,64]{1,0:T(8,128)} %add.48.gram_ref, f32[1,512]{1,0:T(1,128)} %bitcast.20), custom_call_target="tpu_custom_call" | custom-call | tf_op jit(solution)/shard_map/pallas_call | solution.py:180
  108.2 0.0 copy-start.1
  108.2 2.8 %fusion.1 = f32[512,1920]{1,0:T(8,128)S(1)} fusion(f32[64,512]{1,0:T(8,128)} %get-tuple-element.8, f32[8,8,1920]{2,0,1:T(8,128)S(1)} %all-to-all-done), kind=kOutput, calls=%fused_computation.5 | convolution fusion | flops 377487360 | bytes 4554752 | tf_op jit(solution)/shard_map/dot_general | solution.py:196
  111.0 0.0 copy-done.1
  111.0 5.1 %fusion = bf16[1920,512]{0,1:T(8,128)(2,1)S(1)} fusion(f32[512,1920]{1,0:T(8,128)S(1)} %fusion.1, f32[512,512]{1,0:T(8,128)} %get-tuple-element.7, f32[1920,512]{1,0:T(8,128)S(1)} %copy-done.1), kind=kOutput, calls=%fused_computation.1 | convolution fusion | flops 3021864960 | bytes 10878976 | tf_op jit(solution)/shard_map/dot_general | solution.py:196
  116.1 2.3 %copy.4 = bf16[1920,512]{1,0:T(8,128)(2,1)} copy(bf16[1920,512]{0,1:T(8,128)(2,1)S(1)} %fusion) | data formatting | bytes 3932160 | tf_op jit(solution)/shard_map/convert_element_type | solution.py:240
  (11 shorter events, 0.1 us)
Async XLA Ops:
  0.0 21.1 %all-to-all-start = ((f32[8,8,1920]{2,0,1:T(8,128)}), f32[8,8,1920]{2,0,1:T(8,128)S(1)}, u32[]{:S(2)}, u32[]{:S(2)}) async-start(f32[8,8,1920]{2,0,1:T(8,128)} %bitcast.19), calls=%async_computation | async-start | bytes 983040 | tf_op jit(solution)/shard_map/all_to_all | solution.py:231
  21.1 25.3 %copy-start = (f32[1920,512]{1,0:T(8,128)S(1)}, f32[1920,512]{1,0:T(8,128)}, u32[]{:S(2)}) copy-start(f32[1920,512]{1,0:T(8,128)} %param.4) | copy-start | bytes 11796484
  24.7 33.7 %copy-start.2 = (f32[512]{0:T(512)S(1)}, f32[512]{0:T(512)}, u32[]{:S(2)}) copy-start(f32[512]{0:T(512)} %param.5) | copy-start | bytes 6148
  24.7 1.3 %collective-permute-start = (f32[32,512]{1,0:T(8,128)S(1)}, f32[32,512]{1,0:T(8,128)S(1)}, u32[]{:S(2)}, u32[]{:S(2)}) collective-permute-start(f32[32,512]{1,0:T(8,128)S(1)} %slice_select_fusion), channel_id=1, source_target_pairs={{0,1},{1,0},{2,3},{3,2},{4,5},{5,4},{6,7},{7,6},{8,9},{9,8},{10,11... | collective-permute-start | bytes 196616 | tf_op jit(solution)/shard_map/ppermute | solution.py:223
  26.1 4.3 %collective-permute-start.1 = (f32[32,512]{1,0:T(8,128)S(1)}, f32[32,512]{1,0:T(8,128)S(1)}, u32[]{:S(2)}, u32[]{:S(2)}) collective-permute-start(f32[32,512]{1,0:T(8,128)S(1)} %select_add_fusion), channel_id=1, source_target_pairs={{0,2},{1,3},{2,0},{3,1},{4,6},{5,7},{6,4},{7,5},{8,10},{9,11},{10,... | collective-permute-start | bytes 196616 | tf_op jit(solution)/shard_map/ppermute | solution.py:225
  30.4 4.3 %collective-permute-start.2 = (f32[32,512]{1,0:T(8,128)S(1)}, f32[32,512]{1,0:T(8,128)S(1)}, u32[]{:S(2)}, u32[]{:S(2)}) collective-permute-start(f32[32,512]{1,0:T(8,128)S(1)} %add.40), channel_id=1, source_target_pairs={{0,4},{4,0},{8,12},{12,8},{16,20},{20,16},{24,28},{28,24},{1,5},{5... | collective-permute-start | bytes 196616 | tf_op jit(solution)/shard_map/ppermute | solution.py:225
  34.8 4.3 %collective-permute-start.3 = (f32[32,512]{1,0:T(8,128)S(1)}, f32[32,512]{1,0:T(8,128)S(1)}, u32[]{:S(2)}, u32[]{:S(2)}) collective-permute-start(f32[32,512]{1,0:T(8,128)S(1)} %add.41), channel_id=1, source_target_pairs={{0,8},{4,12},{8,0},{12,4},{16,24},{20,28},{24,16},{28,20},{1,9},{5... | collective-permute-start | bytes 196616 | tf_op jit(solution)/shard_map/ppermute | solution.py:225
  39.1 5.9 %collective-permute-start.4 = (f32[32,512]{1,0:T(8,128)S(1)}, f32[32,512]{1,0:T(8,128)S(1)}, u32[]{:S(2)}, u32[]{:S(2)}) collective-permute-start(f32[32,512]{1,0:T(8,128)S(1)} %add.42), channel_id=1, source_target_pairs={{0,16},{4,20},{8,24},{12,28},{16,0},{20,4},{24,8},{28,12},{1,17},{... | collective-permute-start | bytes 196616 | tf_op jit(solution)/shard_map/ppermute | solution.py:225
  45.0 1.3 %collective-permute-start.5 = (f32[32,512]{1,0:T(8,128)S(1)}, f32[32,512]{1,0:T(8,128)S(1)}, u32[]{:S(2)}, u32[]{:S(2)}) collective-permute-start(f32[32,512]{1,0:T(8,128)S(1)} %add.43), channel_id=1, source_target_pairs={{0,1},{1,0},{2,3},{3,2},{4,5},{5,4},{6,7},{7,6},{8,9},{9,8},{10,11... | collective-permute-start | bytes 196616 | tf_op jit(solution)/shard_map/ppermute | solution.py:226
  48.8 1.3 %collective-permute-start.6 = (f32[64,64]{1,0:T(8,128)S(1)}, f32[64,64]{1,0:T(8,128)S(1)}, u32[]{:S(2)}, u32[]{:S(2)}) collective-permute-start(f32[64,64]{1,0:T(8,128)S(1)} %convolution_multiply_fusion.1), channel_id=1, source_target_pairs={{0,1},{1,0},{2,3},{3,2},{4,5},{5,4},{6,7},{7,6},{8,9},{9,8},{10,11... | collective-permute-start | bytes 49160 | tf_op jit(solution)/shard_map/ppermute | solution.py:214
  50.0 3.9 %collective-permute-start.7 = (f32[64,64]{1,0:T(8,128)S(1)}, f32[64,64]{1,0:T(8,128)S(1)}, u32[]{:S(2)}, u32[]{:S(2)}) collective-permute-start(f32[64,64]{1,0:T(8,128)S(1)} %add.44), channel_id=1, source_target_pairs={{0,2},{1,3},{2,0},{3,1},{4,6},{5,7},{6,4},{7,5},{8,10},{9,11},{10,... | collective-permute-start | bytes 49160 | tf_op jit(solution)/shard_map/ppermute | solution.py:214
  54.0 3.9 %collective-permute-start.8 = (f32[64,64]{1,0:T(8,128)S(1)}, f32[64,64]{1,0:T(8,128)S(1)}, u32[]{:S(2)}, u32[]{:S(2)}) collective-permute-start(f32[64,64]{1,0:T(8,128)S(1)} %add.45), channel_id=1, source_target_pairs={{0,4},{4,0},{8,12},{12,8},{16,20},{20,16},{24,28},{28,24},{1,5},{5... | collective-permute-start | bytes 49160 | tf_op jit(solution)/shard_map/ppermute | solution.py:214
  57.9 3.9 %collective-permute-start.9 = (f32[64,64]{1,0:T(8,128)S(1)}, f32[64,64]{1,0:T(8,128)S(1)}, u32[]{:S(2)}, u32[]{:S(2)}) collective-permute-start(f32[64,64]{1,0:T(8,128)S(1)} %add.46), channel_id=1, source_target_pairs={{0,8},{4,12},{8,0},{12,4},{16,24},{20,28},{24,16},{28,20},{1,9},{5... | collective-permute-start | bytes 49160 | tf_op jit(solution)/shard_map/ppermute | solution.py:214
  61.8 5.1 %collective-permute-start.10 = (f32[64,64]{1,0:T(8,128)S(1)}, f32[64,64]{1,0:T(8,128)S(1)}, u32[]{:S(2)}, u32[]{:S(2)}) collective-permute-start(f32[64,64]{1,0:T(8,128)S(1)} %add.47), channel_id=1, source_target_pairs={{0,16},{4,20},{8,24},{12,28},{16,0},{20,4},{24,8},{28,12},{1,17},{... | collective-permute-start | bytes 49160 | tf_op jit(solution)/shard_map/ppermute | solution.py:214
  108.2 2.8 %copy-start.1 = (f32[1920,512]{1,0:T(8,128)S(1)}, f32[1920,512]{1,0:T(8,128)}, u32[]{:S(2)}) copy-start(f32[1920,512]{1,0:T(8,128)} %param.4) | copy-start | bytes 11796484
where the time goes:
time: 119 us; the launch traced here: 118 us
  waiting for transfers between devices  44.3 us (37%)
  Pallas kernels  40.7 us (34%)
  starting transfers between devices  15.2 us (13%)
  matrix products  13.9 us (12%)
  local copies, waits for them, and re-layouts  2.31 us (2%)
  other arithmetic  1.97 us (2%)
    pallas_call x1, Pallas kernels, rotation_of(): pl.pallas_call(rotation_kernel, out_shape=(jax.ShapeDtypeStruct((modes, m...  40.7 us
    ppermute x4, waiting for transfers between devices, sum_all_halved(): kept = kept + lax.ppermute(kept, name, pairs)  14.6 us
    dot_general x5, matrix products, mat(): lax.dot_general(left, right, (contract, ((), ())), precision=precision, p...  13.9 us
    all_to_all x1, waiting for transfers between devices, local(): lax.all_to_all(snapshots, 'tile', split_axis=1, concat_axis=0, tiled=True)  13.8 us
    ppermute x5, waiting for transfers between devices, sum_all(): part = part + lax.ppermute(part, name, pairs)  13.4 us
    all_to_all x1, starting transfers between devices, local(): lax.all_to_all(snapshots, 'tile', split_axis=1, concat_axis=0, tiled=True)  7.31 us
    ppermute x4, starting transfers between devices, sum_all_halved(): kept = kept + lax.ppermute(kept, name, pairs)  4.27 us
    ppermute x5, starting transfers between devices, sum_all(): part = part + lax.ppermute(part, name, pairs)  3.44 us
  transfers between devices with their start and end apart: 12, of which 12 were waited for; matrix products, arithmetic and copies ran while one was open for 1% of the time, Pallas kernels for 0%

commit v1 on v0

v1 whole, which is shorter than its diff:
```python
import jax
import jax.numpy as jnp
from jax import lax
from jax.experimental import pallas as pl
from jax.experimental.pallas import tpu as pltpu
from jax.sharding import PartitionSpec as P

HIGHEST = lax.Precision.HIGHEST
BLOCK = 128


def dot(left, right, contract=((1,), (0,)), precision=HIGHEST):
    return lax.dot_general(
        left, right, (contract, ((), ())), precision=precision, preferred_element_type=jnp.float32
    )


def spread(value, row):
    return jnp.broadcast_to(value[row : row + 1, :], value.shape)


def lane_spread(value, lane):
    return jnp.broadcast_to(value[:, lane : lane + 1], value.shape)


def total(terms):
    while len(terms) > 1:
        terms = [a + b for a, b in zip(terms[::2], terms[1::2])] + terms[len(terms) // 2 * 2 :]
    return terms[0]


def factor_block(work):
    size = work.shape[0]
    lanes = lax.broadcasted_iota(jnp.int32, (8, size), 1)
    subs = lax.broadcasted_iota(jnp.int32, (8, size), 0)
    first = work[pl.ds(0, 8), :]
    cols = [lane_spread(first, j) for j in range(8)]
    for step in range(size // 8):
        base = 8 * step
        inside = (lanes >= base) & (lanes < base + 8)
        last = step + 1 == size // 8
        below = {
            other: work[pl.ds(8 * other, 8), :] for other in range(step + 1, size // 8)
        }
        beside = {
            other: [lane_spread(rows, base + j) for j in range(8)] for other, rows in below.items()
        }
        ratio, recip = {}, []
        for j in range(8):
            pivot = spread(cols[j], j)
            pivots = pivot if j == 0 else jnp.where(subs == j, pivot, pivots)
            recip.append(1.0 / pivot)
            for k in range(j + 1, 8):
                ratio[j, k] = spread(cols[j], k) * recip[j]
                cols[k] = cols[k] - cols[j] * ratio[j, k]
        if not last:
            near = list(beside[step + 1])
            for j in range(8):
                for k in range(j + 1, 8):
                    near[k] = near[k] - near[j] * ratio[j, k]
            own = [lane_spread(below[step + 1], base + 8 + i) for i in range(8)]
            shares = [near[j] * recip[j] for j in range(8)]
            own = [
                own[i] - total([near[j] * spread(shares[j], i) for j in range(8)]) for i in range(8)
            ]
        row = work[pl.ds(base, 8), :]
        row = jnp.where(inside, jnp.where(lanes - base == subs, 1.0, 0.0), row)
        solved = []
        for j in range(8):
            solved.append(spread(row, j) * recip[j])
            if j < 7:
                row = row - jnp.where(subs > j, cols[j], 0.0) * solved[j]
        work[pl.ds(base, 8), :] = row * lax.rsqrt(pivots)
        for j in reversed(range(7)):
            solved[j] = solved[j] - total([ratio[j, k] * solved[k] for k in range(j + 1, 8)])
        for other, rows in below.items():
            work[pl.ds(8 * other, 8), :] = jnp.where(inside, 0.0, rows) - total(
                [beside[other][j] * solved[j] for j in range(8)]
            )
        if not last:
            cols = own


def tril(value):
    rows = lax.broadcasted_iota(jnp.int32, value.shape, 0)
    return jnp.where(lax.broadcasted_iota(jnp.int32, value.shape, 1) <= rows, value, 0.0)


def factor_inverse(gram, work):
    size = gram.shape[0]
    count = size // BLOCK

    def step(index, carry):
        start = pl.multiple_of(index * BLOCK, BLOCK)
        here = pl.ds(start, BLOCK)
        work[...] = gram[here, here]
        factor_block(work)
        inverse = tril(work[...])
        gram[here, here] = jnp.eye(BLOCK, dtype=jnp.float32)
        for block in range(count):

            @pl.when(index == block)
            def _():
                low = BLOCK * block
                rest = size - low - BLOCK
                row = dot(inverse, gram[pl.ds(low, BLOCK), :])
                gram[pl.ds(low, BLOCK), :] = row
                if rest:
                    turned = row[:, low + BLOCK :].T
                    gram[pl.ds(low + BLOCK, rest), pl.ds(low, BLOCK)] = jnp.zeros(
                        (rest, BLOCK), jnp.float32
                    )
                    for other in range(0, rest, BLOCK):
                        rows = pl.ds(low + BLOCK + other, BLOCK)
                        gram[rows, :] = gram[rows, :] - dot(turned[other : other + BLOCK], row)

        return carry

    lax.fori_loop(0, count, step, 0)
    gram[...] = tril(gram[...])


def diagonal(value):
    rows = lax.broadcasted_iota(jnp.int32, value.shape, 0)
    cols = lax.broadcasted_iota(jnp.int32, value.shape, 1)
    return rows == cols


def half(value, offset=0):
    rows = lax.broadcasted_iota(jnp.int32, value.shape, 0) + offset
    cols = lax.broadcasted_iota(jnp.int32, value.shape, 1)
    return jnp.where(rows > cols, value, jnp.where(rows == cols, 0.5 * value, 0.0))


def split(value, parts):
    pieces = []
    for _ in range(parts):
        pieces.append(value.astype(jnp.bfloat16))
        value = value - pieces[-1].astype(jnp.float32)
    return pieces


def dot3(left, right, contract=((1,), (0,))):
    left_top, left_low = split(left, 2)
    right_top, right_low = split(right, 2)
    small = dot(left_low, right_top, contract, None) + dot(left_top, right_low, contract, None)
    return dot(left_top, right_top, contract, None) + small


def outer(left, right):
    a, b, c = split(left, 3)
    d, e, f = split(right, 3)
    left = jnp.concatenate([a, a, b, a, c, b], axis=0).astype(jnp.float32)
    right = jnp.concatenate([d, e, d, f, d, e], axis=0)
    return dot(left.T.astype(jnp.bfloat16), right, precision=None)


NT = ((1,), (1,))
STOP = 1e-5
NEAR = 0.2
BOUND = 1e30
SHIFT = 4e-6


def step_inverse(low, inverse):
    mid = low.shape[0] // 2
    inverse_top, inverse_low = inverse[:mid, :mid], inverse[...]
    inverse[:mid, :mid] = inverse_top - dot3(low[:mid, :mid], inverse_top)
    inverse[mid:, :] = inverse_low[mid:] - dot3(low[mid:], inverse_low)


def rotation(coeffs_ref, gram_ref, squares_ref, inverse, second, upper, work):
    coeffs = coeffs_ref[...]
    mid = coeffs.shape[1] // 2
    square = outer(coeffs, coeffs)
    upper[...] = square + jnp.where(diagonal(square), squares_ref[...], 0.0)

    def first_gram():
        extra = outer(coeffs, dot(gram_ref[...], coeffs))
        second[:mid, :] = dot(upper[:mid, :], upper[...]) + extra[:mid]
        second[mid:, mid:] = dot(upper[mid:, :], upper[:, mid:]) + extra[mid:, mid:]

    first_gram()

    def far(carry):
        return jnp.logical_not(carry[1] < NEAR) & (carry[0] < 8)

    def factor_pass(carry):
        count, _, fresh = carry
        factor_inverse(second, work)

        @pl.when(fresh == 1)
        def _():
            inverse[...] = second[...]

        @pl.when(fresh == 0)
        def _():
            inverse[...] = dot(second[...], inverse[...])

        second[:mid, :] = dot(inverse[:mid, :mid], upper[:mid, :])
        second[mid:, :] = dot(inverse[mid:, :], upper[...])
        part = dot3(inverse[...], coeffs, NT)
        side = dot3(part, gram_ref[...])
        stacked = second[...]
        gram_low = dot3(stacked[mid:], stacked, NT) + dot3(side[mid:], part, NT)
        gram_top = dot3(stacked[:mid], stacked[:mid], NT) + dot3(side[:mid], part[:mid], NT)
        second[:mid, :mid] = gram_top
        second[mid:, :] = gram_low
        second[:mid, mid:] = gram_low[:, :mid].T
        rest = second[...] - jnp.where(diagonal(square), 1.0, 0.0)
        size = jnp.sum(rest * rest)
        failed = jnp.logical_not(size < BOUND)

        @pl.when(failed)
        def _():
            first_gram()
            ends = jnp.where(diagonal(square), second[...], 0.0)
            second[...] = second[...] + jnp.where(diagonal(square), SHIFT * jnp.max(ends), 0.0)

        return count + 1, size, failed.astype(jnp.int32)

    _, size, _ = lax.while_loop(far, factor_pass, (jnp.int32(0), jnp.float32(BOUND), jnp.int32(1)))

    second[...] = second[...] - jnp.where(diagonal(square), 1.0, 0.0)

    def more(carry):
        return (carry[0] >= STOP) & (carry[1] < 16)

    def newton(carry):
        rest = second[...]
        low = half(rest)
        step_inverse(low, inverse)
        mixed = dot3(low, rest)
        rest = dot3(low + mixed, low, NT) - mixed - mixed.T
        second[...] = rest
        return jnp.sum(rest * rest), carry[1] + 1

    lax.while_loop(more, newton, (size, jnp.int32(0)))
    step_inverse(half(second[...]), inverse)


def update_kernel(
    coeffs_ref, gram_ref, squares_ref, snaps_ref, basis_hbm, out_hbm,
    inverse, second, upper, work, basis, out, loaded, stored,
):
    rows, modes = basis.shape
    snaps = coeffs_ref.shape[0]
    mid = modes // 2
    load = pltpu.make_async_copy(basis_hbm, basis, loaded)
    load.start()
    rotation(coeffs_ref, gram_ref, squares_ref, inverse, second, upper, work)
    final = inverse[...]
    turn_top, turn_low = split(final * squares_ref[...], 2)
    across_top, across_low = split(dot(final, coeffs_ref[...], NT).T, 2)
    across = jnp.concatenate([across_top, across_low, across_top], axis=0)
    chunk = chunk_of(rows)
    load.wait()
    copies = []
    for start in range(0, rows, chunk):
        here = pl.ds(start, chunk)
        snaps_top, snaps_low = split(snaps_ref[:, pl.ds(start, chunk)], 2)
        mixed = jnp.concatenate([snaps_top, snaps_top, snaps_low], axis=0).astype(jnp.float32)
        base = dot(mixed.T.astype(jnp.bfloat16), across, precision=None)
        top, low = split(basis[here, :], 2)
        for cols, depth in ((slice(0, mid), mid), (slice(mid, modes), modes)):
            value = base[:, cols]
            for a, b in ((low, turn_top), (top, turn_low), (top, turn_top)):
                value = value + dot(a[:, :depth], b[cols, :depth], NT, None)
            out[here, cols] = value.astype(out.dtype)
        copies.append(pltpu.make_async_copy(out.at[here, :], out_hbm.at[here, :], stored.at[start // chunk]))
        copies[-1].start()
    for copy in copies:
        copy.wait()


def chunk_of(rows):
    for chunk in (640, 512, 384, 256, 128):
        if rows % chunk == 0:
            return chunk
    return rows


def updated_basis(coeffs, gram_res, squares, snap_rows, old_basis):
    rows, modes = old_basis.shape
    whole = pltpu.VMEM((modes, modes), jnp.float32)
    spec = pl.BlockSpec(memory_space=pltpu.VMEM)
    far = pl.BlockSpec(memory_space=pl.ANY)
    return pl.pallas_call(
        update_kernel,
        out_shape=jax.ShapeDtypeStruct((rows, modes), jnp.bfloat16),
        in_specs=[spec] * 4 + [far],
        out_specs=far,
        scratch_shapes=[
            whole, whole, whole, pltpu.VMEM((BLOCK, BLOCK), jnp.float32),
            pltpu.VMEM((rows, modes), jnp.float32), pltpu.VMEM((rows, modes), jnp.bfloat16),
            pltpu.SemaphoreType.DMA, pltpu.SemaphoreType.DMA((rows // chunk_of(rows),)),
        ],
        compiler_params=pltpu.CompilerParams(vmem_limit_bytes=48 * 1024 * 1024),
    )(coeffs, gram_res, squares, snap_rows, old_basis)


HIGH = lax.Precision.HIGH


def mat(left, right, contract, precision=HIGH):
    return lax.dot_general(
        left, right, (contract, ((), ())), precision=precision, preferred_element_type=jnp.float32
    )


def pair_rounds():
    rounds = []
    for name in ("slab", "tile"):
        size = lax.axis_size(name)
        step = 1
        while step < size:
            rounds.append((name, [(i, i ^ step) for i in range(size)]))
            step *= 2
    return rounds


def sum_all(part):
    for name, pairs in pair_rounds():
        part = part + lax.ppermute(part, name, pairs)
    return part


def sum_all_halved(part):
    rounds = pair_rounds()
    half_rows = part.shape[0] // 2
    first = lax.axis_index(rounds[0][0]) % 2 == 0
    top, low = part[:half_rows], part[half_rows:]
    kept = jnp.where(first, top, low) + lax.ppermute(jnp.where(first, low, top), *rounds[0])
    for name, pairs in rounds[1:]:
        kept = kept + lax.ppermute(kept, name, pairs)
    other = lax.ppermute(kept, *rounds[0])
    return jnp.concatenate([jnp.where(first, kept, other), jnp.where(first, other, kept)], axis=0)


def local(snapshots, old_basis, sing_values):
    snap_rows = lax.all_to_all(snapshots, "tile", split_axis=1, concat_axis=0, tiled=True)
    cell_count = old_basis.shape[0] * lax.axis_size("tile") * lax.axis_size("slab")
    weight_cell = 1.0 / cell_count
    coeffs = sum_all_halved(mat(snap_rows, old_basis, ((1,), (0,))) * weight_cell)
    resid = snap_rows - mat(coeffs, old_basis, ((1,), (1,)))
    gram_res = sum_all(mat(resid, resid, ((1,), (1,))) * weight_cell)
    squares = (sing_values * sing_values)[None, :]
    return updated_basis(coeffs, gram_res, squares, snap_rows, old_basis)


def solution(mesh):
    placed = (P("tile", "slab"), P(("slab", "tile"), None), P())
    return jax.shard_map(
        local, mesh=mesh, in_specs=placed, out_specs=P(("slab", "tile"), None), check_vma=False
    )
```

time: 119 us -> 102 us (0.86)
  matrix products: 13.9 us -> 5.98 us
  Pallas kernels: 40.7 us -> 35.2 us
  local copies, waits for them, and re-layouts: 2.31 us -> 0.01 us
  other arithmetic: 1.97 us -> 0.12 us
  waiting for transfers between devices: 44.3 us -> 45.5 us
    dot_general x5 -> x3, matrix products: 13.9 us -> 5.98 us  [mat(): lax.dot_general(left, right, (contract, ((), ())), precision=precision, p...]
    pallas_call x1, Pallas kernels: 40.7 us -> 35.2 us  [updated_basis(): pl.pallas_call(update_kernel, out_shape=jax.ShapeDtypeStruct((rows, modes...]
    convert_element_type x1 -> x0, local copies, waits for them, and re-layouts: 2.3 us -> none  [local(): return result.astype(jnp.bfloat16)]
    ppermute x5, waiting for transfers between devices: 13.4 us -> 14.6 us  [sum_all(): part = part + lax.ppermute(part, name, pairs)]
  transfers between devices with their start and end apart: 12 -> 12, of which waited for: 12 -> 12; matrix products, arithmetic and copies ran while one was open for 1% -> 0% of each run, Pallas kernels for 0% -> 0%
where the time goes in v1:
time: 102 us
  waiting for transfers between devices  45.5 us (45%)
  Pallas kernels  35.2 us (35%)
  starting transfers between devices  15.2 us (15%)
  matrix products  5.98 us (6%)
    pallas_call x1, Pallas kernels, updated_basis(): pl.pallas_call(update_kernel, out_shape=jax.ShapeDtypeStruct((rows, modes...  35.2 us
    ppermute x4, waiting for transfers between devices, sum_all_halved(): kept = kept + lax.ppermute(kept, name, pairs)  14.6 us
    ppermute x5, waiting for transfers between devices, sum_all(): part = part + lax.ppermute(part, name, pairs)  14.6 us
    all_to_all x1, waiting for transfers between devices, local(): lax.all_to_all(snapshots, 'tile', split_axis=1, concat_axis=0, tiled=True)  13.8 us
    all_to_all x1, starting transfers between devices, local(): lax.all_to_all(snapshots, 'tile', split_axis=1, concat_axis=0, tiled=True)  7.31 us
    dot_general x3, matrix products, mat(): lax.dot_general(left, right, (contract, ((), ())), precision=precision, p...  5.98 us
    ppermute x4, starting transfers between devices, sum_all_halved(): kept = kept + lax.ppermute(kept, name, pairs)  4.27 us
    ppermute x5, starting transfers between devices, sum_all(): part = part + lax.ppermute(part, name, pairs)  3.44 us
  transfers between devices with their start and end apart: 12, of which 12 were waited for; matrix products, arithmetic and copies ran while one was open for 0% of the time, Pallas kernels for 0%

profile of v1, /device:TPU:0, one launch (start us, length us, event | category | flops | bytes accessed | tf_op | source)
XLA Modules:
  0.0 102.3 jit_solution(13648976040279167621)
XLA Ops:
  0.0 7.3 %all-to-all-start = ((f32[8,8,1920]{2,0,1:T(8,128)}), f32[8,8,1920]{2,0,1:T(8,128)S(1)}, u32[]{:S(2)}, u32[]{:S(2)}) async-start(f32[8,8,1920]{2,0,1:T(8,128)} %bitcast.14), calls=%async_computation | async-start | bytes 983040 | tf_op jit(solution)/shard_map/all_to_all | solution.py:341
  7.3 13.8 %all-to-all-done = f32[8,8,1920]{2,0,1:T(8,128)S(1)} async-done(((f32[8,8,1920]{2,0,1:T(8,128)}), f32[8,8,1920]{2,0,1:T(8,128)S(1)}, u32[]{:S(2)}, u32[]{:S(2)}) %all-to-all-start) | async-done | bytes 491552 | tf_op jit(solution)/shard_map/all_to_all | solution.py:341
  21.1 0.0 copy-start
  21.1 3.6 %convolution_multiply_fusion = f32[64,512]{1,0:T(8,128)S(1)} fusion(f32[1920,512]{1,0:T(8,128)} %basis_hbm.1, f32[8,8,1920]{2,0,1:T(8,128)S(1)} %all-to-all-done), kind=kOutput, calls=%fused_computation.1 | convolution fusion | flops 377520128 | bytes 4554752 | tf_op jit(solution)/shard_map/dot_general | solution.py:306
  24.7 0.0 copy-start.1
  24.7 0.1 collective-permute-start
  24.8 1.2 %collective-permute-done = f32[32,512]{1,0:T(8,128)S(1)} collective-permute-done((f32[32,512]{1,0:T(8,128)S(1)}, f32[32,512]{1,0:T(8,128)S(1)}, u32[]{:S(2)}, u32[]{:S(2)}) %collective-permute-start) | collective-permute-done | bytes 65568 | tf_op jit(solution)/shard_map/ppermute | solution.py:333
  26.1 1.6 %collective-permute-start.1 = (f32[32,512]{1,0:T(8,128)S(1)}, f32[32,512]{1,0:T(8,128)S(1)}, u32[]{:S(2)}, u32[]{:S(2)}) collective-permute-start(f32[32,512]{1,0:T(8,128)S(1)} %select_add_fusion), channel_id=1, source_target_pairs={{0,2},{1,3},{2,0},{3,1},{4,6},{5,7},{6,4},{7,5},{8,10},{9,11},{10,... | collective-permute-start | bytes 196616 | tf_op jit(solution)/shard_map/ppermute | solution.py:335
  27.6 2.8 %collective-permute-done.1 = f32[32,512]{1,0:T(8,128)S(1)} collective-permute-done((f32[32,512]{1,0:T(8,128)S(1)}, f32[32,512]{1,0:T(8,128)S(1)}, u32[]{:S(2)}, u32[]{:S(2)}) %collective-permute-start.1) | collective-permute-done | bytes 65568 | tf_op jit(solution)/shard_map/ppermute | solution.py:335
  30.4 1.5 %collective-permute-start.2 = (f32[32,512]{1,0:T(8,128)S(1)}, f32[32,512]{1,0:T(8,128)S(1)}, u32[]{:S(2)}, u32[]{:S(2)}) collective-permute-start(f32[32,512]{1,0:T(8,128)S(1)} %add.36), channel_id=1, source_target_pairs={{0,4},{4,0},{8,12},{12,8},{16,20},{20,16},{24,28},{28,24},{1,5},{5... | collective-permute-start | bytes 196616 | tf_op jit(solution)/shard_map/ppermute | solution.py:335
  31.9 2.8 %collective-permute-done.2 = f32[32,512]{1,0:T(8,128)S(1)} collective-permute-done((f32[32,512]{1,0:T(8,128)S(1)}, f32[32,512]{1,0:T(8,128)S(1)}, u32[]{:S(2)}, u32[]{:S(2)}) %collective-permute-start.2) | collective-permute-done | bytes 65568 | tf_op jit(solution)/shard_map/ppermute | solution.py:335
  34.8 0.9 collective-permute-start.3
  35.6 3.5 %collective-permute-done.3 = f32[32,512]{1,0:T(8,128)S(1)} collective-permute-done((f32[32,512]{1,0:T(8,128)S(1)}, f32[32,512]{1,0:T(8,128)S(1)}, u32[]{:S(2)}, u32[]{:S(2)}) %collective-permute-start.3) | collective-permute-done | bytes 65568 | tf_op jit(solution)/shard_map/ppermute | solution.py:335
  39.1 0.3 collective-permute-start.4
  39.4 5.6 %collective-permute-done.4 = f32[32,512]{1,0:T(8,128)S(1)} collective-permute-done((f32[32,512]{1,0:T(8,128)S(1)}, f32[32,512]{1,0:T(8,128)S(1)}, u32[]{:S(2)}, u32[]{:S(2)}) %collective-permute-start.4) | collective-permute-done | bytes 65568 | tf_op jit(solution)/shard_map/ppermute | solution.py:335
  45.0 0.1 collective-permute-start.5
  45.1 1.2 %collective-permute-done.5 = f32[32,512]{1,0:T(8,128)S(1)} collective-permute-done((f32[32,512]{1,0:T(8,128)S(1)}, f32[32,512]{1,0:T(8,128)S(1)}, u32[]{:S(2)}, u32[]{:S(2)}) %collective-permute-start.5) | collective-permute-done | bytes 65568 | tf_op jit(solution)/shard_map/ppermute | solution.py:336
  46.4 0.0 copy-done
  46.4 2.0 %convolution_subtract_fusion = f32[64,1920]{1,0:T(8,128)S(1)} fusion(f32[1920,512]{1,0:T(8,128)S(1)} %copy-done, f32[8,8,1920]{2,0,1:T(8,128)S(1)} %all-to-all-done, f32[32,512]{1,0:T(8,128)S(1)} %get-tuple-element.6, f32[32,512]{1,0:T(8,128)S(1)} %get-tuple-element.5), kind=kOutput, calls=%fused_computation | convolution fusion | flops 377643008 | bytes 5046272 | tf_op jit(solution)/shard_map/dot_general | solution.py:306
  48.4 0.4 convolution_multiply_fusion.1
  48.8 0.2 collective-permute-start.6
  49.0 1.1 %collective-permute-done.6 = f32[64,64]{1,0:T(8,128)S(1)} collective-permute-done((f32[64,64]{1,0:T(8,128)S(1)}, f32[64,64]{1,0:T(8,128)S(1)}, u32[]{:S(2)}, u32[]{:S(2)}) %collective-permute-start.6) | collective-permute-done | bytes 16416 | tf_op jit(solution)/shard_map/ppermute | solution.py:324
  50.1 1.5 %collective-permute-start.7 = (f32[64,64]{1,0:T(8,128)S(1)}, f32[64,64]{1,0:T(8,128)S(1)}, u32[]{:S(2)}, u32[]{:S(2)}) collective-permute-start(f32[64,64]{1,0:T(8,128)S(1)} %add.40), channel_id=1, source_target_pairs={{0,2},{1,3},{2,0},{3,1},{4,6},{5,7},{6,4},{7,5},{8,10},{9,11},{10,... | collective-permute-start | bytes 49160 | tf_op jit(solution)/shard_map/ppermute | solution.py:324
  51.6 2.4 %collective-permute-done.7 = f32[64,64]{1,0:T(8,128)S(1)} collective-permute-done((f32[64,64]{1,0:T(8,128)S(1)}, f32[64,64]{1,0:T(8,128)S(1)}, u32[]{:S(2)}, u32[]{:S(2)}) %collective-permute-start.7) | collective-permute-done | bytes 16416 | tf_op jit(solution)/shard_map/ppermute | solution.py:324
  54.0 1.2 %collective-permute-start.8 = (f32[64,64]{1,0:T(8,128)S(1)}, f32[64,64]{1,0:T(8,128)S(1)}, u32[]{:S(2)}, u32[]{:S(2)}) collective-permute-start(f32[64,64]{1,0:T(8,128)S(1)} %add.41), channel_id=1, source_target_pairs={{0,4},{4,0},{8,12},{12,8},{16,20},{20,16},{24,28},{28,24},{1,5},{5... | collective-permute-start | bytes 49160 | tf_op jit(solution)/shard_map/ppermute | solution.py:324
  55.2 2.7 %collective-permute-done.8 = f32[64,64]{1,0:T(8,128)S(1)} collective-permute-done((f32[64,64]{1,0:T(8,128)S(1)}, f32[64,64]{1,0:T(8,128)S(1)}, u32[]{:S(2)}, u32[]{:S(2)}) %collective-permute-start.8) | collective-permute-done | bytes 16416 | tf_op jit(solution)/shard_map/ppermute | solution.py:324
  57.9 0.5 collective-permute-start.9
  58.4 0.0 copy-done.1
  58.4 3.4 %collective-permute-done.9 = f32[64,64]{1,0:T(8,128)S(1)} collective-permute-done((f32[64,64]{1,0:T(8,128)S(1)}, f32[64,64]{1,0:T(8,128)S(1)}, u32[]{:S(2)}, u32[]{:S(2)}) %collective-permute-start.9) | collective-permute-done | bytes 16416 | tf_op jit(solution)/shard_map/ppermute | solution.py:324
  61.8 0.0 collective-permute-start.10
  61.9 5.0 %collective-permute-done.10 = f32[64,64]{1,0:T(8,128)S(1)} collective-permute-done((f32[64,64]{1,0:T(8,128)S(1)}, f32[64,64]{1,0:T(8,128)S(1)}, u32[]{:S(2)}, u32[]{:S(2)}) %collective-permute-start.10) | collective-permute-done | bytes 16416 | tf_op jit(solution)/shard_map/ppermute | solution.py:324
  66.9 35.2 %shard_map.37 = bf16[1920,512]{1,0:T(8,128)(2,1)} custom-call(f32[64,512]{1,0:T(8,128)S(1)} %pad_maximum_fusion.coeffs_ref, f32[64,64]{1,0:T(8,128)S(1)} %add.44.gram_ref, f32[1,512]{1,0:T(1,128)S(1)} %bitcast.13, f32[64,1920]{1,0:T(8,128)S(1)} %bitcast.12, f32[1920,512]{1,0:T(8,128)S(1)} %copy-done), custom_call_target="tpu_custom_call" | custom-call | tf_op jit(solution)/shard_map/pallas_call | solution.py:288
  (14 shorter events, 0.1 us)
Async XLA Ops:
  0.0 21.1 %all-to-all-start = ((f32[8,8,1920]{2,0,1:T(8,128)}), f32[8,8,1920]{2,0,1:T(8,128)S(1)}, u32[]{:S(2)}, u32[]{:S(2)}) async-start(f32[8,8,1920]{2,0,1:T(8,128)} %bitcast.14), calls=%async_computation | async-start | bytes 983040 | tf_op jit(solution)/shard_map/all_to_all | solution.py:341
  21.1 25.3 %copy-start = (f32[1920,512]{1,0:T(8,128)S(1)}, f32[1920,512]{1,0:T(8,128)}, u32[]{:S(2)}) copy-start(f32[1920,512]{1,0:T(8,128)} %basis_hbm.1) | copy-start | bytes 11796484
  24.7 33.7 %copy-start.1 = (f32[512]{0:T(512)S(1)}, f32[512]{0:T(512)}, u32[]{:S(2)}) copy-start(f32[512]{0:T(512)} %param.5) | copy-start | bytes 6148
  24.7 1.3 %collective-permute-start = (f32[32,512]{1,0:T(8,128)S(1)}, f32[32,512]{1,0:T(8,128)S(1)}, u32[]{:S(2)}, u32[]{:S(2)}) collective-permute-start(f32[32,512]{1,0:T(8,128)S(1)} %slice_select_fusion), channel_id=1, source_target_pairs={{0,1},{1,0},{2,3},{3,2},{4,5},{5,4},{6,7},{7,6},{8,9},{9,8},{10,11... | collective-permute-start | bytes 196616 | tf_op jit(solution)/shard_map/ppermute | solution.py:333
  26.1 4.3 %collective-permute-start.1 = (f32[32,512]{1,0:T(8,128)S(1)}, f32[32,512]{1,0:T(8,128)S(1)}, u32[]{:S(2)}, u32[]{:S(2)}) collective-permute-start(f32[32,512]{1,0:T(8,128)S(1)} %select_add_fusion), channel_id=1, source_target_pairs={{0,2},{1,3},{2,0},{3,1},{4,6},{5,7},{6,4},{7,5},{8,10},{9,11},{10,... | collective-permute-start | bytes 196616 | tf_op jit(solution)/shard_map/ppermute | solution.py:335
  30.4 4.3 %collective-permute-start.2 = (f32[32,512]{1,0:T(8,128)S(1)}, f32[32,512]{1,0:T(8,128)S(1)}, u32[]{:S(2)}, u32[]{:S(2)}) collective-permute-start(f32[32,512]{1,0:T(8,128)S(1)} %add.36), channel_id=1, source_target_pairs={{0,4},{4,0},{8,12},{12,8},{16,20},{20,16},{24,28},{28,24},{1,5},{5... | collective-permute-start | bytes 196616 | tf_op jit(solution)/shard_map/ppermute | solution.py:335
  34.8 4.3 %collective-permute-start.3 = (f32[32,512]{1,0:T(8,128)S(1)}, f32[32,512]{1,0:T(8,128)S(1)}, u32[]{:S(2)}, u32[]{:S(2)}) collective-permute-start(f32[32,512]{1,0:T(8,128)S(1)} %add.37), channel_id=1, source_target_pairs={{0,8},{4,12},{8,0},{12,4},{16,24},{20,28},{24,16},{28,20},{1,9},{5... | collective-permute-start | bytes 196616 | tf_op jit(solution)/shard_map/ppermute | solution.py:335
  39.1 5.9 %collective-permute-start.4 = (f32[32,512]{1,0:T(8,128)S(1)}, f32[32,512]{1,0:T(8,128)S(1)}, u32[]{:S(2)}, u32[]{:S(2)}) collective-permute-start(f32[32,512]{1,0:T(8,128)S(1)} %add.38), channel_id=1, source_target_pairs={{0,16},{4,20},{8,24},{12,28},{16,0},{20,4},{24,8},{28,12},{1,17},{... | collective-permute-start | bytes 196616 | tf_op jit(solution)/shard_map/ppermute | solution.py:335
  45.0 1.3 %collective-permute-start.5 = (f32[32,512]{1,0:T(8,128)S(1)}, f32[32,512]{1,0:T(8,128)S(1)}, u32[]{:S(2)}, u32[]{:S(2)}) collective-permute-start(f32[32,512]{1,0:T(8,128)S(1)} %add.39), channel_id=1, source_target_pairs={{0,1},{1,0},{2,3},{3,2},{4,5},{5,4},{6,7},{7,6},{8,9},{9,8},{10,11... | collective-permute-start | bytes 196616 | tf_op jit(solution)/shard_map/ppermute | solution.py:336
  48.8 1.3 %collective-permute-start.6 = (f32[64,64]{1,0:T(8,128)S(1)}, f32[64,64]{1,0:T(8,128)S(1)}, u32[]{:S(2)}, u32[]{:S(2)}) collective-permute-start(f32[64,64]{1,0:T(8,128)S(1)} %convolution_multiply_fusion.1), channel_id=1, source_target_pairs={{0,1},{1,0},{2,3},{3,2},{4,5},{5,4},{6,7},{7,6},{8,9},{9,8},{10,11... | collective-permute-start | bytes 49160 | tf_op jit(solution)/shard_map/ppermute | solution.py:324
  50.1 3.9 %collective-permute-start.7 = (f32[64,64]{1,0:T(8,128)S(1)}, f32[64,64]{1,0:T(8,128)S(1)}, u32[]{:S(2)}, u32[]{:S(2)}) collective-permute-start(f32[64,64]{1,0:T(8,128)S(1)} %add.40), channel_id=1, source_target_pairs={{0,2},{1,3},{2,0},{3,1},{4,6},{5,7},{6,4},{7,5},{8,10},{9,11},{10,... | collective-permute-start | bytes 49160 | tf_op jit(solution)/shard_map/ppermute | solution.py:324
  54.0 3.9 %collective-permute-start.8 = (f32[64,64]{1,0:T(8,128)S(1)}, f32[64,64]{1,0:T(8,128)S(1)}, u32[]{:S(2)}, u32[]{:S(2)}) collective-permute-start(f32[64,64]{1,0:T(8,128)S(1)} %add.41), channel_id=1, source_target_pairs={{0,4},{4,0},{8,12},{12,8},{16,20},{20,16},{24,28},{28,24},{1,5},{5... | collective-permute-start | bytes 49160 | tf_op jit(solution)/shard_map/ppermute | solution.py:324
  57.9 3.9 %collective-permute-start.9 = (f32[64,64]{1,0:T(8,128)S(1)}, f32[64,64]{1,0:T(8,128)S(1)}, u32[]{:S(2)}, u32[]{:S(2)}) collective-permute-start(f32[64,64]{1,0:T(8,128)S(1)} %add.42), channel_id=1, source_target_pairs={{0,8},{4,12},{8,0},{12,4},{16,24},{20,28},{24,16},{28,20},{1,9},{5... | collective-permute-start | bytes 49160 | tf_op jit(solution)/shard_map/ppermute | solution.py:324
  61.8 5.1 %collective-permute-start.10 = (f32[64,64]{1,0:T(8,128)S(1)}, f32[64,64]{1,0:T(8,128)S(1)}, u32[]{:S(2)}, u32[]{:S(2)}) collective-permute-start(f32[64,64]{1,0:T(8,128)S(1)} %add.43), channel_id=1, source_target_pairs={{0,16},{4,20},{8,24},{12,28},{16,0},{20,4},{24,8},{28,12},{1,17},{... | collective-permute-start | bytes 49160 | tf_op jit(solution)/shard_map/ppermute | solution.py:324

commit v2 on v1

--- a/solution.py
+++ b/solution.py
@@ -1,3 +1,5 @@
+import functools
+
 import jax
 import jax.numpy as jnp
 from jax import lax
@@ -86,6 +88,23 @@
     return jnp.where(lax.broadcasted_iota(jnp.int32, value.shape, 1) <= rows, value, 0.0)
 
 
+def split(value, parts):
+    pieces = []
+    for _ in range(parts):
+        pieces.append(value.astype(jnp.bfloat16))
+        value = value - pieces[-1].astype(jnp.float32)
+    return pieces
+
+
+def block_dot(left, right):
+    a, b, c = split(left, 3)
+    d, e, f = split(right, 3)
+    both = jnp.concatenate([d, e], axis=0)
+    value = dot(jnp.concatenate([a, c], axis=1), jnp.concatenate([f, d], axis=0), precision=None)
+    value = value + dot(jnp.concatenate([b, b], axis=1), both, precision=None)
+    return value + dot(jnp.concatenate([a, a], axis=1), both, precision=None)
+
+
 def factor_inverse(gram, work):
     size = gram.shape[0]
     count = size // BLOCK
@@ -102,17 +121,12 @@
             @pl.when(index == block)
             def _():
                 low = BLOCK * block
-                rest = size - low - BLOCK
-                row = dot(inverse, gram[pl.ds(low, BLOCK), :])
-                gram[pl.ds(low, BLOCK), :] = row
-                if rest:
-                    turned = row[:, low + BLOCK :].T
-                    gram[pl.ds(low + BLOCK, rest), pl.ds(low, BLOCK)] = jnp.zeros(
-                        (rest, BLOCK), jnp.float32
-                    )
-                    for other in range(0, rest, BLOCK):
-                        rows = pl.ds(low + BLOCK + other, BLOCK)
-                        gram[rows, :] = gram[rows, :] - dot(turned[other : other + BLOCK], row)
+                high = low + BLOCK
+                row = block_dot(inverse, gram[low:high, :])
+                gram[low:high, :] = row
+                if high < size:
+                    gram[high:, low:high] = jnp.zeros((size - high, BLOCK), jnp.float32)
+                    gram[high:, :] = gram[high:, :] - block_dot(row[:, high:].T, row)
 
         return carry
 
@@ -130,14 +144,6 @@
     rows = lax.broadcasted_iota(jnp.int32, value.shape, 0) + offset
     cols = lax.broadcasted_iota(jnp.int32, value.shape, 1)
     return jnp.where(rows > cols, value, jnp.where(rows == cols, 0.5 * value, 0.0))
-
-
-def split(value, parts):
-    pieces = []
-    for _ in range(parts):
-        pieces.append(value.astype(jnp.bfloat16))
-        value = value - pieces[-1].astype(jnp.float32)
-    return pieces
 
 
 def dot3(left, right, contract=((1,), (0,))):
@@ -169,16 +175,55 @@
     inverse[mid:, :] = inverse_low[mid:] - dot3(low[mid:], inverse_low)
 
 
-def rotation(coeffs_ref, gram_ref, squares_ref, inverse, second, upper, work):
+def opening_kernel(coeffs_ref, squares_ref, upper, square):
     coeffs = coeffs_ref[...]
     mid = coeffs.shape[1] // 2
-    square = outer(coeffs, coeffs)
-    upper[...] = square + jnp.where(diagonal(square), squares_ref[...], 0.0)
+    value = outer(coeffs, coeffs)
+    upper[...] = value + jnp.where(diagonal(value), squares_ref[...], 0.0)
+    square[:mid, :] = dot(upper[:mid, :], upper[...])
+    square[mid:, :mid] = jnp.zeros((mid, mid), jnp.float32)
+    square[mid:, mid:] = dot(upper[mid:, :], upper[:, mid:])
+
+
+def opening(coeffs, squares):
+    modes = coeffs.shape[1]
+    spec = pl.BlockSpec(memory_space=pltpu.VMEM)
+    shape = jax.ShapeDtypeStruct((modes, modes), jnp.float32)
+    return pl.pallas_call(
+        opening_kernel, out_shape=(shape, shape), in_specs=[spec] * 2, out_specs=(spec, spec),
+        cost_estimate=pl.CostEstimate(
+            flops=12 * modes**3, bytes_accessed=8 * modes**2, transcendentals=0
+        ),
+    )(coeffs, squares)
+
+
+def coeffs_kernel(weight, snaps_ref, basis_ref, out_ref):
+    rows = basis_ref.shape[0]
+    chunk = chunk_of(rows)
+    total_value = None
+    for start in range(0, rows, chunk):
+        here = pl.ds(start, chunk)
+        term = dot3(snaps_ref[:, here], basis_ref[here, :])
+        total_value = term if total_value is None else total_value + term
+    out_ref[...] = total_value * weight
+
+
+def local_coeffs(snap_rows, old_basis, weight):
+    spec = pl.BlockSpec(memory_space=pltpu.VMEM)
+    return pl.pallas_call(
+        functools.partial(coeffs_kernel, weight),
+        out_shape=jax.ShapeDtypeStruct((snap_rows.shape[0], old_basis.shape[1]), jnp.float32),
+        in_specs=[spec] * 2, out_specs=spec,
+    )(snap_rows, old_basis)
+
+
+def rotation(coeffs_ref, gram_ref, upper, square_ref, inverse, second, work):
+    coeffs = coeffs_ref[...]
+    mid = coeffs.shape[1] // 2
+    square = square_ref
 
     def first_gram():
-        extra = outer(coeffs, dot(gram_ref[...], coeffs))
-        second[:mid, :] = dot(upper[:mid, :], upper[...]) + extra[:mid]
-        second[mid:, mid:] = dot(upper[mid:, :], upper[:, mid:]) + extra[mid:, mid:]
+        second[...] = square_ref[...] + outer(coeffs, dot(gram_ref[...], coeffs))
 
     first_gram()
 
@@ -240,15 +285,15 @@
 
 
 def update_kernel(
-    coeffs_ref, gram_ref, squares_ref, snaps_ref, basis_hbm, out_hbm,
-    inverse, second, upper, work, basis, out, loaded, stored,
+    coeffs_ref, gram_ref, squares_ref, upper, square_ref, snaps_ref, basis_hbm, out_hbm,
+    inverse, second, work, basis, out, loaded, stored,
 ):
     rows, modes = basis.shape
     snaps = coeffs_ref.shape[0]
     mid = modes // 2
     load = pltpu.make_async_copy(basis_hbm, basis, loaded)
     load.start()
-    rotation(coeffs_ref, gram_ref, squares_ref, inverse, second, upper, work)
+    rotation(coeffs_ref, gram_ref, upper, square_ref, inverse, second, work)
     final = inverse[...]
     turn_top, turn_low = split(final * squares_ref[...], 2)
     across_top, across_low = split(dot(final, coeffs_ref[...], NT).T, 2)
@@ -280,7 +325,7 @@
     return rows
 
 
-def updated_basis(coeffs, gram_res, squares, snap_rows, old_basis):
+def updated_basis(coeffs, gram_res, squares, upper, square, snap_rows, old_basis):
     rows, modes = old_basis.shape
     whole = pltpu.VMEM((modes, modes), jnp.float32)
     spec = pl.BlockSpec(memory_space=pltpu.VMEM)
@@ -288,15 +333,15 @@
     return pl.pallas_call(
         update_kernel,
         out_shape=jax.ShapeDtypeStruct((rows, modes), jnp.bfloat16),
-        in_specs=[spec] * 4 + [far],
+        in_specs=[spec] * 6 + [far],
         out_specs=far,
         scratch_shapes=[
-            whole, whole, whole, pltpu.VMEM((BLOCK, BLOCK), jnp.float32),
+            whole, whole, pltpu.VMEM((BLOCK, BLOCK), jnp.float32),
             pltpu.VMEM((rows, modes), jnp.float32), pltpu.VMEM((rows, modes), jnp.bfloat16),
             pltpu.SemaphoreType.DMA, pltpu.SemaphoreType.DMA((rows // chunk_of(rows),)),
         ],
         compiler_params=pltpu.CompilerParams(vmem_limit_bytes=48 * 1024 * 1024),
-    )(coeffs, gram_res, squares, snap_rows, old_basis)
+    )(coeffs, gram_res, squares, upper, square, snap_rows, old_basis)
 
 
 HIGH = lax.Precision.HIGH
@@ -308,32 +353,45 @@
     )
 
 
-def pair_rounds():
-    rounds = []
-    for name in ("slab", "tile"):
-        size = lax.axis_size(name)
-        step = 1
-        while step < size:
-            rounds.append((name, [(i, i ^ step) for i in range(size)]))
-            step *= 2
+AXES = ("tile", "slab")
+
+
+def exchange(part, mask):
+    count = lax.axis_size(AXES[0]) * lax.axis_size(AXES[1])
+    return lax.ppermute(part, AXES, [(i, i ^ mask) for i in range(count)])
+
+
+def sum_rounds():
+    count = lax.axis_size(AXES[0]) * lax.axis_size(AXES[1])
+    rounds, bit = [], 2
+    while bit < count:
+        rounds.append([bit, 2 * bit, 3 * bit] if 2 * bit < count else [bit])
+        bit *= 4
     return rounds
 
 
+def sum_round(part, masks):
+    others = [exchange(part, mask) for mask in masks]
+    if len(others) == 1:
+        return part + others[0]
+    return (part + others[0]) + (others[1] + others[2])
+
+
 def sum_all(part):
-    for name, pairs in pair_rounds():
-        part = part + lax.ppermute(part, name, pairs)
+    part = part + exchange(part, 1)
+    for masks in sum_rounds():
+        part = sum_round(part, masks)
     return part
 
 
 def sum_all_halved(part):
-    rounds = pair_rounds()
     half_rows = part.shape[0] // 2
-    first = lax.axis_index(rounds[0][0]) % 2 == 0
+    first = lax.axis_index(AXES[1]) % 2 == 0
     top, low = part[:half_rows], part[half_rows:]
-    kept = jnp.where(first, top, low) + lax.ppermute(jnp.where(first, low, top), *rounds[0])
-    for name, pairs in rounds[1:]:
-        kept = kept + lax.ppermute(kept, name, pairs)
-    other = lax.ppermute(kept, *rounds[0])
+    kept = jnp.where(first, top, low) + exchange(jnp.where(first, low, top), 1)
+    for masks in sum_rounds():
+        kept = sum_round(kept, masks)
+    other = exchange(kept, 1)
     return jnp.concatenate([jnp.where(first, kept, other), jnp.where(first, other, kept)], axis=0)
 
 
@@ -341,11 +399,13 @@
     snap_rows = lax.all_to_all(snapshots, "tile", split_axis=1, concat_axis=0, tiled=True)
     cell_count = old_basis.shape[0] * lax.axis_size("tile") * lax.axis_size("slab")
     weight_cell = 1.0 / cell_count
-    coeffs = sum_all_halved(mat(snap_rows, old_basis, ((1,), (0,))) * weight_cell)
+    coeffs = sum_all_halved(local_coeffs(snap_rows, old_basis, weight_cell))
     resid = snap_rows - mat(coeffs, old_basis, ((1,), (1,)))
-    gram_res = sum_all(mat(resid, resid, ((1,), (1,))) * weight_cell)
+    gram_part = mat(resid, resid, ((1,), (1,))) * weight_cell
     squares = (sing_values * sing_values)[None, :]
-    return updated_basis(coeffs, gram_res, squares, snap_rows, old_basis)
+    gram_res = sum_all(gram_part)
+    upper, square = opening(lax.optimization_barrier((coeffs, gram_part))[0], squares)
+    return updated_basis(coeffs, gram_res, squares, upper, square, snap_rows, old_basis)
 
 
 def solution(mesh):

time: 102 us -> 102 us (level)
  waiting for transfers between devices: 45.5 us -> 26.5 us
  starting transfers between devices: 15.2 us -> 23.6 us
  Pallas kernels: 35.2 us -> 40.7 us
  local copies, waits for them, and re-layouts: 0.01 us -> 3.24 us
  other arithmetic: 0.12 us -> 3.12 us
  matrix products: 5.98 us -> 4.51 us
    ppermute x11 -> x15, waiting for transfers between devices: 31.7 us -> 12.8 us  [exchange(): return lax.ppermute(part, AXES, [(i, i ^ mask) for i in range(count)])]
    ppermute x11 -> x15, starting transfers between devices: 7.86 us -> 16.3 us  [exchange(): return lax.ppermute(part, AXES, [(i, i ^ mask) for i in range(count)])]
    pallas_call x0 -> x2, Pallas kernels: none -> 8.21 us  [the longest x1 4.16 us: local_coeffs(): pl.pallas_call(functools.partial(coeffs_kernel, weight), out_shape=jax.Sh...]
    unnamed x4 -> x14, local copies, waits for them, and re-layouts: 0.01 us -> 3.24 us
    pallas_call x1, Pallas kernels: 35.2 us -> 32.4 us  [updated_basis(): pl.pallas_call(update_kernel, out_shape=jax.ShapeDtypeStruct((rows, modes...]
    dot_general x3 -> x2, matrix products: 5.98 us -> 4.51 us  [mat(): lax.dot_general(left, right, (contract, ((), ())), precision=precision, p...]
  transfers between devices with their start and end apart: 12 -> 16, of which waited for: 12 -> 12; matrix products, arithmetic and copies ran while one was open for 0% -> 1% of each run, Pallas kernels for 0% -> 4%
where the time goes in v2:
time: 102 us
  Pallas kernels  40.7 us (40%)
  waiting for transfers between devices  26.5 us (26%)
  starting transfers between devices  23.6 us (23%)
  matrix products  4.51 us (4%)
  local copies, waits for them, and re-layouts  3.24 us (3%)
  other arithmetic  3.12 us (3%)
    pallas_call x1, Pallas kernels, updated_basis(): pl.pallas_call(update_kernel, out_shape=jax.ShapeDtypeStruct((rows, modes...  32.4 us
    ppermute x15, starting transfers between devices, exchange(): return lax.ppermute(part, AXES, [(i, i ^ mask) for i in range(count)])  16.3 us
    all_to_all x1, waiting for transfers between devices, local(): lax.all_to_all(snapshots, 'tile', split_axis=1, concat_axis=0, tiled=True)  13.8 us
    ppermute x15, waiting for transfers between devices, exchange(): return lax.ppermute(part, AXES, [(i, i ^ mask) for i in range(count)])  12.8 us
    all_to_all x1, starting transfers between devices, local(): lax.all_to_all(snapshots, 'tile', split_axis=1, concat_axis=0, tiled=True)  7.31 us
    dot_general x2, matrix products, mat(): lax.dot_general(left, right, (contract, ((), ())), precision=precision, p...  4.51 us
    pallas_call x1, Pallas kernels, local_coeffs(): pl.pallas_call(functools.partial(coeffs_kernel, weight), out_shape=jax.Sh...  4.16 us
    pallas_call x1, Pallas kernels, opening(): pl.pallas_call(opening_kernel, out_shape=(shape, shape), in_specs=[spec]...  4.05 us
  transfers between devices with their start and end apart: 16, of which 12 were waited for; matrix products, arithmetic and copies ran while one was open for 1% of the time, Pallas kernels for 4%

profile of v2, /device:TPU:0, one launch (start us, length us, event | category | flops | bytes accessed | tf_op | source)
XLA Modules:
  0.0 102.0 jit_solution(6426502507337948115)
XLA Ops:
  0.0 7.3 %all-to-all-start = ((f32[8,8,1920]{2,0,1:T(8,128)}), f32[8,8,1920]{2,0,1:T(8,128)S(1)}, u32[]{:S(2)}, u32[]{:S(2)}) async-start(f32[8,8,1920]{2,0,1:T(8,128)} %bitcast.13), calls=%async_computation | async-start | bytes 983040 | tf_op jit(solution)/shard_map/all_to_all | solution.py:399
  7.3 13.8 %all-to-all-done = f32[8,8,1920]{2,0,1:T(8,128)S(1)} async-done(((f32[8,8,1920]{2,0,1:T(8,128)}), f32[8,8,1920]{2,0,1:T(8,128)S(1)}, u32[]{:S(2)}, u32[]{:S(2)}) %all-to-all-start) | async-done | bytes 491552 | tf_op jit(solution)/shard_map/all_to_all | solution.py:399
  21.1 0.0 copy-start
  21.1 0.8 copy-done
  21.9 4.2 %shard_map.37 = f32[64,512]{1,0:T(8,128)} custom-call(f32[64,1920]{1,0:T(8,128)} %bitcast.9, f32[1920,512]{1,0:T(8,128)} %basis_hbm.1), custom_call_target="tpu_custom_call" | custom-call | tf_op jit(solution)/shard_map/pallas_call | solution.py:213
  26.0 0.0 copy-start.6
  26.0 0.9 slice_select_fusion
  26.9 0.1 collective-permute-start
  27.0 1.2 %collective-permute-done = f32[32,512]{1,0:T(8,128)S(1)} collective-permute-done((f32[32,512]{1,0:T(8,128)S(1)}, f32[32,512]{1,0:T(8,128)S(1)}, u32[]{:S(2)}, u32[]{:S(2)}) %collective-permute-start) | collective-permute-done | bytes 65568 | tf_op jit(solution)/shard_map/ppermute | solution.py:361
  28.3 0.9 select_add_fusion
  29.1 2.5 %collective-permute-start.3 = (f32[32,512]{1,0:T(8,128)S(1)}, f32[32,512]{1,0:T(8,128)S(1)}, u32[]{:S(2)}, u32[]{:S(2)}) collective-permute-start(f32[32,512]{1,0:T(8,128)S(1)} %select_add_fusion), channel_id=1, source_target_pairs={{0,6},{1,7},{2,4},{3,5},{4,2},{5,3},{6,0},{7,1},{8,14},{9,15},{10,... | collective-permute-start | bytes 196616 | tf_op jit(solution)/shard_map/ppermute | solution.py:361
  31.6 0.6 collective-permute-start.2
  32.2 0.5 collective-permute-start.1
  32.7 1.7 %collective-permute-done.3 = f32[32,512]{1,0:T(8,128)S(1)} collective-permute-done((f32[32,512]{1,0:T(8,128)S(1)}, f32[32,512]{1,0:T(8,128)S(1)}, u32[]{:S(2)}, u32[]{:S(2)}) %collective-permute-start.3) | collective-permute-done | bytes 65568 | tf_op jit(solution)/shard_map/ppermute | solution.py:361
  34.4 1.5 %collective-permute-done.2 = f32[32,512]{1,0:T(8,128)S(1)} collective-permute-done((f32[32,512]{1,0:T(8,128)S(1)}, f32[32,512]{1,0:T(8,128)S(1)}, u32[]{:S(2)}, u32[]{:S(2)}) %collective-permute-start.2) | collective-permute-done | bytes 65568 | tf_op jit(solution)/shard_map/ppermute | solution.py:361
  35.9 0.6 collective-permute-done.1
  36.5 1.2 %collective-permute-start.6 = (f32[32,512]{1,0:T(8,128)S(1)}, f32[32,512]{1,0:T(8,128)S(1)}, u32[]{:S(2)}, u32[]{:S(2)}) collective-permute-start(f32[32,512]{1,0:T(8,128)S(1)} %add_add_fusion.1), channel_id=1, source_target_pairs={{0,24},{1,25},{2,26},{3,27},{4,28},{5,29},{6,30},{7,31},{8,16},{9,... | collective-permute-start | bytes 196616 | tf_op jit(solution)/shard_map/ppermute | solution.py:361
  37.7 1.1 %collective-permute-start.5 = (f32[32,512]{1,0:T(8,128)S(1)}, f32[32,512]{1,0:T(8,128)S(1)}, u32[]{:S(2)}, u32[]{:S(2)}) collective-permute-start(f32[32,512]{1,0:T(8,128)S(1)} %add_add_fusion.1), channel_id=1, source_target_pairs={{0,16},{1,17},{2,18},{3,19},{4,20},{5,21},{6,22},{7,23},{8,24},{9,... | collective-permute-start | bytes 196616 | tf_op jit(solution)/shard_map/ppermute | solution.py:361
  38.8 2.1 %collective-permute-start.4 = (f32[32,512]{1,0:T(8,128)S(1)}, f32[32,512]{1,0:T(8,128)S(1)}, u32[]{:S(2)}, u32[]{:S(2)}) collective-permute-start(f32[32,512]{1,0:T(8,128)S(1)} %add_add_fusion.1), channel_id=1, source_target_pairs={{0,8},{1,9},{2,10},{3,11},{4,12},{5,13},{6,14},{7,15},{8,0},{9,1},... | collective-permute-start | bytes 196616 | tf_op jit(solution)/shard_map/ppermute | solution.py:361
  40.9 1.8 %collective-permute-done.6 = f32[32,512]{1,0:T(8,128)S(1)} collective-permute-done((f32[32,512]{1,0:T(8,128)S(1)}, f32[32,512]{1,0:T(8,128)S(1)}, u32[]{:S(2)}, u32[]{:S(2)}) %collective-permute-start.6) | collective-permute-done | bytes 65568 | tf_op jit(solution)/shard_map/ppermute | solution.py:361
  42.7 1.6 %collective-permute-done.5 = f32[32,512]{1,0:T(8,128)S(1)} collective-permute-done((f32[32,512]{1,0:T(8,128)S(1)}, f32[32,512]{1,0:T(8,128)S(1)}, u32[]{:S(2)}, u32[]{:S(2)}) %collective-permute-start.5) | collective-permute-done | bytes 65568 | tf_op jit(solution)/shard_map/ppermute | solution.py:361
  44.3 0.0 collective-permute-done.4
  44.3 0.1 collective-permute-start.7
  44.4 1.2 %collective-permute-done.7 = f32[32,512]{1,0:T(8,128)S(1)} collective-permute-done((f32[32,512]{1,0:T(8,128)S(1)}, f32[32,512]{1,0:T(8,128)S(1)}, u32[]{:S(2)}, u32[]{:S(2)}) %collective-permute-start.7) | collective-permute-done | bytes 65568 | tf_op jit(solution)/shard_map/ppermute | solution.py:361
  45.7 4.1 %convolution_subtract_fusion = f32[64,1920]{1,0:T(8,128)S(1)} fusion(f32[1920,512]{1,0:T(8,128)} %basis_hbm.1, f32[8,8,1920]{2,0,1:T(8,128)} %copy-done, f32[32,512]{1,0:T(8,128)S(1)} %get-tuple-element.12, f32[32,512]{1,0:T(8,128)S(1)} %get-tuple-element.11), kind=kOutput, calls=%fused_computation | convolution fusion | flops 377643008 | bytes 5046272 | tf_op jit(solution)/shard_map/dot_general | solution.py:351
  49.8 0.0 copy-start.1
  49.8 0.4 convolution_multiply_fusion
  50.2 0.2 collective-permute-start.8
  50.4 0.0 copy-done.6
  50.4 0.6 mul.11
  51.0 0.0 copy-start.5
  51.0 0.4 collective-permute-done.8
  51.5 1.7 %collective-permute-start.11 = (f32[64,64]{1,0:T(8,128)S(1)}, f32[64,64]{1,0:T(8,128)S(1)}, u32[]{:S(2)}, u32[]{:S(2)}) collective-permute-start(f32[64,64]{1,0:T(8,128)S(1)} %add.54), channel_id=1, source_target_pairs={{0,6},{1,7},{2,4},{3,5},{4,2},{5,3},{6,0},{7,1},{8,14},{9,15},{10,... | collective-permute-start | bytes 49160 | tf_op jit(solution)/shard_map/ppermute | solution.py:361
  53.1 1.3 %collective-permute-start.10 = (f32[64,64]{1,0:T(8,128)S(1)}, f32[64,64]{1,0:T(8,128)S(1)}, u32[]{:S(2)}, u32[]{:S(2)}) collective-permute-start(f32[64,64]{1,0:T(8,128)S(1)} %add.54), channel_id=1, source_target_pairs={{0,4},{1,5},{2,6},{3,7},{4,0},{5,1},{6,2},{7,3},{8,12},{9,13},{10,... | collective-permute-start | bytes 49160 | tf_op jit(solution)/shard_map/ppermute | solution.py:361
  54.4 0.6 collective-permute-start.9
  55.0 0.7 pad_maximum_fusion.coeffs_ref
  55.6 0.0 copy-start.4
  55.6 0.7 collective-permute-done.11
  56.3 0.7 collective-permute-done.10
  57.0 1.3 %collective-permute-done.9 = f32[64,64]{1,0:T(8,128)S(1)} collective-permute-done((f32[64,64]{1,0:T(8,128)S(1)}, f32[64,64]{1,0:T(8,128)S(1)}, u32[]{:S(2)}, u32[]{:S(2)}) %collective-permute-start.9) | collective-permute-done | bytes 16416 | tf_op jit(solution)/shard_map/ppermute | solution.py:361
  58.3 1.2 %collective-permute-start.14 = (f32[64,64]{1,0:T(8,128)S(1)}, f32[64,64]{1,0:T(8,128)S(1)}, u32[]{:S(2)}, u32[]{:S(2)}) collective-permute-start(f32[64,64]{1,0:T(8,128)S(1)} %add_add_fusion.3), channel_id=1, source_target_pairs={{0,24},{1,25},{2,26},{3,27},{4,28},{5,29},{6,30},{7,31},{8,16},{9,... | collective-permute-start | bytes 49160 | tf_op jit(solution)/shard_map/ppermute | solution.py:361
  59.5 0.5 collective-permute-start.13
  60.0 2.8 %collective-permute-start.12 = (f32[64,64]{1,0:T(8,128)S(1)}, f32[64,64]{1,0:T(8,128)S(1)}, u32[]{:S(2)}, u32[]{:S(2)}) collective-permute-start(f32[64,64]{1,0:T(8,128)S(1)} %add_add_fusion.3), channel_id=1, source_target_pairs={{0,8},{1,9},{2,10},{3,11},{4,12},{5,13},{6,14},{7,15},{8,0},{9,1},... | collective-permute-start | bytes 49160 | tf_op jit(solution)/shard_map/ppermute | solution.py:361
  62.8 4.0 %shard_map.38 = (f32[512,512]{1,0:T(8,128)}, f32[512,512]{1,0:T(8,128)}) custom-call(f32[64,512]{1,0:T(8,128)} %pad_maximum_fusion.coeffs_ref, f32[1,512]{1,0:T(1,128)} %bitcast.11), custom_call_target="tpu_custom_call" | custom-call | flops 1610612736 | bytes 2097152 | tf_op jit(solution)/shard_map/pallas_call | solution.py:192
  66.8 0.0 collective-permute-done.14
  66.8 0.0 collective-permute-done.13
  66.8 0.0 collective-permute-done.12
  66.9 0.0 copy-done.1
  66.9 0.0 copy-done.5
  66.9 0.0 copy-done.4
  66.9 0.0 copy-start.2
  66.9 1.2 %copy-done.2 = f32[512,512]{1,0:T(8,128)S(1)} copy-done((f32[512,512]{1,0:T(8,128)S(1)}, f32[512,512]{1,0:T(8,128)}, u32[]{:S(2)}) %copy-start.2) | copy-done | bytes 1048600
  68.1 0.0 copy-start.3
  68.1 1.2 %copy-done.3 = f32[512,512]{1,0:T(8,128)S(1)} copy-done((f32[512,512]{1,0:T(8,128)S(1)}, f32[512,512]{1,0:T(8,128)}, u32[]{:S(2)}) %copy-start.3) | copy-done | bytes 1048600
  69.3 32.4 %shard_map.39 = bf16[1920,512]{1,0:T(8,128)(2,1)} custom-call(f32[64,512]{1,0:T(8,128)S(1)} %copy-done.4, f32[64,64]{1,0:T(8,128)S(1)} %add_add_fusion.2.gram_ref, f32[1,512]{1,0:T(1,128)S(1)} %bitcast.12, f32[512,512]{1,0:T(8,128)S(1)} %copy-done.2, f32[512,512]{1,0:T(8,128)S(1)} %copy-done.3, f32[64,1920]{1,0:T(8,128)S(1)} %bitcast.10, f32[1920,512]{1,0:T(8,128)} %basis_hbm.1), custom_call_target="tpu_custom_call" | custom-call | tf_op jit(solution)/shard_map/pallas_call | solution.py:333
  (6 shorter events, 0.1 us)
Async XLA Ops:
  0.0 21.1 %all-to-all-start = ((f32[8,8,1920]{2,0,1:T(8,128)}), f32[8,8,1920]{2,0,1:T(8,128)S(1)}, u32[]{:S(2)}, u32[]{:S(2)}) async-start(f32[8,8,1920]{2,0,1:T(8,128)} %bitcast.13), calls=%async_computation | async-start | bytes 983040 | tf_op jit(solution)/shard_map/all_to_all | solution.py:399
  21.1 0.8 copy-start
  26.0 24.4 %copy-start.6 = (f32[512]{0:T(512)S(1)}, f32[512]{0:T(512)}, u32[]{:S(2)}) copy-start(f32[512]{0:T(512)} %param.5) | copy-start | bytes 6148
  26.9 1.3 %collective-permute-start = (f32[32,512]{1,0:T(8,128)S(1)}, f32[32,512]{1,0:T(8,128)S(1)}, u32[]{:S(2)}, u32[]{:S(2)}) collective-permute-start(f32[32,512]{1,0:T(8,128)S(1)} %slice_select_fusion), channel_id=1, source_target_pairs={{0,1},{1,0},{2,3},{3,2},{4,5},{5,4},{6,7},{7,6},{8,9},{9,8},{10,11... | collective-permute-start | bytes 196616 | tf_op jit(solution)/shard_map/ppermute | solution.py:361
  29.1 5.3 %collective-permute-start.3 = (f32[32,512]{1,0:T(8,128)S(1)}, f32[32,512]{1,0:T(8,128)S(1)}, u32[]{:S(2)}, u32[]{:S(2)}) collective-permute-start(f32[32,512]{1,0:T(8,128)S(1)} %select_add_fusion), channel_id=1, source_target_pairs={{0,6},{1,7},{2,4},{3,5},{4,2},{5,3},{6,0},{7,1},{8,14},{9,15},{10,... | collective-permute-start | bytes 196616 | tf_op jit(solution)/shard_map/ppermute | solution.py:361
  31.6 4.3 %collective-permute-start.2 = (f32[32,512]{1,0:T(8,128)S(1)}, f32[32,512]{1,0:T(8,128)S(1)}, u32[]{:S(2)}, u32[]{:S(2)}) collective-permute-start(f32[32,512]{1,0:T(8,128)S(1)} %select_add_fusion), channel_id=1, source_target_pairs={{0,4},{1,5},{2,6},{3,7},{4,0},{5,1},{6,2},{7,3},{8,12},{9,13},{10,... | collective-permute-start | bytes 196616 | tf_op jit(solution)/shard_map/ppermute | solution.py:361
  32.2 4.3 %collective-permute-start.1 = (f32[32,512]{1,0:T(8,128)S(1)}, f32[32,512]{1,0:T(8,128)S(1)}, u32[]{:S(2)}, u32[]{:S(2)}) collective-permute-start(f32[32,512]{1,0:T(8,128)S(1)} %select_add_fusion), channel_id=1, source_target_pairs={{0,2},{1,3},{2,0},{3,1},{4,6},{5,7},{6,4},{7,5},{8,10},{9,11},{10,... | collective-permute-start | bytes 196616 | tf_op jit(solution)/shard_map/ppermute | solution.py:361
  36.5 6.2 %collective-permute-start.6 = (f32[32,512]{1,0:T(8,128)S(1)}, f32[32,512]{1,0:T(8,128)S(1)}, u32[]{:S(2)}, u32[]{:S(2)}) collective-permute-start(f32[32,512]{1,0:T(8,128)S(1)} %add_add_fusion.1), channel_id=1, source_target_pairs={{0,24},{1,25},{2,26},{3,27},{4,28},{5,29},{6,30},{7,31},{8,16},{9,... | collective-permute-start | bytes 196616 | tf_op jit(solution)/shard_map/ppermute | solution.py:361
  37.7 6.6 %collective-permute-start.5 = (f32[32,512]{1,0:T(8,128)S(1)}, f32[32,512]{1,0:T(8,128)S(1)}, u32[]{:S(2)}, u32[]{:S(2)}) collective-permute-start(f32[32,512]{1,0:T(8,128)S(1)} %add_add_fusion.1), channel_id=1, source_target_pairs={{0,16},{1,17},{2,18},{3,19},{4,20},{5,21},{6,22},{7,23},{8,24},{9,... | collective-permute-start | bytes 196616 | tf_op jit(solution)/shard_map/ppermute | solution.py:361
  38.8 5.5 %collective-permute-start.4 = (f32[32,512]{1,0:T(8,128)S(1)}, f32[32,512]{1,0:T(8,128)S(1)}, u32[]{:S(2)}, u32[]{:S(2)}) collective-permute-start(f32[32,512]{1,0:T(8,128)S(1)} %add_add_fusion.1), channel_id=1, source_target_pairs={{0,8},{1,9},{2,10},{3,11},{4,12},{5,13},{6,14},{7,15},{8,0},{9,1},... | collective-permute-start | bytes 196616 | tf_op jit(solution)/shard_map/ppermute | solution.py:361
  44.3 1.3 %collective-permute-start.7 = (f32[32,512]{1,0:T(8,128)S(1)}, f32[32,512]{1,0:T(8,128)S(1)}, u32[]{:S(2)}, u32[]{:S(2)}) collective-permute-start(f32[32,512]{1,0:T(8,128)S(1)} %add_add_fusion), channel_id=1, source_target_pairs={{0,1},{1,0},{2,3},{3,2},{4,5},{5,4},{6,7},{7,6},{8,9},{9,8},{10,11... | collective-permute-start | bytes 196616 | tf_op jit(solution)/shard_map/ppermute | solution.py:361
  49.8 17.1 %copy-start.1 = (f32[8,8,1920]{2,0,1:T(8,128)S(1)}, f32[8,8,1920]{2,0,1:T(8,128)}, u32[]{:S(2)}) copy-start(f32[8,8,1920]{2,0,1:T(8,128)} %copy-done) | copy-start | bytes 1474564
  50.2 1.3 %collective-permute-start.8 = (f32[64,64]{1,0:T(8,128)S(1)}, f32[64,64]{1,0:T(8,128)S(1)}, u32[]{:S(2)}, u32[]{:S(2)}) collective-permute-start(f32[64,64]{1,0:T(8,128)S(1)} %convolution_multiply_fusion), channel_id=1, source_target_pairs={{0,1},{1,0},{2,3},{3,2},{4,5},{5,4},{6,7},{7,6},{8,9},{9,8},{10,11... | collective-permute-start | bytes 49160 | tf_op jit(solution)/shard_map/ppermute | solution.py:361
  51.0 15.9 %copy-start.5 = (f32[512]{0:T(512)S(1)}, f32[512]{0:T(512)}, u32[]{:S(2)}) copy-start(f32[512]{0:T(512)} %mul.11) | copy-start | bytes 6148
  51.5 4.8 %collective-permute-start.11 = (f32[64,64]{1,0:T(8,128)S(1)}, f32[64,64]{1,0:T(8,128)S(1)}, u32[]{:S(2)}, u32[]{:S(2)}) collective-permute-start(f32[64,64]{1,0:T(8,128)S(1)} %add.54), channel_id=1, source_target_pairs={{0,6},{1,7},{2,4},{3,5},{4,2},{5,3},{6,0},{7,1},{8,14},{9,15},{10,... | collective-permute-start | bytes 49160 | tf_op jit(solution)/shard_map/ppermute | solution.py:361
  53.1 3.9 %collective-permute-start.10 = (f32[64,64]{1,0:T(8,128)S(1)}, f32[64,64]{1,0:T(8,128)S(1)}, u32[]{:S(2)}, u32[]{:S(2)}) collective-permute-start(f32[64,64]{1,0:T(8,128)S(1)} %add.54), channel_id=1, source_target_pairs={{0,4},{1,5},{2,6},{3,7},{4,0},{5,1},{6,2},{7,3},{8,12},{9,13},{10,... | collective-permute-start | bytes 49160 | tf_op jit(solution)/shard_map/ppermute | solution.py:361
  54.4 3.9 %collective-permute-start.9 = (f32[64,64]{1,0:T(8,128)S(1)}, f32[64,64]{1,0:T(8,128)S(1)}, u32[]{:S(2)}, u32[]{:S(2)}) collective-permute-start(f32[64,64]{1,0:T(8,128)S(1)} %add.54), channel_id=1, source_target_pairs={{0,2},{1,3},{2,0},{3,1},{4,6},{5,7},{6,4},{7,5},{8,10},{9,11},{10,... | collective-permute-start | bytes 49160 | tf_op jit(solution)/shard_map/ppermute | solution.py:361
  55.6 11.3 %copy-start.4 = (f32[64,512]{1,0:T(8,128)S(1)}, f32[64,512]{1,0:T(8,128)}, u32[]{:S(2)}) copy-start(f32[64,512]{1,0:T(8,128)} %pad_maximum_fusion.coeffs_ref) | copy-start | bytes 393220
  58.3 8.5 %collective-permute-start.14 = (f32[64,64]{1,0:T(8,128)S(1)}, f32[64,64]{1,0:T(8,128)S(1)}, u32[]{:S(2)}, u32[]{:S(2)}) collective-permute-start(f32[64,64]{1,0:T(8,128)S(1)} %add_add_fusion.3), channel_id=1, source_target_pairs={{0,24},{1,25},{2,26},{3,27},{4,28},{5,29},{6,30},{7,31},{8,16},{9,... | collective-permute-start | bytes 49160 | tf_op jit(solution)/shard_map/ppermute | solution.py:361
  59.5 7.3 %collective-permute-start.13 = (f32[64,64]{1,0:T(8,128)S(1)}, f32[64,64]{1,0:T(8,128)S(1)}, u32[]{:S(2)}, u32[]{:S(2)}) collective-permute-start(f32[64,64]{1,0:T(8,128)S(1)} %add_add_fusion.3), channel_id=1, source_target_pairs={{0,16},{1,17},{2,18},{3,19},{4,20},{5,21},{6,22},{7,23},{8,24},{9,... | collective-permute-start | bytes 49160 | tf_op jit(solution)/shard_map/ppermute | solution.py:361
  60.0 6.9 %collective-permute-start.12 = (f32[64,64]{1,0:T(8,128)S(1)}, f32[64,64]{1,0:T(8,128)S(1)}, u32[]{:S(2)}, u32[]{:S(2)}) collective-permute-start(f32[64,64]{1,0:T(8,128)S(1)} %add_add_fusion.3), channel_id=1, source_target_pairs={{0,8},{1,9},{2,10},{3,11},{4,12},{5,13},{6,14},{7,15},{8,0},{9,1},... | collective-permute-start | bytes 49160 | tf_op jit(solution)/shard_map/ppermute | solution.py:361
  66.9 1.2 %copy-start.2 = (f32[512,512]{1,0:T(8,128)S(1)}, f32[512,512]{1,0:T(8,128)}, u32[]{:S(2)}) copy-start(f32[512,512]{1,0:T(8,128)} %get-tuple-element.9.upper) | copy-start | bytes 3145732
  68.1 1.2 %copy-start.3 = (f32[512,512]{1,0:T(8,128)S(1)}, f32[512,512]{1,0:T(8,128)}, u32[]{:S(2)}) copy-start(f32[512,512]{1,0:T(8,128)} %get-tuple-element.10.square_ref) | copy-start | bytes 3145732

commit v3 on v2

--- a/solution.py
+++ b/solution.py
@@ -9,6 +9,7 @@
 
 HIGHEST = lax.Precision.HIGHEST
 BLOCK = 128
+VMEM = 28 * 1024 * 1024
 
 
 def dot(left, right, contract=((1,), (0,)), precision=HIGHEST):
@@ -191,30 +192,11 @@
     shape = jax.ShapeDtypeStruct((modes, modes), jnp.float32)
     return pl.pallas_call(
         opening_kernel, out_shape=(shape, shape), in_specs=[spec] * 2, out_specs=(spec, spec),
+        compiler_params=pltpu.CompilerParams(vmem_limit_bytes=VMEM),
         cost_estimate=pl.CostEstimate(
             flops=12 * modes**3, bytes_accessed=8 * modes**2, transcendentals=0
         ),
     )(coeffs, squares)
-
-
-def coeffs_kernel(weight, snaps_ref, basis_ref, out_ref):
-    rows = basis_ref.shape[0]
-    chunk = chunk_of(rows)
-    total_value = None
-    for start in range(0, rows, chunk):
-        here = pl.ds(start, chunk)
-        term = dot3(snaps_ref[:, here], basis_ref[here, :])
-        total_value = term if total_value is None else total_value + term
-    out_ref[...] = total_value * weight
-
-
-def local_coeffs(snap_rows, old_basis, weight):
-    spec = pl.BlockSpec(memory_space=pltpu.VMEM)
-    return pl.pallas_call(
-        functools.partial(coeffs_kernel, weight),
-        out_shape=jax.ShapeDtypeStruct((snap_rows.shape[0], old_basis.shape[1]), jnp.float32),
-        in_specs=[spec] * 2, out_specs=spec,
-    )(snap_rows, old_basis)
 
 
 def rotation(coeffs_ref, gram_ref, upper, square_ref, inverse, second, work):
@@ -340,7 +322,7 @@
             pltpu.VMEM((rows, modes), jnp.float32), pltpu.VMEM((rows, modes), jnp.bfloat16),
             pltpu.SemaphoreType.DMA, pltpu.SemaphoreType.DMA((rows // chunk_of(rows),)),
         ],
-        compiler_params=pltpu.CompilerParams(vmem_limit_bytes=48 * 1024 * 1024),
+        compiler_params=pltpu.CompilerParams(vmem_limit_bytes=VMEM),
     )(coeffs, gram_res, squares, upper, square, snap_rows, old_basis)
 
 
@@ -399,7 +381,7 @@
     snap_rows = lax.all_to_all(snapshots, "tile", split_axis=1, concat_axis=0, tiled=True)
     cell_count = old_basis.shape[0] * lax.axis_size("tile") * lax.axis_size("slab")
     weight_cell = 1.0 / cell_count
-    coeffs = sum_all_halved(local_coeffs(snap_rows, old_basis, weight_cell))
+    coeffs = sum_all_halved(mat(snap_rows, old_basis, ((1,), (0,))) * weight_cell)
     resid = snap_rows - mat(coeffs, old_basis, ((1,), (1,)))
     gram_part = mat(resid, resid, ((1,), (1,))) * weight_cell
     squares = (sing_values * sing_values)[None, :]

time: 102 us -> 92.9 us (0.911)
  Pallas kernels: 40.7 us -> 34.9 us
  local copies, waits for them, and re-layouts: 3.24 us -> 0.01 us
  other arithmetic: 3.12 us -> 0.12 us
  matrix products: 4.51 us -> 5.98 us
  waiting for transfers between devices: 26.5 us -> 27.8 us
    pallas_call x1 -> x0, Pallas kernels: 4.16 us -> none  [local_coeffs(): pl.pallas_call(functools.partial(coeffs_kernel, weight), out_shape=jax.Sh...]
    unnamed x14 -> x4, local copies, waits for them, and re-layouts: 3.24 us -> 0.01 us
    pallas_call x1, Pallas kernels: 4.05 us -> 2.15 us  [opening(): pl.pallas_call(opening_kernel, out_shape=(shape, shape), in_specs=[spec]...]
    dot_general x2 -> x3, matrix products: 4.51 us -> 5.98 us  [mat(): lax.dot_general(left, right, (contract, ((), ())), precision=precision, p...]
    ppermute x15, waiting for transfers between devices: 12.8 us -> 14 us  [exchange(): return lax.ppermute(part, AXES, [(i, i ^ mask) for i in range(count)])]
  transfers between devices with their start and end apart: 16 -> 16, of which waited for: 12 -> 12; matrix products, arithmetic and copies ran while one was open for 1% -> 0% of each run, Pallas kernels for 4% -> 2%
where the time goes in v3:
time: 92.9 us; the launch traced here: 92.7 us
  Pallas kernels  34.9 us (38%)
  waiting for transfers between devices  27.8 us (30%)
  starting transfers between devices  23.6 us (25%)
  matrix products  5.98 us (6%)
    pallas_call x1, Pallas kernels, updated_basis(): pl.pallas_call(update_kernel, out_shape=jax.ShapeDtypeStruct((rows, modes...  32.7 us
    ppermute x15, starting transfers between devices, exchange(): return lax.ppermute(part, AXES, [(i, i ^ mask) for i in range(count)])  16.3 us
    ppermute x15, waiting for transfers between devices, exchange(): return lax.ppermute(part, AXES, [(i, i ^ mask) for i in range(count)])  14 us
    all_to_all x1, waiting for transfers between devices, local(): lax.all_to_all(snapshots, 'tile', split_axis=1, concat_axis=0, tiled=True)  13.8 us
    all_to_all x1, starting transfers between devices, local(): lax.all_to_all(snapshots, 'tile', split_axis=1, concat_axis=0, tiled=True)  7.31 us
    dot_general x3, matrix products, mat(): lax.dot_general(left, right, (contract, ((), ())), precision=precision, p...  5.98 us
    pallas_call x1, Pallas kernels, opening(): pl.pallas_call(opening_kernel, out_shape=(shape, shape), in_specs=[spec]...  2.15 us
  transfers between devices with their start and end apart: 16, of which 12 were waited for; matrix products, arithmetic and copies ran while one was open for 0% of the time, Pallas kernels for 2%

profile of v3, /device:TPU:0, one launch (start us, length us, event | category | flops | bytes accessed | tf_op | source)
XLA Modules:
  0.0 92.7 jit_solution(4754273485761872254)
XLA Ops:
  0.0 7.3 %all-to-all-start = ((f32[8,8,1920]{2,0,1:T(8,128)}), f32[8,8,1920]{2,0,1:T(8,128)S(1)}, u32[]{:S(2)}, u32[]{:S(2)}) async-start(f32[8,8,1920]{2,0,1:T(8,128)} %bitcast.15), calls=%async_computation | async-start | bytes 983040 | tf_op jit(solution)/shard_map/all_to_all | solution.py:381
  7.3 13.8 %all-to-all-done = f32[8,8,1920]{2,0,1:T(8,128)S(1)} async-done(((f32[8,8,1920]{2,0,1:T(8,128)}), f32[8,8,1920]{2,0,1:T(8,128)S(1)}, u32[]{:S(2)}, u32[]{:S(2)}) %all-to-all-start) | async-done | bytes 491552 | tf_op jit(solution)/shard_map/all_to_all | solution.py:381
  21.1 0.0 copy-start
  21.1 3.6 %convolution_multiply_fusion = f32[64,512]{1,0:T(8,128)S(1)} fusion(f32[1920,512]{1,0:T(8,128)} %basis_hbm.1, f32[8,8,1920]{2,0,1:T(8,128)S(1)} %all-to-all-done), kind=kOutput, calls=%fused_computation.1 | convolution fusion | flops 377520128 | bytes 4554752 | tf_op jit(solution)/shard_map/dot_general | solution.py:333
  24.7 0.0 copy-start.1
  24.7 0.1 collective-permute-start
  24.8 1.2 %collective-permute-done = f32[32,512]{1,0:T(8,128)S(1)} collective-permute-done((f32[32,512]{1,0:T(8,128)S(1)}, f32[32,512]{1,0:T(8,128)S(1)}, u32[]{:S(2)}, u32[]{:S(2)}) %collective-permute-start) | collective-permute-done | bytes 65568 | tf_op jit(solution)/shard_map/ppermute | solution.py:343
  26.1 2.5 %collective-permute-start.3 = (f32[32,512]{1,0:T(8,128)S(1)}, f32[32,512]{1,0:T(8,128)S(1)}, u32[]{:S(2)}, u32[]{:S(2)}) collective-permute-start(f32[32,512]{1,0:T(8,128)S(1)} %select_add_fusion), channel_id=1, source_target_pairs={{0,6},{1,7},{2,4},{3,5},{4,2},{5,3},{6,0},{7,1},{8,14},{9,15},{10,... | collective-permute-start | bytes 196616 | tf_op jit(solution)/shard_map/ppermute | solution.py:343
  28.5 0.6 collective-permute-start.2
  29.1 0.5 collective-permute-start.1
  29.6 1.7 %collective-permute-done.3 = f32[32,512]{1,0:T(8,128)S(1)} collective-permute-done((f32[32,512]{1,0:T(8,128)S(1)}, f32[32,512]{1,0:T(8,128)S(1)}, u32[]{:S(2)}, u32[]{:S(2)}) %collective-permute-start.3) | collective-permute-done | bytes 65568 | tf_op jit(solution)/shard_map/ppermute | solution.py:343
  31.3 1.5 %collective-permute-done.2 = f32[32,512]{1,0:T(8,128)S(1)} collective-permute-done((f32[32,512]{1,0:T(8,128)S(1)}, f32[32,512]{1,0:T(8,128)S(1)}, u32[]{:S(2)}, u32[]{:S(2)}) %collective-permute-start.2) | collective-permute-done | bytes 65568 | tf_op jit(solution)/shard_map/ppermute | solution.py:343
  32.8 0.6 collective-permute-done.1
  33.4 1.2 %collective-permute-start.6 = (f32[32,512]{1,0:T(8,128)S(1)}, f32[32,512]{1,0:T(8,128)S(1)}, u32[]{:S(2)}, u32[]{:S(2)}) collective-permute-start(f32[32,512]{1,0:T(8,128)S(1)} %add_add_fusion.1), channel_id=1, source_target_pairs={{0,24},{1,25},{2,26},{3,27},{4,28},{5,29},{6,30},{7,31},{8,16},{9,... | collective-permute-start | bytes 196616 | tf_op jit(solution)/shard_map/ppermute | solution.py:343
  34.6 1.1 %collective-permute-start.5 = (f32[32,512]{1,0:T(8,128)S(1)}, f32[32,512]{1,0:T(8,128)S(1)}, u32[]{:S(2)}, u32[]{:S(2)}) collective-permute-start(f32[32,512]{1,0:T(8,128)S(1)} %add_add_fusion.1), channel_id=1, source_target_pairs={{0,16},{1,17},{2,18},{3,19},{4,20},{5,21},{6,22},{7,23},{8,24},{9,... | collective-permute-start | bytes 196616 | tf_op jit(solution)/shard_map/ppermute | solution.py:343
  35.7 2.1 %collective-permute-start.4 = (f32[32,512]{1,0:T(8,128)S(1)}, f32[32,512]{1,0:T(8,128)S(1)}, u32[]{:S(2)}, u32[]{:S(2)}) collective-permute-start(f32[32,512]{1,0:T(8,128)S(1)} %add_add_fusion.1), channel_id=1, source_target_pairs={{0,8},{1,9},{2,10},{3,11},{4,12},{5,13},{6,14},{7,15},{8,0},{9,1},... | collective-permute-start | bytes 196616 | tf_op jit(solution)/shard_map/ppermute | solution.py:343
  37.8 1.8 %collective-permute-done.6 = f32[32,512]{1,0:T(8,128)S(1)} collective-permute-done((f32[32,512]{1,0:T(8,128)S(1)}, f32[32,512]{1,0:T(8,128)S(1)}, u32[]{:S(2)}, u32[]{:S(2)}) %collective-permute-start.6) | collective-permute-done | bytes 65568 | tf_op jit(solution)/shard_map/ppermute | solution.py:343
  39.6 1.6 %collective-permute-done.5 = f32[32,512]{1,0:T(8,128)S(1)} collective-permute-done((f32[32,512]{1,0:T(8,128)S(1)}, f32[32,512]{1,0:T(8,128)S(1)}, u32[]{:S(2)}, u32[]{:S(2)}) %collective-permute-start.5) | collective-permute-done | bytes 65568 | tf_op jit(solution)/shard_map/ppermute | solution.py:343
  41.2 0.0 collective-permute-done.4
  41.2 0.1 collective-permute-start.7
  41.3 1.2 %collective-permute-done.7 = f32[32,512]{1,0:T(8,128)S(1)} collective-permute-done((f32[32,512]{1,0:T(8,128)S(1)}, f32[32,512]{1,0:T(8,128)S(1)}, u32[]{:S(2)}, u32[]{:S(2)}) %collective-permute-start.7) | collective-permute-done | bytes 65568 | tf_op jit(solution)/shard_map/ppermute | solution.py:343
  42.6 0.0 copy-done
  42.6 2.0 %convolution_subtract_fusion = f32[64,1920]{1,0:T(8,128)S(1)} fusion(f32[1920,512]{1,0:T(8,128)S(1)} %copy-done, f32[8,8,1920]{2,0,1:T(8,128)S(1)} %all-to-all-done, f32[32,512]{1,0:T(8,128)S(1)} %get-tuple-element.12, f32[32,512]{1,0:T(8,128)S(1)} %get-tuple-element.11), kind=kOutput, calls=%fused_computation | convolution fusion | flops 377643008 | bytes 5046272 | tf_op jit(solution)/shard_map/dot_general | solution.py:333
  44.6 0.4 convolution_multiply_fusion.1
  45.0 0.2 collective-permute-start.8
  45.2 0.0 copy-done.1
  45.2 1.0 %collective-permute-done.8 = f32[64,64]{1,0:T(8,128)S(1)} collective-permute-done((f32[64,64]{1,0:T(8,128)S(1)}, f32[64,64]{1,0:T(8,128)S(1)}, u32[]{:S(2)}, u32[]{:S(2)}) %collective-permute-start.8) | collective-permute-done | bytes 16416 | tf_op jit(solution)/shard_map/ppermute | solution.py:343
  46.3 1.7 %collective-permute-start.11 = (f32[64,64]{1,0:T(8,128)S(1)}, f32[64,64]{1,0:T(8,128)S(1)}, u32[]{:S(2)}, u32[]{:S(2)}) collective-permute-start(f32[64,64]{1,0:T(8,128)S(1)} %add.54), channel_id=1, source_target_pairs={{0,6},{1,7},{2,4},{3,5},{4,2},{5,3},{6,0},{7,1},{8,14},{9,15},{10,... | collective-permute-start | bytes 49160 | tf_op jit(solution)/shard_map/ppermute | solution.py:343
  47.9 1.3 %collective-permute-start.10 = (f32[64,64]{1,0:T(8,128)S(1)}, f32[64,64]{1,0:T(8,128)S(1)}, u32[]{:S(2)}, u32[]{:S(2)}) collective-permute-start(f32[64,64]{1,0:T(8,128)S(1)} %add.54), channel_id=1, source_target_pairs={{0,4},{1,5},{2,6},{3,7},{4,0},{5,1},{6,2},{7,3},{8,12},{9,13},{10,... | collective-permute-start | bytes 49160 | tf_op jit(solution)/shard_map/ppermute | solution.py:343
  49.2 0.5 collective-permute-start.9
  49.8 1.3 %collective-permute-done.11 = f32[64,64]{1,0:T(8,128)S(1)} collective-permute-done((f32[64,64]{1,0:T(8,128)S(1)}, f32[64,64]{1,0:T(8,128)S(1)}, u32[]{:S(2)}, u32[]{:S(2)}) %collective-permute-start.11) | collective-permute-done | bytes 16416 | tf_op jit(solution)/shard_map/ppermute | solution.py:343
  51.1 0.7 collective-permute-done.10
  51.9 1.3 %collective-permute-done.9 = f32[64,64]{1,0:T(8,128)S(1)} collective-permute-done((f32[64,64]{1,0:T(8,128)S(1)}, f32[64,64]{1,0:T(8,128)S(1)}, u32[]{:S(2)}, u32[]{:S(2)}) %collective-permute-start.9) | collective-permute-done | bytes 16416 | tf_op jit(solution)/shard_map/ppermute | solution.py:343
  53.1 1.2 %collective-permute-start.14 = (f32[64,64]{1,0:T(8,128)S(1)}, f32[64,64]{1,0:T(8,128)S(1)}, u32[]{:S(2)}, u32[]{:S(2)}) collective-permute-start(f32[64,64]{1,0:T(8,128)S(1)} %add_add_fusion.3), channel_id=1, source_target_pairs={{0,24},{1,25},{2,26},{3,27},{4,28},{5,29},{6,30},{7,31},{8,16},{9,... | collective-permute-start | bytes 49160 | tf_op jit(solution)/shard_map/ppermute | solution.py:343
  54.4 0.4 collective-permute-start.13
  54.8 2.8 %collective-permute-start.12 = (f32[64,64]{1,0:T(8,128)S(1)}, f32[64,64]{1,0:T(8,128)S(1)}, u32[]{:S(2)}, u32[]{:S(2)}) collective-permute-start(f32[64,64]{1,0:T(8,128)S(1)} %add_add_fusion.3), channel_id=1, source_target_pairs={{0,8},{1,9},{2,10},{3,11},{4,12},{5,13},{6,14},{7,15},{8,0},{9,1},... | collective-permute-start | bytes 49160 | tf_op jit(solution)/shard_map/ppermute | solution.py:343
  57.6 2.1 %shard_map.37 = (f32[512,512]{1,0:T(8,128)S(1)}, f32[512,512]{1,0:T(8,128)S(1)}) custom-call(f32[64,512]{1,0:T(8,128)S(1)} %pad_maximum_fusion.coeffs_ref, f32[1,512]{1,0:T(1,128)S(1)} %bitcast.13), custom_call_target="tpu_custom_call" | custom-call | flops 1610612736 | bytes 2097152 | tf_op jit(solution)/shard_map/pallas_call | solution.py:193
  59.7 0.0 collective-permute-done.14
  59.8 0.0 collective-permute-done.13
  59.8 0.0 collective-permute-done.12
  59.8 32.7 %shard_map.38 = bf16[1920,512]{1,0:T(8,128)(2,1)} custom-call(f32[64,512]{1,0:T(8,128)S(1)} %pad_maximum_fusion.coeffs_ref, f32[64,64]{1,0:T(8,128)S(1)} %add_add_fusion.2.gram_ref, f32[1,512]{1,0:T(1,128)S(1)} %bitcast.14, f32[512,512]{1,0:T(8,128)S(1)} %get-tuple-element.9.upper, f32[512,512]{1,0:T(8,128)S(1)} %get-tuple-element.10.square_ref, ...), custom_call_target="tpu_custom_call" | custom-call | tf_op jit(solution)/shard_map/pallas_call | solution.py:315
  (10 shorter events, 0.1 us)
Async XLA Ops:
  0.0 21.1 %all-to-all-start = ((f32[8,8,1920]{2,0,1:T(8,128)}), f32[8,8,1920]{2,0,1:T(8,128)S(1)}, u32[]{:S(2)}, u32[]{:S(2)}) async-start(f32[8,8,1920]{2,0,1:T(8,128)} %bitcast.15), calls=%async_computation | async-start | bytes 983040 | tf_op jit(solution)/shard_map/all_to_all | solution.py:381
  21.1 21.5 %copy-start = (f32[1920,512]{1,0:T(8,128)S(1)}, f32[1920,512]{1,0:T(8,128)}, u32[]{:S(2)}) copy-start(f32[1920,512]{1,0:T(8,128)} %basis_hbm.1) | copy-start | bytes 11796484
  24.7 20.5 %copy-start.1 = (f32[512]{0:T(512)S(1)}, f32[512]{0:T(512)}, u32[]{:S(2)}) copy-start(f32[512]{0:T(512)} %param.5) | copy-start | bytes 6148
  24.7 1.3 %collective-permute-start = (f32[32,512]{1,0:T(8,128)S(1)}, f32[32,512]{1,0:T(8,128)S(1)}, u32[]{:S(2)}, u32[]{:S(2)}) collective-permute-start(f32[32,512]{1,0:T(8,128)S(1)} %slice_select_fusion), channel_id=1, source_target_pairs={{0,1},{1,0},{2,3},{3,2},{4,5},{5,4},{6,7},{7,6},{8,9},{9,8},{10,11... | collective-permute-start | bytes 196616 | tf_op jit(solution)/shard_map/ppermute | solution.py:343
  26.1 5.3 %collective-permute-start.3 = (f32[32,512]{1,0:T(8,128)S(1)}, f32[32,512]{1,0:T(8,128)S(1)}, u32[]{:S(2)}, u32[]{:S(2)}) collective-permute-start(f32[32,512]{1,0:T(8,128)S(1)} %select_add_fusion), channel_id=1, source_target_pairs={{0,6},{1,7},{2,4},{3,5},{4,2},{5,3},{6,0},{7,1},{8,14},{9,15},{10,... | collective-permute-start | bytes 196616 | tf_op jit(solution)/shard_map/ppermute | solution.py:343
  28.5 4.3 %collective-permute-start.2 = (f32[32,512]{1,0:T(8,128)S(1)}, f32[32,512]{1,0:T(8,128)S(1)}, u32[]{:S(2)}, u32[]{:S(2)}) collective-permute-start(f32[32,512]{1,0:T(8,128)S(1)} %select_add_fusion), channel_id=1, source_target_pairs={{0,4},{1,5},{2,6},{3,7},{4,0},{5,1},{6,2},{7,3},{8,12},{9,13},{10,... | collective-permute-start | bytes 196616 | tf_op jit(solution)/shard_map/ppermute | solution.py:343
  29.1 4.3 %collective-permute-start.1 = (f32[32,512]{1,0:T(8,128)S(1)}, f32[32,512]{1,0:T(8,128)S(1)}, u32[]{:S(2)}, u32[]{:S(2)}) collective-permute-start(f32[32,512]{1,0:T(8,128)S(1)} %select_add_fusion), channel_id=1, source_target_pairs={{0,2},{1,3},{2,0},{3,1},{4,6},{5,7},{6,4},{7,5},{8,10},{9,11},{10,... | collective-permute-start | bytes 196616 | tf_op jit(solution)/shard_map/ppermute | solution.py:343
  33.4 6.2 %collective-permute-start.6 = (f32[32,512]{1,0:T(8,128)S(1)}, f32[32,512]{1,0:T(8,128)S(1)}, u32[]{:S(2)}, u32[]{:S(2)}) collective-permute-start(f32[32,512]{1,0:T(8,128)S(1)} %add_add_fusion.1), channel_id=1, source_target_pairs={{0,24},{1,25},{2,26},{3,27},{4,28},{5,29},{6,30},{7,31},{8,16},{9,... | collective-permute-start | bytes 196616 | tf_op jit(solution)/shard_map/ppermute | solution.py:343
  34.6 6.6 %collective-permute-start.5 = (f32[32,512]{1,0:T(8,128)S(1)}, f32[32,512]{1,0:T(8,128)S(1)}, u32[]{:S(2)}, u32[]{:S(2)}) collective-permute-start(f32[32,512]{1,0:T(8,128)S(1)} %add_add_fusion.1), channel_id=1, source_target_pairs={{0,16},{1,17},{2,18},{3,19},{4,20},{5,21},{6,22},{7,23},{8,24},{9,... | collective-permute-start | bytes 196616 | tf_op jit(solution)/shard_map/ppermute | solution.py:343
  35.7 5.5 %collective-permute-start.4 = (f32[32,512]{1,0:T(8,128)S(1)}, f32[32,512]{1,0:T(8,128)S(1)}, u32[]{:S(2)}, u32[]{:S(2)}) collective-permute-start(f32[32,512]{1,0:T(8,128)S(1)} %add_add_fusion.1), channel_id=1, source_target_pairs={{0,8},{1,9},{2,10},{3,11},{4,12},{5,13},{6,14},{7,15},{8,0},{9,1},... | collective-permute-start | bytes 196616 | tf_op jit(solution)/shard_map/ppermute | solution.py:343
  41.2 1.3 %collective-permute-start.7 = (f32[32,512]{1,0:T(8,128)S(1)}, f32[32,512]{1,0:T(8,128)S(1)}, u32[]{:S(2)}, u32[]{:S(2)}) collective-permute-start(f32[32,512]{1,0:T(8,128)S(1)} %add_add_fusion), channel_id=1, source_target_pairs={{0,1},{1,0},{2,3},{3,2},{4,5},{5,4},{6,7},{7,6},{8,9},{9,8},{10,11... | collective-permute-start | bytes 196616 | tf_op jit(solution)/shard_map/ppermute | solution.py:343
  45.0 1.3 %collective-permute-start.8 = (f32[64,64]{1,0:T(8,128)S(1)}, f32[64,64]{1,0:T(8,128)S(1)}, u32[]{:S(2)}, u32[]{:S(2)}) collective-permute-start(f32[64,64]{1,0:T(8,128)S(1)} %convolution_multiply_fusion.1), channel_id=1, source_target_pairs={{0,1},{1,0},{2,3},{3,2},{4,5},{5,4},{6,7},{7,6},{8,9},{9,8},{10,11... | collective-permute-start | bytes 49160 | tf_op jit(solution)/shard_map/ppermute | solution.py:343
  46.3 4.9 %collective-permute-start.11 = (f32[64,64]{1,0:T(8,128)S(1)}, f32[64,64]{1,0:T(8,128)S(1)}, u32[]{:S(2)}, u32[]{:S(2)}) collective-permute-start(f32[64,64]{1,0:T(8,128)S(1)} %add.54), channel_id=1, source_target_pairs={{0,6},{1,7},{2,4},{3,5},{4,2},{5,3},{6,0},{7,1},{8,14},{9,15},{10,... | collective-permute-start | bytes 49160 | tf_op jit(solution)/shard_map/ppermute | solution.py:343
  47.9 3.9 %collective-permute-start.10 = (f32[64,64]{1,0:T(8,128)S(1)}, f32[64,64]{1,0:T(8,128)S(1)}, u32[]{:S(2)}, u32[]{:S(2)}) collective-permute-start(f32[64,64]{1,0:T(8,128)S(1)} %add.54), channel_id=1, source_target_pairs={{0,4},{1,5},{2,6},{3,7},{4,0},{5,1},{6,2},{7,3},{8,12},{9,13},{10,... | collective-permute-start | bytes 49160 | tf_op jit(solution)/shard_map/ppermute | solution.py:343
  49.2 3.9 %collective-permute-start.9 = (f32[64,64]{1,0:T(8,128)S(1)}, f32[64,64]{1,0:T(8,128)S(1)}, u32[]{:S(2)}, u32[]{:S(2)}) collective-permute-start(f32[64,64]{1,0:T(8,128)S(1)} %add.54), channel_id=1, source_target_pairs={{0,2},{1,3},{2,0},{3,1},{4,6},{5,7},{6,4},{7,5},{8,10},{9,11},{10,... | collective-permute-start | bytes 49160 | tf_op jit(solution)/shard_map/ppermute | solution.py:343
  53.1 6.6 %collective-permute-start.14 = (f32[64,64]{1,0:T(8,128)S(1)}, f32[64,64]{1,0:T(8,128)S(1)}, u32[]{:S(2)}, u32[]{:S(2)}) collective-permute-start(f32[64,64]{1,0:T(8,128)S(1)} %add_add_fusion.3), channel_id=1, source_target_pairs={{0,24},{1,25},{2,26},{3,27},{4,28},{5,29},{6,30},{7,31},{8,16},{9,... | collective-permute-start | bytes 49160 | tf_op jit(solution)/shard_map/ppermute | solution.py:343
  54.4 5.4 %collective-permute-start.13 = (f32[64,64]{1,0:T(8,128)S(1)}, f32[64,64]{1,0:T(8,128)S(1)}, u32[]{:S(2)}, u32[]{:S(2)}) collective-permute-start(f32[64,64]{1,0:T(8,128)S(1)} %add_add_fusion.3), channel_id=1, source_target_pairs={{0,16},{1,17},{2,18},{3,19},{4,20},{5,21},{6,22},{7,23},{8,24},{9,... | collective-permute-start | bytes 49160 | tf_op jit(solution)/shard_map/ppermute | solution.py:343
  54.8 5.0 %collective-permute-start.12 = (f32[64,64]{1,0:T(8,128)S(1)}, f32[64,64]{1,0:T(8,128)S(1)}, u32[]{:S(2)}, u32[]{:S(2)}) collective-permute-start(f32[64,64]{1,0:T(8,128)S(1)} %add_add_fusion.3), channel_id=1, source_target_pairs={{0,8},{1,9},{2,10},{3,11},{4,12},{5,13},{6,14},{7,15},{8,0},{9,1},... | collective-permute-start | bytes 49160 | tf_op jit(solution)/shard_map/ppermute | solution.py:343

commit v4 on v3

--- a/solution.py
+++ b/solution.py
@@ -9,6 +9,7 @@
 
 HIGHEST = lax.Precision.HIGHEST
 BLOCK = 128
+LANES = 128
 VMEM = 28 * 1024 * 1024
 
 
@@ -199,6 +200,103 @@
     )(coeffs, squares)
 
 
+def pieces_kernel(basis_hbm, top, low, held, loaded):
+    chunk = held.shape[1]
+    count = basis_hbm.shape[0] // chunk
+    copies = [
+        pltpu.make_async_copy(
+            basis_hbm.at[pl.ds(index * chunk, chunk), :], held.at[index % 2], loaded.at[index % 2]
+        )
+        for index in range(count)
+    ]
+    copies[0].start()
+    for index in range(count):
+        if index + 1 < count:
+            copies[index + 1].start()
+        copies[index].wait()
+        here = pl.ds(index * chunk, chunk)
+        top[here, :], low[here, :] = split(held[index % 2], 2)
+
+
+def basis_pieces(old_basis):
+    rows, modes = old_basis.shape
+    chunk = chunk_of(rows)
+    spec = pl.BlockSpec(memory_space=pltpu.VMEM)
+    shape = jax.ShapeDtypeStruct((rows, modes), jnp.bfloat16)
+    return pl.pallas_call(
+        pieces_kernel, out_shape=(shape, shape),
+        in_specs=[pl.BlockSpec(memory_space=pl.ANY)], out_specs=(spec, spec),
+        scratch_shapes=[
+            pltpu.VMEM((2, chunk, modes), jnp.float32), pltpu.SemaphoreType.DMA((2,))
+        ],
+        compiler_params=pltpu.CompilerParams(vmem_limit_bytes=VMEM),
+        cost_estimate=pl.CostEstimate(
+            flops=1000 * rows * modes, bytes_accessed=8 * rows * modes, transcendentals=0
+        ),
+    )(old_basis)
+
+
+def deal_kernel(name, snaps_hbm, *refs):
+    blocks, done = refs[:-1], refs[-1]
+    cells = blocks[0].shape[1]
+    index = lax.axis_index(name)
+    copies = []
+    for mask, block in enumerate(blocks):
+        start = pl.multiple_of(jnp.bitwise_xor(index, mask) * cells, LANES)
+        copies.append(
+            pltpu.make_async_copy(snaps_hbm.at[:, pl.ds(start, cells)], block, done.at[mask])
+        )
+        copies[-1].start()
+    for copy in copies:
+        copy.wait()
+
+
+def deal(snapshots, name):
+    count = lax.axis_size(name)
+    rows, cells = snapshots.shape[0], snapshots.shape[1] // count
+    spec = pl.BlockSpec(memory_space=pltpu.VMEM)
+    return pl.pallas_call(
+        functools.partial(deal_kernel, name),
+        out_shape=[jax.ShapeDtypeStruct((rows, cells), jnp.float32)] * count,
+        in_specs=[pl.BlockSpec(memory_space=pl.ANY)], out_specs=[spec] * count,
+        scratch_shapes=[pltpu.SemaphoreType.DMA((count,))],
+        compiler_params=pltpu.CompilerParams(vmem_limit_bytes=VMEM),
+    )(snapshots)
+
+
+def coeffs_kernel(name, weight, count, *refs):
+    top_ref, low_ref, out_ref, snaps_ref = refs[count:]
+    if count == 1:
+        snaps_ref[...] = refs[0][...]
+    else:
+        rows = refs[0].shape[0]
+        index = lax.axis_index(name)
+        for mask in range(count):
+            start = pl.multiple_of(jnp.bitwise_xor(index, mask) * rows, rows)
+            snaps_ref[pl.ds(start, rows), :] = refs[mask][...]
+    snaps = snaps_ref.shape[0]
+    top, low = split(snaps_ref[...], 2)
+    value = dot(jnp.concatenate([top, low], axis=0), top_ref[...], precision=None)
+    value = value[:snaps] + (value[snaps:] + dot(top, low_ref[...], precision=None))
+    out_ref[...] = value * weight
+
+
+def local_coeffs(blocks, basis_top, basis_low, weight):
+    count = len(blocks)
+    rows, modes = basis_top.shape
+    snaps = count * blocks[0].shape[0]
+    spec = pl.BlockSpec(memory_space=pltpu.VMEM)
+    return pl.pallas_call(
+        functools.partial(coeffs_kernel, AXES[0], weight, count),
+        out_shape=(
+            jax.ShapeDtypeStruct((snaps, modes), jnp.float32),
+            jax.ShapeDtypeStruct((snaps, rows), jnp.float32),
+        ),
+        in_specs=[spec] * (count + 2), out_specs=(spec, spec),
+        compiler_params=pltpu.CompilerParams(vmem_limit_bytes=VMEM),
+    )(*blocks, basis_top, basis_low)
+
+
 def rotation(coeffs_ref, gram_ref, upper, square_ref, inverse, second, work):
     coeffs = coeffs_ref[...]
     mid = coeffs.shape[1] // 2
@@ -267,28 +365,24 @@
 
 
 def update_kernel(
-    coeffs_ref, gram_ref, squares_ref, upper, square_ref, snaps_ref, basis_hbm, out_hbm,
-    inverse, second, work, basis, out, loaded, stored,
+    coeffs_ref, gram_ref, squares_ref, upper, square_ref, snaps_ref, top_ref, low_ref, out_hbm,
+    inverse, second, work, out, stored,
 ):
-    rows, modes = basis.shape
-    snaps = coeffs_ref.shape[0]
+    rows, modes = top_ref.shape
     mid = modes // 2
-    load = pltpu.make_async_copy(basis_hbm, basis, loaded)
-    load.start()
     rotation(coeffs_ref, gram_ref, upper, square_ref, inverse, second, work)
     final = inverse[...]
     turn_top, turn_low = split(final * squares_ref[...], 2)
     across_top, across_low = split(dot(final, coeffs_ref[...], NT).T, 2)
     across = jnp.concatenate([across_top, across_low, across_top], axis=0)
     chunk = chunk_of(rows)
-    load.wait()
     copies = []
     for start in range(0, rows, chunk):
         here = pl.ds(start, chunk)
         snaps_top, snaps_low = split(snaps_ref[:, pl.ds(start, chunk)], 2)
         mixed = jnp.concatenate([snaps_top, snaps_top, snaps_low], axis=0).astype(jnp.float32)
         base = dot(mixed.T.astype(jnp.bfloat16), across, precision=None)
-        top, low = split(basis[here, :], 2)
+        top, low = top_ref[here, :], low_ref[here, :]
         for cols, depth in ((slice(0, mid), mid), (slice(mid, modes), modes)):
             value = base[:, cols]
             for a, b in ((low, turn_top), (top, turn_low), (top, turn_top)):
@@ -307,23 +401,22 @@
     return rows
 
 
-def updated_basis(coeffs, gram_res, squares, upper, square, snap_rows, old_basis):
-    rows, modes = old_basis.shape
+def updated_basis(coeffs, gram_res, squares, upper, square, snap_rows, basis_top, basis_low):
+    rows, modes = basis_top.shape
     whole = pltpu.VMEM((modes, modes), jnp.float32)
     spec = pl.BlockSpec(memory_space=pltpu.VMEM)
     far = pl.BlockSpec(memory_space=pl.ANY)
     return pl.pallas_call(
         update_kernel,
         out_shape=jax.ShapeDtypeStruct((rows, modes), jnp.bfloat16),
-        in_specs=[spec] * 6 + [far],
+        in_specs=[spec] * 8,
         out_specs=far,
         scratch_shapes=[
             whole, whole, pltpu.VMEM((BLOCK, BLOCK), jnp.float32),
-            pltpu.VMEM((rows, modes), jnp.float32), pltpu.VMEM((rows, modes), jnp.bfloat16),
-            pltpu.SemaphoreType.DMA, pltpu.SemaphoreType.DMA((rows // chunk_of(rows),)),
+            pltpu.VMEM((rows, modes), jnp.bfloat16), pltpu.SemaphoreType.DMA((rows // chunk_of(rows),)),
         ],
         compiler_params=pltpu.CompilerParams(vmem_limit_bytes=VMEM),
-    )(coeffs, gram_res, squares, upper, square, snap_rows, old_basis)
+    )(coeffs, gram_res, squares, upper, square, snap_rows, basis_top, basis_low)
 
 
 HIGH = lax.Precision.HIGH
@@ -377,17 +470,33 @@
     return jnp.concatenate([jnp.where(first, kept, other), jnp.where(first, other, kept)], axis=0)
 
 
+def exchange_rows(snapshots):
+    name = AXES[0]
+    count = lax.axis_size(name)
+    if count > 8 or count & (count - 1) or snapshots.shape[0] % 8:
+        return [lax.all_to_all(snapshots, name, split_axis=1, concat_axis=0, tiled=True)]
+    blocks = deal(snapshots, name)
+    return [
+        lax.ppermute(block, name, [(i, i ^ mask) for i in range(count)]) if mask else block
+        for mask, block in enumerate(blocks)
+    ]
+
+
 def local(snapshots, old_basis, sing_values):
-    snap_rows = lax.all_to_all(snapshots, "tile", split_axis=1, concat_axis=0, tiled=True)
+    basis_top, basis_low = basis_pieces(old_basis)
+    blocks = exchange_rows(snapshots)
     cell_count = old_basis.shape[0] * lax.axis_size("tile") * lax.axis_size("slab")
     weight_cell = 1.0 / cell_count
-    coeffs = sum_all_halved(mat(snap_rows, old_basis, ((1,), (0,))) * weight_cell)
+    part, snap_rows = local_coeffs(blocks, basis_top, basis_low, weight_cell)
+    coeffs = sum_all_halved(part)
     resid = snap_rows - mat(coeffs, old_basis, ((1,), (1,)))
     gram_part = mat(resid, resid, ((1,), (1,))) * weight_cell
     squares = (sing_values * sing_values)[None, :]
     gram_res = sum_all(gram_part)
     upper, square = opening(lax.optimization_barrier((coeffs, gram_part))[0], squares)
-    return updated_basis(coeffs, gram_res, squares, upper, square, snap_rows, old_basis)
+    return updated_basis(
+        coeffs, gram_res, squares, upper, square, snap_rows, basis_top, basis_low
+    )
 
 
 def solution(mesh):

time: 92.9 us -> 88.7 us (0.955)
  waiting for transfers between devices: 27.8 us -> 17.8 us
  starting transfers between devices: 23.6 us -> 28.8 us
  matrix products: 5.98 us -> 2.3 us
  local copies, waits for them, and re-layouts: 0.01 us -> 3.15 us
  Pallas kernels: 34.9 us -> 36 us
    all_to_all x1 -> x0, waiting for transfers between devices: 13.8 us -> none  [local(): lax.all_to_all(snapshots, 'tile', split_axis=1, concat_axis=0, tiled=True)]
    ppermute x0 -> x7, starting transfers between devices: none -> 12.5 us  [exchange_rows(): lax.ppermute(block, name, [(i, i ^ mask) for i in range(count)])]
    all_to_all x1 -> x0, starting transfers between devices: 7.31 us -> none  [local(): lax.all_to_all(snapshots, 'tile', split_axis=1, concat_axis=0, tiled=True)]
    ppermute x0 -> x7, waiting for transfers between devices: none -> 4.06 us  [exchange_rows(): lax.ppermute(block, name, [(i, i ^ mask) for i in range(count)])]
    dot_general x3 -> x2, matrix products: 5.98 us -> 2.3 us  [mat(): lax.dot_general(left, right, (contract, ((), ())), precision=precision, p...]
    unnamed x4 -> x8, local copies, waits for them, and re-layouts: 0.01 us -> 3.15 us
    pallas_call x0 -> x3, Pallas kernels: none -> 2.27 us  [the longest x1 0.81 us: basis_pieces(): pl.pallas_call(pieces_kernel, out_shape=(shape, shape), in_specs=[pl.Bloc...]
    pallas_call x1, Pallas kernels: 32.7 us -> 31.5 us  [updated_basis(): pl.pallas_call(update_kernel, out_shape=jax.ShapeDtypeStruct((rows, modes...]
  transfers between devices with their start and end apart: 16 -> 22, of which waited for: 12 -> 14; matrix products, arithmetic and copies ran while one was open for 0% -> 0% of each run, Pallas kernels for 2% -> 3%
where the time goes in v4:
time: 88.7 us; the launch traced here: 88.5 us
  Pallas kernels  36 us (41%)
  starting transfers between devices  28.8 us (32%)
  waiting for transfers between devices  17.8 us (20%)
  local copies, waits for them, and re-layouts  3.15 us (4%)
  matrix products  2.3 us (3%)
    pallas_call x1, Pallas kernels, updated_basis(): pl.pallas_call(update_kernel, out_shape=jax.ShapeDtypeStruct((rows, modes...  31.5 us
    ppermute x15, starting transfers between devices, exchange(): return lax.ppermute(part, AXES, [(i, i ^ mask) for i in range(count)])  16.3 us
    ppermute x15, waiting for transfers between devices, exchange(): return lax.ppermute(part, AXES, [(i, i ^ mask) for i in range(count)])  13.7 us
    ppermute x7, starting transfers between devices, exchange_rows(): lax.ppermute(block, name, [(i, i ^ mask) for i in range(count)])  12.5 us
    ppermute x7, waiting for transfers between devices, exchange_rows(): lax.ppermute(block, name, [(i, i ^ mask) for i in range(count)])  4.06 us
    unnamed x8, local copies, waits for them, and re-layouts  3.15 us
    dot_general x2, matrix products, mat(): lax.dot_general(left, right, (contract, ((), ())), precision=precision, p...  2.3 us
    pallas_call x1, Pallas kernels, opening(): pl.pallas_call(opening_kernel, out_shape=(shape, shape), in_specs=[spec]...  2.19 us
  transfers between devices with their start and end apart: 22, of which 14 were waited for; matrix products, arithmetic and copies ran while one was open for 0% of the time, Pallas kernels for 3%

profile of v4, /device:TPU:0, one launch (start us, length us, event | category | flops | bytes accessed | tf_op | source)
XLA Modules:
  0.0 88.5 jit_solution(938233302939218823)
XLA Ops:
  0.0 0.0 copy-start.2
  0.0 1.0 %copy-done.2 = f32[8,15360]{1,0:T(8,128)S(1)} copy-done((f32[8,15360]{1,0:T(8,128)S(1)}, f32[8,15360]{1,0:T(8,128)}, u32[]{:S(2)}) %copy-start.2) | copy-done | bytes 491544
  1.0 0.7 shard_map.37
  1.7 3.1 %collective-permute-start = (f32[8,1920]{1,0:T(8,128)S(1)}, f32[8,1920]{1,0:T(8,128)S(1)}, u32[]{:S(2)}, u32[]{:S(2)}) collective-permute-start(f32[8,1920]{1,0:T(8,128)S(1)} %get-tuple-element.21), channel_id=1, source_target_pairs={{0,4},{4,0},{8,12},{12,8},{16,20},{20,16},{24,28},{28,24},{1,5},{5... | collective-permute-start | bytes 184328 | tf_op jit(solution)/shard_map/ppermute | solution.py:480
  4.8 1.6 %collective-permute-start.1 = (f32[8,1920]{1,0:T(8,128)S(1)}, f32[8,1920]{1,0:T(8,128)S(1)}, u32[]{:S(2)}, u32[]{:S(2)}) collective-permute-start(f32[8,1920]{1,0:T(8,128)S(1)} %get-tuple-element.22), channel_id=1, source_target_pairs={{0,8},{4,12},{8,0},{12,4},{16,24},{20,28},{24,16},{28,20},{1,9},{5... | collective-permute-start | bytes 184328 | tf_op jit(solution)/shard_map/ppermute | solution.py:480
  6.4 0.0 collective-permute-start.2
  6.4 3.0 %collective-permute-start.3 = (f32[8,1920]{1,0:T(8,128)S(1)}, f32[8,1920]{1,0:T(8,128)S(1)}, u32[]{:S(2)}, u32[]{:S(2)}) collective-permute-start(f32[8,1920]{1,0:T(8,128)S(1)} %get-tuple-element.24), channel_id=1, source_target_pairs={{0,16},{4,20},{8,24},{12,28},{16,0},{20,4},{24,8},{28,12},{1,17},{... | collective-permute-start | bytes 184328 | tf_op jit(solution)/shard_map/ppermute | solution.py:480
  9.4 1.3 %collective-permute-start.4 = (f32[8,1920]{1,0:T(8,128)S(1)}, f32[8,1920]{1,0:T(8,128)S(1)}, u32[]{:S(2)}, u32[]{:S(2)}) collective-permute-start(f32[8,1920]{1,0:T(8,128)S(1)} %get-tuple-element.25), channel_id=1, source_target_pairs={{0,20},{4,16},{8,28},{12,24},{16,4},{20,0},{24,12},{28,8},{1,21},{... | collective-permute-start | bytes 184328 | tf_op jit(solution)/shard_map/ppermute | solution.py:480
  10.6 0.0 collective-permute-done.refs_1_
  10.7 3.6 %collective-permute-start.5 = (f32[8,1920]{1,0:T(8,128)S(1)}, f32[8,1920]{1,0:T(8,128)S(1)}, u32[]{:S(2)}, u32[]{:S(2)}) collective-permute-start(f32[8,1920]{1,0:T(8,128)S(1)} %get-tuple-element.26), channel_id=1, source_target_pairs={{0,24},{4,28},{8,16},{12,20},{16,8},{20,12},{24,0},{28,4},{1,25},{... | collective-permute-start | bytes 184328 | tf_op jit(solution)/shard_map/ppermute | solution.py:480
  14.3 0.0 collective-permute-done.1.refs_2_
  14.3 0.0 collective-permute-start.6
  14.3 0.0 copy-start
  14.3 2.1 %copy-done = f32[1920,512]{1,0:T(8,128)S(1)} copy-done((f32[1920,512]{1,0:T(8,128)S(1)}, f32[1920,512]{1,0:T(8,128)}, u32[]{:S(2)}) %copy-start) | copy-done | bytes 3932184
  16.4 0.0 copy-start.1
  16.4 0.8 shard_map.38
  17.2 0.0 collective-permute-done.2.refs_3_
  17.2 0.0 collective-permute-done.3.refs_4_
  17.2 1.8 %collective-permute-done.4.refs_5_ = f32[8,1920]{1,0:T(8,128)S(1)} collective-permute-done((f32[8,1920]{1,0:T(8,128)S(1)}, f32[8,1920]{1,0:T(8,128)S(1)}, u32[]{:S(2)}, u32[]{:S(2)}) %collective-permute-start.4) | collective-permute-done | bytes 61472 | tf_op jit(solution)/shard_map/ppermute | solution.py:480
  19.0 0.0 collective-permute-done.5.refs_6_
  19.0 2.2 %collective-permute-done.6.refs_7_ = f32[8,1920]{1,0:T(8,128)S(1)} collective-permute-done((f32[8,1920]{1,0:T(8,128)S(1)}, f32[8,1920]{1,0:T(8,128)S(1)}, u32[]{:S(2)}, u32[]{:S(2)}) %collective-permute-start.6) | collective-permute-done | bytes 61472 | tf_op jit(solution)/shard_map/ppermute | solution.py:480
  21.3 0.8 shard_map.39
  22.0 0.0 copy-start.3
  22.1 0.1 collective-permute-start.7
  22.2 1.2 %collective-permute-done.7 = f32[32,512]{1,0:T(8,128)S(1)} collective-permute-done((f32[32,512]{1,0:T(8,128)S(1)}, f32[32,512]{1,0:T(8,128)S(1)}, u32[]{:S(2)}, u32[]{:S(2)}) %collective-permute-start.7) | collective-permute-done | bytes 65568 | tf_op jit(solution)/shard_map/ppermute | solution.py:436
  23.4 1.5 %collective-permute-start.10 = (f32[32,512]{1,0:T(8,128)S(1)}, f32[32,512]{1,0:T(8,128)S(1)}, u32[]{:S(2)}, u32[]{:S(2)}) collective-permute-start(f32[32,512]{1,0:T(8,128)S(1)} %select_add_fusion), channel_id=1, source_target_pairs={{0,6},{1,7},{2,4},{3,5},{4,2},{5,3},{6,0},{7,1},{8,14},{9,15},{10,... | collective-permute-start | bytes 196616 | tf_op jit(solution)/shard_map/ppermute | solution.py:436
  24.9 1.5 %collective-permute-start.9 = (f32[32,512]{1,0:T(8,128)S(1)}, f32[32,512]{1,0:T(8,128)S(1)}, u32[]{:S(2)}, u32[]{:S(2)}) collective-permute-start(f32[32,512]{1,0:T(8,128)S(1)} %select_add_fusion), channel_id=1, source_target_pairs={{0,4},{1,5},{2,6},{3,7},{4,0},{5,1},{6,2},{7,3},{8,12},{9,13},{10,... | collective-permute-start | bytes 196616 | tf_op jit(solution)/shard_map/ppermute | solution.py:436
  26.4 0.5 collective-permute-start.8
  27.0 1.7 %collective-permute-done.10 = f32[32,512]{1,0:T(8,128)S(1)} collective-permute-done((f32[32,512]{1,0:T(8,128)S(1)}, f32[32,512]{1,0:T(8,128)S(1)}, u32[]{:S(2)}, u32[]{:S(2)}) %collective-permute-start.10) | collective-permute-done | bytes 65568 | tf_op jit(solution)/shard_map/ppermute | solution.py:436
  28.7 1.2 %collective-permute-done.9 = f32[32,512]{1,0:T(8,128)S(1)} collective-permute-done((f32[32,512]{1,0:T(8,128)S(1)}, f32[32,512]{1,0:T(8,128)S(1)}, u32[]{:S(2)}, u32[]{:S(2)}) %collective-permute-start.9) | collective-permute-done | bytes 65568 | tf_op jit(solution)/shard_map/ppermute | solution.py:436
  29.9 0.8 collective-permute-done.8
  30.7 1.2 %collective-permute-start.13 = (f32[32,512]{1,0:T(8,128)S(1)}, f32[32,512]{1,0:T(8,128)S(1)}, u32[]{:S(2)}, u32[]{:S(2)}) collective-permute-start(f32[32,512]{1,0:T(8,128)S(1)} %add_add_fusion.1), channel_id=1, source_target_pairs={{0,24},{1,25},{2,26},{3,27},{4,28},{5,29},{6,30},{7,31},{8,16},{9,... | collective-permute-start | bytes 196616 | tf_op jit(solution)/shard_map/ppermute | solution.py:436
  31.9 1.4 %collective-permute-start.12 = (f32[32,512]{1,0:T(8,128)S(1)}, f32[32,512]{1,0:T(8,128)S(1)}, u32[]{:S(2)}, u32[]{:S(2)}) collective-permute-start(f32[32,512]{1,0:T(8,128)S(1)} %add_add_fusion.1), channel_id=1, source_target_pairs={{0,16},{1,17},{2,18},{3,19},{4,20},{5,21},{6,22},{7,23},{8,24},{9,... | collective-permute-start | bytes 196616 | tf_op jit(solution)/shard_map/ppermute | solution.py:436
  33.2 1.9 %collective-permute-start.11 = (f32[32,512]{1,0:T(8,128)S(1)}, f32[32,512]{1,0:T(8,128)S(1)}, u32[]{:S(2)}, u32[]{:S(2)}) collective-permute-start(f32[32,512]{1,0:T(8,128)S(1)} %add_add_fusion.1), channel_id=1, source_target_pairs={{0,8},{1,9},{2,10},{3,11},{4,12},{5,13},{6,14},{7,15},{8,0},{9,1},... | collective-permute-start | bytes 196616 | tf_op jit(solution)/shard_map/ppermute | solution.py:436
  35.2 2.3 %collective-permute-done.13 = f32[32,512]{1,0:T(8,128)S(1)} collective-permute-done((f32[32,512]{1,0:T(8,128)S(1)}, f32[32,512]{1,0:T(8,128)S(1)}, u32[]{:S(2)}, u32[]{:S(2)}) %collective-permute-start.13) | collective-permute-done | bytes 65568 | tf_op jit(solution)/shard_map/ppermute | solution.py:436
  37.5 1.8 %collective-permute-done.12 = f32[32,512]{1,0:T(8,128)S(1)} collective-permute-done((f32[32,512]{1,0:T(8,128)S(1)}, f32[32,512]{1,0:T(8,128)S(1)}, u32[]{:S(2)}, u32[]{:S(2)}) %collective-permute-start.12) | collective-permute-done | bytes 65568 | tf_op jit(solution)/shard_map/ppermute | solution.py:436
  39.3 0.0 collective-permute-done.11
  39.3 0.1 collective-permute-start.14
  39.4 1.2 %collective-permute-done.14 = f32[32,512]{1,0:T(8,128)S(1)} collective-permute-done((f32[32,512]{1,0:T(8,128)S(1)}, f32[32,512]{1,0:T(8,128)S(1)}, u32[]{:S(2)}, u32[]{:S(2)}) %collective-permute-start.14) | collective-permute-done | bytes 65568 | tf_op jit(solution)/shard_map/ppermute | solution.py:436
  40.6 0.0 copy-done.1
  40.6 1.9 %convolution_subtract_fusion = f32[64,1920]{1,0:T(8,128)S(1)} fusion(f32[64,1920]{1,0:T(8,128)S(1)} %get-tuple-element.31.snaps_ref, f32[1920,512]{1,0:T(8,128)S(1)} %copy-done.1, f32[32,512]{1,0:T(8,128)S(1)} %get-tuple-element.36, f32[32,512]{1,0:T(8,128)S(1)} %get-tuple-element.35), kind=kOutput, calls=%fused_computation | convolution fusion | flops 377643008 | bytes 5046272 | tf_op jit(solution)/shard_map/dot_general | solution.py:426
  42.6 0.4 convolution_multiply_fusion
  42.9 0.2 collective-permute-start.15
  43.2 0.0 copy-done.3
  43.2 1.0 %collective-permute-done.15 = f32[64,64]{1,0:T(8,128)S(1)} collective-permute-done((f32[64,64]{1,0:T(8,128)S(1)}, f32[64,64]{1,0:T(8,128)S(1)}, u32[]{:S(2)}, u32[]{:S(2)}) %collective-permute-start.15) | collective-permute-done | bytes 16416 | tf_op jit(solution)/shard_map/ppermute | solution.py:436
  44.2 1.3 %collective-permute-start.18 = (f32[64,64]{1,0:T(8,128)S(1)}, f32[64,64]{1,0:T(8,128)S(1)}, u32[]{:S(2)}, u32[]{:S(2)}) collective-permute-start(f32[64,64]{1,0:T(8,128)S(1)} %add.54), channel_id=1, source_target_pairs={{0,6},{1,7},{2,4},{3,5},{4,2},{5,3},{6,0},{7,1},{8,14},{9,15},{10,... | collective-permute-start | bytes 49160 | tf_op jit(solution)/shard_map/ppermute | solution.py:436
  45.5 0.2 collective-permute-start.17
  45.7 2.0 %collective-permute-start.16 = (f32[64,64]{1,0:T(8,128)S(1)}, f32[64,64]{1,0:T(8,128)S(1)}, u32[]{:S(2)}, u32[]{:S(2)}) collective-permute-start(f32[64,64]{1,0:T(8,128)S(1)} %add.54), channel_id=1, source_target_pairs={{0,2},{1,3},{2,0},{3,1},{4,6},{5,7},{6,4},{7,5},{8,10},{9,11},{10,... | collective-permute-start | bytes 49160 | tf_op jit(solution)/shard_map/ppermute | solution.py:436
  47.7 1.3 %collective-permute-done.18 = f32[64,64]{1,0:T(8,128)S(1)} collective-permute-done((f32[64,64]{1,0:T(8,128)S(1)}, f32[64,64]{1,0:T(8,128)S(1)}, u32[]{:S(2)}, u32[]{:S(2)}) %collective-permute-start.18) | collective-permute-done | bytes 16416 | tf_op jit(solution)/shard_map/ppermute | solution.py:436
  49.0 0.4 collective-permute-done.17
  49.5 0.2 collective-permute-done.16
  49.6 2.3 %collective-permute-start.21 = (f32[64,64]{1,0:T(8,128)S(1)}, f32[64,64]{1,0:T(8,128)S(1)}, u32[]{:S(2)}, u32[]{:S(2)}) collective-permute-start(f32[64,64]{1,0:T(8,128)S(1)} %add_add_fusion.3), channel_id=1, source_target_pairs={{0,24},{1,25},{2,26},{3,27},{4,28},{5,29},{6,30},{7,31},{8,16},{9,... | collective-permute-start | bytes 49160 | tf_op jit(solution)/shard_map/ppermute | solution.py:436
  52.0 0.0 collective-permute-start.20
  52.0 2.1 %collective-permute-start.19 = (f32[64,64]{1,0:T(8,128)S(1)}, f32[64,64]{1,0:T(8,128)S(1)}, u32[]{:S(2)}, u32[]{:S(2)}) collective-permute-start(f32[64,64]{1,0:T(8,128)S(1)} %add_add_fusion.3), channel_id=1, source_target_pairs={{0,8},{1,9},{2,10},{3,11},{4,12},{5,13},{6,14},{7,15},{8,0},{9,1},... | collective-permute-start | bytes 49160 | tf_op jit(solution)/shard_map/ppermute | solution.py:436
  54.1 2.2 %shard_map.40 = (f32[512,512]{1,0:T(8,128)S(1)}, f32[512,512]{1,0:T(8,128)S(1)}) custom-call(f32[64,512]{1,0:T(8,128)S(1)} %pad_maximum_fusion.coeffs_ref, f32[1,512]{1,0:T(1,128)S(1)} %bitcast.4), custom_call_target="tpu_custom_call" | custom-call | flops 1610612736 | bytes 2097152 | tf_op jit(solution)/shard_map/pallas_call | solution.py:194
  56.3 0.0 collective-permute-done.21
  56.3 0.5 collective-permute-done.20
  56.8 0.0 collective-permute-done.19
  56.8 31.5 %shard_map.41 = bf16[1920,512]{1,0:T(8,128)(2,1)} custom-call(f32[64,512]{1,0:T(8,128)S(1)} %pad_maximum_fusion.coeffs_ref, f32[64,64]{1,0:T(8,128)S(1)} %add_add_fusion.2.gram_ref, f32[1,512]{1,0:T(1,128)S(1)} %bitcast.5, f32[512,512]{1,0:T(8,128)S(1)} %get-tuple-element.33.upper, f32[512,512]{1,0:T(8,128)S(1)} %get-tuple-element.34.square_ref, ...), custom_call_target="tpu_custom_call" | custom-call | tf_op jit(solution)/shard_map/pallas_call | solution.py:409
  (10 shorter events, 0.1 us)
Async XLA Ops:
  0.0 1.0 %copy-start.2 = (f32[8,15360]{1,0:T(8,128)S(1)}, f32[8,15360]{1,0:T(8,128)}, u32[]{:S(2)}) copy-start(f32[8,15360]{1,0:T(8,128)} %snaps_hbm.1) | copy-start | bytes 1474564
  1.7 8.9 %collective-permute-start = (f32[8,1920]{1,0:T(8,128)S(1)}, f32[8,1920]{1,0:T(8,128)S(1)}, u32[]{:S(2)}, u32[]{:S(2)}) collective-permute-start(f32[8,1920]{1,0:T(8,128)S(1)} %get-tuple-element.21), channel_id=1, source_target_pairs={{0,4},{4,0},{8,12},{12,8},{16,20},{20,16},{24,28},{28,24},{1,5},{5... | collective-permute-start | bytes 184328 | tf_op jit(solution)/shard_map/ppermute | solution.py:480
  4.8 9.5 %collective-permute-start.1 = (f32[8,1920]{1,0:T(8,128)S(1)}, f32[8,1920]{1,0:T(8,128)S(1)}, u32[]{:S(2)}, u32[]{:S(2)}) collective-permute-start(f32[8,1920]{1,0:T(8,128)S(1)} %get-tuple-element.22), channel_id=1, source_target_pairs={{0,8},{4,12},{8,0},{12,4},{16,24},{20,28},{24,16},{28,20},{1,9},{5... | collective-permute-start | bytes 184328 | tf_op jit(solution)/shard_map/ppermute | solution.py:480
  6.4 10.8 %collective-permute-start.2 = (f32[8,1920]{1,0:T(8,128)S(1)}, f32[8,1920]{1,0:T(8,128)S(1)}, u32[]{:S(2)}, u32[]{:S(2)}) collective-permute-start(f32[8,1920]{1,0:T(8,128)S(1)} %get-tuple-element.23), channel_id=1, source_target_pairs={{0,12},{4,8},{8,4},{12,0},{16,28},{20,24},{24,20},{28,16},{1,13},{... | collective-permute-start | bytes 184328 | tf_op jit(solution)/shard_map/ppermute | solution.py:480
  6.4 10.8 %collective-permute-start.3 = (f32[8,1920]{1,0:T(8,128)S(1)}, f32[8,1920]{1,0:T(8,128)S(1)}, u32[]{:S(2)}, u32[]{:S(2)}) collective-permute-start(f32[8,1920]{1,0:T(8,128)S(1)} %get-tuple-element.24), channel_id=1, source_target_pairs={{0,16},{4,20},{8,24},{12,28},{16,0},{20,4},{24,8},{28,12},{1,17},{... | collective-permute-start | bytes 184328 | tf_op jit(solution)/shard_map/ppermute | solution.py:480
  9.4 9.7 %collective-permute-start.4 = (f32[8,1920]{1,0:T(8,128)S(1)}, f32[8,1920]{1,0:T(8,128)S(1)}, u32[]{:S(2)}, u32[]{:S(2)}) collective-permute-start(f32[8,1920]{1,0:T(8,128)S(1)} %get-tuple-element.25), channel_id=1, source_target_pairs={{0,20},{4,16},{8,28},{12,24},{16,4},{20,0},{24,12},{28,8},{1,21},{... | collective-permute-start | bytes 184328 | tf_op jit(solution)/shard_map/ppermute | solution.py:480
  10.7 8.4 %collective-permute-start.5 = (f32[8,1920]{1,0:T(8,128)S(1)}, f32[8,1920]{1,0:T(8,128)S(1)}, u32[]{:S(2)}, u32[]{:S(2)}) collective-permute-start(f32[8,1920]{1,0:T(8,128)S(1)} %get-tuple-element.26), channel_id=1, source_target_pairs={{0,24},{4,28},{8,16},{12,20},{16,8},{20,12},{24,0},{28,4},{1,25},{... | collective-permute-start | bytes 184328 | tf_op jit(solution)/shard_map/ppermute | solution.py:480
  14.3 7.0 %collective-permute-start.6 = (f32[8,1920]{1,0:T(8,128)S(1)}, f32[8,1920]{1,0:T(8,128)S(1)}, u32[]{:S(2)}, u32[]{:S(2)}) collective-permute-start(f32[8,1920]{1,0:T(8,128)S(1)} %get-tuple-element.27), channel_id=1, source_target_pairs={{0,28},{4,24},{8,20},{12,16},{16,12},{20,8},{24,4},{28,0},{1,29},{... | collective-permute-start | bytes 184328 | tf_op jit(solution)/shard_map/ppermute | solution.py:480
  14.3 2.1 %copy-start = (f32[1920,512]{1,0:T(8,128)S(1)}, f32[1920,512]{1,0:T(8,128)}, u32[]{:S(2)}) copy-start(f32[1920,512]{1,0:T(8,128)} %basis_hbm.1) | copy-start | bytes 11796484
  16.4 24.2 %copy-start.1 = (f32[1920,512]{1,0:T(8,128)S(1)}, f32[1920,512]{1,0:T(8,128)}, u32[]{:S(2)}) copy-start(f32[1920,512]{1,0:T(8,128)} %basis_hbm.1) | copy-start | bytes 11796484
  22.0 21.1 %copy-start.3 = (f32[512]{0:T(512)S(1)}, f32[512]{0:T(512)}, u32[]{:S(2)}) copy-start(f32[512]{0:T(512)} %param.5) | copy-start | bytes 6148
  22.1 1.3 %collective-permute-start.7 = (f32[32,512]{1,0:T(8,128)S(1)}, f32[32,512]{1,0:T(8,128)S(1)}, u32[]{:S(2)}, u32[]{:S(2)}) collective-permute-start(f32[32,512]{1,0:T(8,128)S(1)} %slice_select_fusion), channel_id=1, source_target_pairs={{0,1},{1,0},{2,3},{3,2},{4,5},{5,4},{6,7},{7,6},{8,9},{9,8},{10,11... | collective-permute-start | bytes 196616 | tf_op jit(solution)/shard_map/ppermute | solution.py:436
  23.4 5.3 %collective-permute-start.10 = (f32[32,512]{1,0:T(8,128)S(1)}, f32[32,512]{1,0:T(8,128)S(1)}, u32[]{:S(2)}, u32[]{:S(2)}) collective-permute-start(f32[32,512]{1,0:T(8,128)S(1)} %select_add_fusion), channel_id=1, source_target_pairs={{0,6},{1,7},{2,4},{3,5},{4,2},{5,3},{6,0},{7,1},{8,14},{9,15},{10,... | collective-permute-start | bytes 196616 | tf_op jit(solution)/shard_map/ppermute | solution.py:436
  24.9 5.0 %collective-permute-start.9 = (f32[32,512]{1,0:T(8,128)S(1)}, f32[32,512]{1,0:T(8,128)S(1)}, u32[]{:S(2)}, u32[]{:S(2)}) collective-permute-start(f32[32,512]{1,0:T(8,128)S(1)} %select_add_fusion), channel_id=1, source_target_pairs={{0,4},{1,5},{2,6},{3,7},{4,0},{5,1},{6,2},{7,3},{8,12},{9,13},{10,... | collective-permute-start | bytes 196616 | tf_op jit(solution)/shard_map/ppermute | solution.py:436
  26.4 4.3 %collective-permute-start.8 = (f32[32,512]{1,0:T(8,128)S(1)}, f32[32,512]{1,0:T(8,128)S(1)}, u32[]{:S(2)}, u32[]{:S(2)}) collective-permute-start(f32[32,512]{1,0:T(8,128)S(1)} %select_add_fusion), channel_id=1, source_target_pairs={{0,2},{1,3},{2,0},{3,1},{4,6},{5,7},{6,4},{7,5},{8,10},{9,11},{10,... | collective-permute-start | bytes 196616 | tf_op jit(solution)/shard_map/ppermute | solution.py:436
  30.7 6.7 %collective-permute-start.13 = (f32[32,512]{1,0:T(8,128)S(1)}, f32[32,512]{1,0:T(8,128)S(1)}, u32[]{:S(2)}, u32[]{:S(2)}) collective-permute-start(f32[32,512]{1,0:T(8,128)S(1)} %add_add_fusion.1), channel_id=1, source_target_pairs={{0,24},{1,25},{2,26},{3,27},{4,28},{5,29},{6,30},{7,31},{8,16},{9,... | collective-permute-start | bytes 196616 | tf_op jit(solution)/shard_map/ppermute | solution.py:436
  31.9 7.4 %collective-permute-start.12 = (f32[32,512]{1,0:T(8,128)S(1)}, f32[32,512]{1,0:T(8,128)S(1)}, u32[]{:S(2)}, u32[]{:S(2)}) collective-permute-start(f32[32,512]{1,0:T(8,128)S(1)} %add_add_fusion.1), channel_id=1, source_target_pairs={{0,16},{1,17},{2,18},{3,19},{4,20},{5,21},{6,22},{7,23},{8,24},{9,... | collective-permute-start | bytes 196616 | tf_op jit(solution)/shard_map/ppermute | solution.py:436
  33.2 6.0 %collective-permute-start.11 = (f32[32,512]{1,0:T(8,128)S(1)}, f32[32,512]{1,0:T(8,128)S(1)}, u32[]{:S(2)}, u32[]{:S(2)}) collective-permute-start(f32[32,512]{1,0:T(8,128)S(1)} %add_add_fusion.1), channel_id=1, source_target_pairs={{0,8},{1,9},{2,10},{3,11},{4,12},{5,13},{6,14},{7,15},{8,0},{9,1},... | collective-permute-start | bytes 196616 | tf_op jit(solution)/shard_map/ppermute | solution.py:436
  39.3 1.3 %collective-permute-start.14 = (f32[32,512]{1,0:T(8,128)S(1)}, f32[32,512]{1,0:T(8,128)S(1)}, u32[]{:S(2)}, u32[]{:S(2)}) collective-permute-start(f32[32,512]{1,0:T(8,128)S(1)} %add_add_fusion), channel_id=1, source_target_pairs={{0,1},{1,0},{2,3},{3,2},{4,5},{5,4},{6,7},{7,6},{8,9},{9,8},{10,11... | collective-permute-start | bytes 196616 | tf_op jit(solution)/shard_map/ppermute | solution.py:436
  42.9 1.3 %collective-permute-start.15 = (f32[64,64]{1,0:T(8,128)S(1)}, f32[64,64]{1,0:T(8,128)S(1)}, u32[]{:S(2)}, u32[]{:S(2)}) collective-permute-start(f32[64,64]{1,0:T(8,128)S(1)} %convolution_multiply_fusion), channel_id=1, source_target_pairs={{0,1},{1,0},{2,3},{3,2},{4,5},{5,4},{6,7},{7,6},{8,9},{9,8},{10,11... | collective-permute-start | bytes 49160 | tf_op jit(solution)/shard_map/ppermute | solution.py:436
  44.2 4.8 %collective-permute-start.18 = (f32[64,64]{1,0:T(8,128)S(1)}, f32[64,64]{1,0:T(8,128)S(1)}, u32[]{:S(2)}, u32[]{:S(2)}) collective-permute-start(f32[64,64]{1,0:T(8,128)S(1)} %add.54), channel_id=1, source_target_pairs={{0,6},{1,7},{2,4},{3,5},{4,2},{5,3},{6,0},{7,1},{8,14},{9,15},{10,... | collective-permute-start | bytes 49160 | tf_op jit(solution)/shard_map/ppermute | solution.py:436
  45.5 3.9 %collective-permute-start.17 = (f32[64,64]{1,0:T(8,128)S(1)}, f32[64,64]{1,0:T(8,128)S(1)}, u32[]{:S(2)}, u32[]{:S(2)}) collective-permute-start(f32[64,64]{1,0:T(8,128)S(1)} %add.54), channel_id=1, source_target_pairs={{0,4},{1,5},{2,6},{3,7},{4,0},{5,1},{6,2},{7,3},{8,12},{9,13},{10,... | collective-permute-start | bytes 49160 | tf_op jit(solution)/shard_map/ppermute | solution.py:436
  45.7 3.9 %collective-permute-start.16 = (f32[64,64]{1,0:T(8,128)S(1)}, f32[64,64]{1,0:T(8,128)S(1)}, u32[]{:S(2)}, u32[]{:S(2)}) collective-permute-start(f32[64,64]{1,0:T(8,128)S(1)} %add.54), channel_id=1, source_target_pairs={{0,2},{1,3},{2,0},{3,1},{4,6},{5,7},{6,4},{7,5},{8,10},{9,11},{10,... | collective-permute-start | bytes 49160 | tf_op jit(solution)/shard_map/ppermute | solution.py:436
  49.6 6.7 %collective-permute-start.21 = (f32[64,64]{1,0:T(8,128)S(1)}, f32[64,64]{1,0:T(8,128)S(1)}, u32[]{:S(2)}, u32[]{:S(2)}) collective-permute-start(f32[64,64]{1,0:T(8,128)S(1)} %add_add_fusion.3), channel_id=1, source_target_pairs={{0,24},{1,25},{2,26},{3,27},{4,28},{5,29},{6,30},{7,31},{8,16},{9,... | collective-permute-start | bytes 49160 | tf_op jit(solution)/shard_map/ppermute | solution.py:436
  52.0 4.8 %collective-permute-start.20 = (f32[64,64]{1,0:T(8,128)S(1)}, f32[64,64]{1,0:T(8,128)S(1)}, u32[]{:S(2)}, u32[]{:S(2)}) collective-permute-start(f32[64,64]{1,0:T(8,128)S(1)} %add_add_fusion.3), channel_id=1, source_target_pairs={{0,16},{1,17},{2,18},{3,19},{4,20},{5,21},{6,22},{7,23},{8,24},{9,... | collective-permute-start | bytes 49160 | tf_op jit(solution)/shard_map/ppermute | solution.py:436
  52.0 4.8 %collective-permute-start.19 = (f32[64,64]{1,0:T(8,128)S(1)}, f32[64,64]{1,0:T(8,128)S(1)}, u32[]{:S(2)}, u32[]{:S(2)}) collective-permute-start(f32[64,64]{1,0:T(8,128)S(1)} %add_add_fusion.3), channel_id=1, source_target_pairs={{0,8},{1,9},{2,10},{3,11},{4,12},{5,13},{6,14},{7,15},{8,0},{9,1},... | collective-permute-start | bytes 49160 | tf_op jit(solution)/shard_map/ppermute | solution.py:436

commit v5 on v4

--- a/solution.py
+++ b/solution.py
@@ -155,12 +155,12 @@
     return dot(left_top, right_top, contract, None) + small
 
 
-def outer(left, right):
+def outer(left, right, exact=True):
     a, b, c = split(left, 3)
     d, e, f = split(right, 3)
-    left = jnp.concatenate([a, a, b, a, c, b], axis=0).astype(jnp.float32)
-    right = jnp.concatenate([d, e, d, f, d, e], axis=0)
-    return dot(left.T.astype(jnp.bfloat16), right, precision=None)
+    lefts, rights = ([a, a, b, a, c, b], [d, e, d, f, d, e]) if exact else ([a, a, b], [d, e, d])
+    left = jnp.concatenate(lefts, axis=0).astype(jnp.float32)
+    return dot(left.T.astype(jnp.bfloat16), jnp.concatenate(rights, axis=0), precision=None)
 
 
 NT = ((1,), (1,))
@@ -225,7 +225,7 @@
     shape = jax.ShapeDtypeStruct((rows, modes), jnp.bfloat16)
     return pl.pallas_call(
         pieces_kernel, out_shape=(shape, shape),
-        in_specs=[pl.BlockSpec(memory_space=pl.ANY)], out_specs=(spec, spec),
+        in_specs=[pl.BlockSpec(memory_space=pltpu.HBM)], out_specs=(spec, spec),
         scratch_shapes=[
             pltpu.VMEM((2, chunk, modes), jnp.float32), pltpu.SemaphoreType.DMA((2,))
         ],
@@ -236,19 +236,12 @@
     )(old_basis)
 
 
-def deal_kernel(name, snaps_hbm, *refs):
-    blocks, done = refs[:-1], refs[-1]
+def deal_kernel(name, snaps_ref, *blocks):
     cells = blocks[0].shape[1]
     index = lax.axis_index(name)
-    copies = []
     for mask, block in enumerate(blocks):
         start = pl.multiple_of(jnp.bitwise_xor(index, mask) * cells, LANES)
-        copies.append(
-            pltpu.make_async_copy(snaps_hbm.at[:, pl.ds(start, cells)], block, done.at[mask])
-        )
-        copies[-1].start()
-    for copy in copies:
-        copy.wait()
+        block[...] = snaps_ref[:, pl.ds(start, cells)]
 
 
 def deal(snapshots, name):
@@ -258,8 +251,7 @@
     return pl.pallas_call(
         functools.partial(deal_kernel, name),
         out_shape=[jax.ShapeDtypeStruct((rows, cells), jnp.float32)] * count,
-        in_specs=[pl.BlockSpec(memory_space=pl.ANY)], out_specs=[spec] * count,
-        scratch_shapes=[pltpu.SemaphoreType.DMA((count,))],
+        in_specs=[spec], out_specs=[spec] * count,
         compiler_params=pltpu.CompilerParams(vmem_limit_bytes=VMEM),
     )(snapshots)
 
@@ -300,7 +292,6 @@
 def rotation(coeffs_ref, gram_ref, upper, square_ref, inverse, second, work):
     coeffs = coeffs_ref[...]
     mid = coeffs.shape[1] // 2
-    square = square_ref
 
     def first_gram():
         second[...] = square_ref[...] + outer(coeffs, dot(gram_ref[...], coeffs))
@@ -308,10 +299,20 @@
     first_gram()
 
     def far(carry):
-        return jnp.logical_not(carry[1] < NEAR) & (carry[0] < 8)
+        return jnp.logical_not(carry[1] < NEAR) & (carry[0] < 12)
+
+    one = jnp.where(diagonal(square_ref), 1.0, 0.0)
+
+    def mirror():
+        second[:mid, mid:] = second[mid:, :mid].T
 
     def factor_pass(carry):
-        count, _, fresh = carry
+        count, _, fresh, shift = carry
+
+        @pl.when(count > 0)
+        def _():
+            second[...] = second[...] + one
+
         factor_inverse(second, work)
 
         @pl.when(fresh == 1)
@@ -322,31 +323,37 @@
         def _():
             inverse[...] = dot(second[...], inverse[...])
 
+        part = dot3(coeffs, inverse[...], NT)
+        side = dot3(gram_ref[...], part)
+        extra = outer(side, part, False) - one
         second[:mid, :] = dot(inverse[:mid, :mid], upper[:mid, :])
         second[mid:, :] = dot(inverse[mid:, :], upper[...])
-        part = dot3(inverse[...], coeffs, NT)
-        side = dot3(part, gram_ref[...])
         stacked = second[...]
-        gram_low = dot3(stacked[mid:], stacked, NT) + dot3(side[mid:], part, NT)
-        gram_top = dot3(stacked[:mid], stacked[:mid], NT) + dot3(side[:mid], part[:mid], NT)
-        second[:mid, :mid] = gram_top
-        second[mid:, :] = gram_low
-        second[:mid, mid:] = gram_low[:, :mid].T
-        rest = second[...] - jnp.where(diagonal(square), 1.0, 0.0)
-        size = jnp.sum(rest * rest)
+        rest_low = dot3(stacked[mid:], stacked, NT) + extra[mid:]
+        rest_top = dot3(stacked[:mid], stacked[:mid], NT) + extra[:mid, :mid]
+        second[:mid, :mid] = rest_top
+        second[mid:, :] = rest_low
+        size = (
+            jnp.sum(rest_top * rest_top)
+            + jnp.sum(rest_low[:, mid:] * rest_low[:, mid:])
+            + 2.0 * jnp.sum(rest_low[:, :mid] * rest_low[:, :mid])
+        )
         failed = jnp.logical_not(size < BOUND)
 
         @pl.when(failed)
         def _():
             first_gram()
-            ends = jnp.where(diagonal(square), second[...], 0.0)
-            second[...] = second[...] + jnp.where(diagonal(square), SHIFT * jnp.max(ends), 0.0)
-
-        return count + 1, size, failed.astype(jnp.int32)
-
-    _, size, _ = lax.while_loop(far, factor_pass, (jnp.int32(0), jnp.float32(BOUND), jnp.int32(1)))
-
-    second[...] = second[...] - jnp.where(diagonal(square), 1.0, 0.0)
+            ends = one * second[...]
+            second[...] = second[...] + (shift * jnp.max(ends) - 1.0) * one
+
+        @pl.when(jnp.logical_not(failed) & (size >= STOP))
+        def _():
+            mirror()
+
+        return count + 1, size, failed.astype(jnp.int32), jnp.where(failed, 8.0 * shift, shift)
+
+    first = (jnp.int32(0), jnp.float32(BOUND), jnp.int32(1), jnp.float32(SHIFT))
+    size = lax.while_loop(far, factor_pass, first)[1]
 
     def more(carry):
         return (carry[0] >= STOP) & (carry[1] < 16)
@@ -373,7 +380,7 @@
     rotation(coeffs_ref, gram_ref, upper, square_ref, inverse, second, work)
     final = inverse[...]
     turn_top, turn_low = split(final * squares_ref[...], 2)
-    across_top, across_low = split(dot(final, coeffs_ref[...], NT).T, 2)
+    across_top, across_low = split(dot(coeffs_ref[...], final, NT), 2)
     across = jnp.concatenate([across_top, across_low, across_top], axis=0)
     chunk = chunk_of(rows)
     copies = []
@@ -473,9 +480,9 @@
 def exchange_rows(snapshots):
     name = AXES[0]
     count = lax.axis_size(name)
-    if count > 8 or count & (count - 1) or snapshots.shape[0] % 8:
+    if count > 8 or count & (count - 1) or snapshots.shape[0] % 8 or snapshots.shape[1] % (count * LANES):
         return [lax.all_to_all(snapshots, name, split_axis=1, concat_axis=0, tiled=True)]
-    blocks = deal(snapshots, name)
+    blocks = list(deal(snapshots, name))
     return [
         lax.ppermute(block, name, [(i, i ^ mask) for i in range(count)]) if mask else block
         for mask, block in enumerate(blocks)

time: 88.7 us -> 87.6 us (0.988)
  Pallas kernels: 36 us -> 34.8 us
where the time goes in v5:
time: 87.6 us; the launch traced here: 87.4 us
  Pallas kernels  34.8 us (40%)
  starting transfers between devices  28.8 us (33%)
  waiting for transfers between devices  17.9 us (20%)
  local copies, waits for them, and re-layouts  3.15 us (4%)
  matrix products  2.3 us (3%)
    pallas_call x1, Pallas kernels, updated_basis(): pl.pallas_call(update_kernel, out_shape=jax.ShapeDtypeStruct((rows, modes...  31 us
    ppermute x15, starting transfers between devices, exchange(): return lax.ppermute(part, AXES, [(i, i ^ mask) for i in range(count)])  16.3 us
    ppermute x15, waiting for transfers between devices, exchange(): return lax.ppermute(part, AXES, [(i, i ^ mask) for i in range(count)])  13.8 us
    ppermute x7, starting transfers between devices, exchange_rows(): lax.ppermute(block, name, [(i, i ^ mask) for i in range(count)])  12.5 us
    ppermute x7, waiting for transfers between devices, exchange_rows(): lax.ppermute(block, name, [(i, i ^ mask) for i in range(count)])  4.06 us
    unnamed x8, local copies, waits for them, and re-layouts  3.15 us
    dot_general x2, matrix products, mat(): lax.dot_general(left, right, (contract, ((), ())), precision=precision, p...  2.3 us
    pallas_call x1, Pallas kernels, opening(): pl.pallas_call(opening_kernel, out_shape=(shape, shape), in_specs=[spec]...  2.19 us
  transfers between devices with their start and end apart: 22, of which 14 were waited for; matrix products, arithmetic and copies ran while one was open for 0% of the time, Pallas kernels for 3%

profile of v5, /device:TPU:0, one launch (start us, length us, event | category | flops | bytes accessed | tf_op | source)
XLA Modules:
  0.0 87.4 jit_solution(11790382608675967234)
XLA Ops:
  0.0 0.0 copy-start.2
  0.0 1.0 %copy-done.2 = f32[8,15360]{1,0:T(8,128)S(1)} copy-done((f32[8,15360]{1,0:T(8,128)S(1)}, f32[8,15360]{1,0:T(8,128)}, u32[]{:S(2)}) %copy-start.2) | copy-done | bytes 491544
  1.1 3.1 %collective-permute-start = (f32[8,1920]{1,0:T(8,128)S(1)}, f32[8,1920]{1,0:T(8,128)S(1)}, u32[]{:S(2)}, u32[]{:S(2)}) collective-permute-start(f32[8,1920]{1,0:T(8,128)S(1)} %get-tuple-element.21), channel_id=1, source_target_pairs={{0,4},{4,0},{8,12},{12,8},{16,20},{20,16},{24,28},{28,24},{1,5},{5... | collective-permute-start | bytes 184328 | tf_op jit(solution)/shard_map/ppermute | solution.py:487
  4.1 1.6 %collective-permute-start.1 = (f32[8,1920]{1,0:T(8,128)S(1)}, f32[8,1920]{1,0:T(8,128)S(1)}, u32[]{:S(2)}, u32[]{:S(2)}) collective-permute-start(f32[8,1920]{1,0:T(8,128)S(1)} %get-tuple-element.22), channel_id=1, source_target_pairs={{0,8},{4,12},{8,0},{12,4},{16,24},{20,28},{24,16},{28,20},{1,9},{5... | collective-permute-start | bytes 184328 | tf_op jit(solution)/shard_map/ppermute | solution.py:487
  5.7 0.0 collective-permute-start.2
  5.7 3.0 %collective-permute-start.3 = (f32[8,1920]{1,0:T(8,128)S(1)}, f32[8,1920]{1,0:T(8,128)S(1)}, u32[]{:S(2)}, u32[]{:S(2)}) collective-permute-start(f32[8,1920]{1,0:T(8,128)S(1)} %get-tuple-element.24), channel_id=1, source_target_pairs={{0,16},{4,20},{8,24},{12,28},{16,0},{20,4},{24,8},{28,12},{1,17},{... | collective-permute-start | bytes 184328 | tf_op jit(solution)/shard_map/ppermute | solution.py:487
  8.7 1.3 %collective-permute-start.4 = (f32[8,1920]{1,0:T(8,128)S(1)}, f32[8,1920]{1,0:T(8,128)S(1)}, u32[]{:S(2)}, u32[]{:S(2)}) collective-permute-start(f32[8,1920]{1,0:T(8,128)S(1)} %get-tuple-element.25), channel_id=1, source_target_pairs={{0,20},{4,16},{8,28},{12,24},{16,4},{20,0},{24,12},{28,8},{1,21},{... | collective-permute-start | bytes 184328 | tf_op jit(solution)/shard_map/ppermute | solution.py:487
  10.0 0.0 collective-permute-done.refs_1_
  10.0 3.6 %collective-permute-start.5 = (f32[8,1920]{1,0:T(8,128)S(1)}, f32[8,1920]{1,0:T(8,128)S(1)}, u32[]{:S(2)}, u32[]{:S(2)}) collective-permute-start(f32[8,1920]{1,0:T(8,128)S(1)} %get-tuple-element.26), channel_id=1, source_target_pairs={{0,24},{4,28},{8,16},{12,20},{16,8},{20,12},{24,0},{28,4},{1,25},{... | collective-permute-start | bytes 184328 | tf_op jit(solution)/shard_map/ppermute | solution.py:487
  13.6 0.0 collective-permute-done.1.refs_2_
  13.6 0.0 collective-permute-start.6
  13.6 0.0 copy-start
  13.6 2.1 %copy-done = f32[1920,512]{1,0:T(8,128)S(1)} copy-done((f32[1920,512]{1,0:T(8,128)S(1)}, f32[1920,512]{1,0:T(8,128)}, u32[]{:S(2)}) %copy-start) | copy-done | bytes 3932184
  15.7 0.0 copy-start.1
  15.7 0.8 shard_map.38
  16.5 0.0 collective-permute-done.2.refs_3_
  16.5 0.0 collective-permute-done.3.refs_4_
  16.6 1.8 %collective-permute-done.4.refs_5_ = f32[8,1920]{1,0:T(8,128)S(1)} collective-permute-done((f32[8,1920]{1,0:T(8,128)S(1)}, f32[8,1920]{1,0:T(8,128)S(1)}, u32[]{:S(2)}, u32[]{:S(2)}) %collective-permute-start.4) | collective-permute-done | bytes 61472 | tf_op jit(solution)/shard_map/ppermute | solution.py:487
  18.4 0.0 collective-permute-done.5.refs_6_
  18.4 2.2 %collective-permute-done.6.refs_7_ = f32[8,1920]{1,0:T(8,128)S(1)} collective-permute-done((f32[8,1920]{1,0:T(8,128)S(1)}, f32[8,1920]{1,0:T(8,128)S(1)}, u32[]{:S(2)}, u32[]{:S(2)}) %collective-permute-start.6) | collective-permute-done | bytes 61472 | tf_op jit(solution)/shard_map/ppermute | solution.py:487
  20.6 0.8 shard_map.39
  21.4 0.0 copy-start.3
  21.4 0.1 collective-permute-start.7
  21.5 1.2 %collective-permute-done.7 = f32[32,512]{1,0:T(8,128)S(1)} collective-permute-done((f32[32,512]{1,0:T(8,128)S(1)}, f32[32,512]{1,0:T(8,128)S(1)}, u32[]{:S(2)}, u32[]{:S(2)}) %collective-permute-start.7) | collective-permute-done | bytes 65568 | tf_op jit(solution)/shard_map/ppermute | solution.py:443
  22.8 1.5 %collective-permute-start.10 = (f32[32,512]{1,0:T(8,128)S(1)}, f32[32,512]{1,0:T(8,128)S(1)}, u32[]{:S(2)}, u32[]{:S(2)}) collective-permute-start(f32[32,512]{1,0:T(8,128)S(1)} %select_add_fusion), channel_id=1, source_target_pairs={{0,6},{1,7},{2,4},{3,5},{4,2},{5,3},{6,0},{7,1},{8,14},{9,15},{10,... | collective-permute-start | bytes 196616 | tf_op jit(solution)/shard_map/ppermute | solution.py:443
  24.3 1.5 %collective-permute-start.9 = (f32[32,512]{1,0:T(8,128)S(1)}, f32[32,512]{1,0:T(8,128)S(1)}, u32[]{:S(2)}, u32[]{:S(2)}) collective-permute-start(f32[32,512]{1,0:T(8,128)S(1)} %select_add_fusion), channel_id=1, source_target_pairs={{0,4},{1,5},{2,6},{3,7},{4,0},{5,1},{6,2},{7,3},{8,12},{9,13},{10,... | collective-permute-start | bytes 196616 | tf_op jit(solution)/shard_map/ppermute | solution.py:443
  25.8 0.5 collective-permute-start.8
  26.3 1.8 %collective-permute-done.10 = f32[32,512]{1,0:T(8,128)S(1)} collective-permute-done((f32[32,512]{1,0:T(8,128)S(1)}, f32[32,512]{1,0:T(8,128)S(1)}, u32[]{:S(2)}, u32[]{:S(2)}) %collective-permute-start.10) | collective-permute-done | bytes 65568 | tf_op jit(solution)/shard_map/ppermute | solution.py:443
  28.1 1.2 %collective-permute-done.9 = f32[32,512]{1,0:T(8,128)S(1)} collective-permute-done((f32[32,512]{1,0:T(8,128)S(1)}, f32[32,512]{1,0:T(8,128)S(1)}, u32[]{:S(2)}, u32[]{:S(2)}) %collective-permute-start.9) | collective-permute-done | bytes 65568 | tf_op jit(solution)/shard_map/ppermute | solution.py:443
  29.3 0.8 collective-permute-done.8
  30.1 1.2 %collective-permute-start.13 = (f32[32,512]{1,0:T(8,128)S(1)}, f32[32,512]{1,0:T(8,128)S(1)}, u32[]{:S(2)}, u32[]{:S(2)}) collective-permute-start(f32[32,512]{1,0:T(8,128)S(1)} %add_add_fusion.1), channel_id=1, source_target_pairs={{0,24},{1,25},{2,26},{3,27},{4,28},{5,29},{6,30},{7,31},{8,16},{9,... | collective-permute-start | bytes 196616 | tf_op jit(solution)/shard_map/ppermute | solution.py:443
  31.2 1.4 %collective-permute-start.12 = (f32[32,512]{1,0:T(8,128)S(1)}, f32[32,512]{1,0:T(8,128)S(1)}, u32[]{:S(2)}, u32[]{:S(2)}) collective-permute-start(f32[32,512]{1,0:T(8,128)S(1)} %add_add_fusion.1), channel_id=1, source_target_pairs={{0,16},{1,17},{2,18},{3,19},{4,20},{5,21},{6,22},{7,23},{8,24},{9,... | collective-permute-start | bytes 196616 | tf_op jit(solution)/shard_map/ppermute | solution.py:443
  32.6 1.9 %collective-permute-start.11 = (f32[32,512]{1,0:T(8,128)S(1)}, f32[32,512]{1,0:T(8,128)S(1)}, u32[]{:S(2)}, u32[]{:S(2)}) collective-permute-start(f32[32,512]{1,0:T(8,128)S(1)} %add_add_fusion.1), channel_id=1, source_target_pairs={{0,8},{1,9},{2,10},{3,11},{4,12},{5,13},{6,14},{7,15},{8,0},{9,1},... | collective-permute-start | bytes 196616 | tf_op jit(solution)/shard_map/ppermute | solution.py:443
  34.5 2.3 %collective-permute-done.13 = f32[32,512]{1,0:T(8,128)S(1)} collective-permute-done((f32[32,512]{1,0:T(8,128)S(1)}, f32[32,512]{1,0:T(8,128)S(1)}, u32[]{:S(2)}, u32[]{:S(2)}) %collective-permute-start.13) | collective-permute-done | bytes 65568 | tf_op jit(solution)/shard_map/ppermute | solution.py:443
  36.8 1.8 %collective-permute-done.12 = f32[32,512]{1,0:T(8,128)S(1)} collective-permute-done((f32[32,512]{1,0:T(8,128)S(1)}, f32[32,512]{1,0:T(8,128)S(1)}, u32[]{:S(2)}, u32[]{:S(2)}) %collective-permute-start.12) | collective-permute-done | bytes 65568 | tf_op jit(solution)/shard_map/ppermute | solution.py:443
  38.6 0.0 collective-permute-done.11
  38.6 0.1 collective-permute-start.14
  38.7 1.2 %collective-permute-done.14 = f32[32,512]{1,0:T(8,128)S(1)} collective-permute-done((f32[32,512]{1,0:T(8,128)S(1)}, f32[32,512]{1,0:T(8,128)S(1)}, u32[]{:S(2)}, u32[]{:S(2)}) %collective-permute-start.14) | collective-permute-done | bytes 65568 | tf_op jit(solution)/shard_map/ppermute | solution.py:443
  40.0 0.0 copy-done.1
  40.0 1.9 %convolution_subtract_fusion = f32[64,1920]{1,0:T(8,128)S(1)} fusion(f32[64,1920]{1,0:T(8,128)S(1)} %get-tuple-element.31.snaps_ref, f32[1920,512]{1,0:T(8,128)S(1)} %copy-done.1, f32[32,512]{1,0:T(8,128)S(1)} %get-tuple-element.36, f32[32,512]{1,0:T(8,128)S(1)} %get-tuple-element.35), kind=kOutput, calls=%fused_computation | convolution fusion | flops 377643008 | bytes 5046272 | tf_op jit(solution)/shard_map/dot_general | solution.py:433
  41.9 0.4 convolution_multiply_fusion
  42.3 0.2 collective-permute-start.15
  42.5 0.0 copy-done.3
  42.5 1.0 %collective-permute-done.15 = f32[64,64]{1,0:T(8,128)S(1)} collective-permute-done((f32[64,64]{1,0:T(8,128)S(1)}, f32[64,64]{1,0:T(8,128)S(1)}, u32[]{:S(2)}, u32[]{:S(2)}) %collective-permute-start.15) | collective-permute-done | bytes 16416 | tf_op jit(solution)/shard_map/ppermute | solution.py:443
  43.5 1.3 %collective-permute-start.18 = (f32[64,64]{1,0:T(8,128)S(1)}, f32[64,64]{1,0:T(8,128)S(1)}, u32[]{:S(2)}, u32[]{:S(2)}) collective-permute-start(f32[64,64]{1,0:T(8,128)S(1)} %add.54), channel_id=1, source_target_pairs={{0,6},{1,7},{2,4},{3,5},{4,2},{5,3},{6,0},{7,1},{8,14},{9,15},{10,... | collective-permute-start | bytes 49160 | tf_op jit(solution)/shard_map/ppermute | solution.py:443
  44.9 0.2 collective-permute-start.17
  45.0 2.0 %collective-permute-start.16 = (f32[64,64]{1,0:T(8,128)S(1)}, f32[64,64]{1,0:T(8,128)S(1)}, u32[]{:S(2)}, u32[]{:S(2)}) collective-permute-start(f32[64,64]{1,0:T(8,128)S(1)} %add.54), channel_id=1, source_target_pairs={{0,2},{1,3},{2,0},{3,1},{4,6},{5,7},{6,4},{7,5},{8,10},{9,11},{10,... | collective-permute-start | bytes 49160 | tf_op jit(solution)/shard_map/ppermute | solution.py:443
  47.0 1.3 %collective-permute-done.18 = f32[64,64]{1,0:T(8,128)S(1)} collective-permute-done((f32[64,64]{1,0:T(8,128)S(1)}, f32[64,64]{1,0:T(8,128)S(1)}, u32[]{:S(2)}, u32[]{:S(2)}) %collective-permute-start.18) | collective-permute-done | bytes 16416 | tf_op jit(solution)/shard_map/ppermute | solution.py:443
  48.4 0.4 collective-permute-done.17
  48.8 0.2 collective-permute-done.16
  49.0 2.4 %collective-permute-start.21 = (f32[64,64]{1,0:T(8,128)S(1)}, f32[64,64]{1,0:T(8,128)S(1)}, u32[]{:S(2)}, u32[]{:S(2)}) collective-permute-start(f32[64,64]{1,0:T(8,128)S(1)} %add_add_fusion.3), channel_id=1, source_target_pairs={{0,24},{1,25},{2,26},{3,27},{4,28},{5,29},{6,30},{7,31},{8,16},{9,... | collective-permute-start | bytes 49160 | tf_op jit(solution)/shard_map/ppermute | solution.py:443
  51.4 0.0 collective-permute-start.20
  51.4 2.0 %collective-permute-start.19 = (f32[64,64]{1,0:T(8,128)S(1)}, f32[64,64]{1,0:T(8,128)S(1)}, u32[]{:S(2)}, u32[]{:S(2)}) collective-permute-start(f32[64,64]{1,0:T(8,128)S(1)} %add_add_fusion.3), channel_id=1, source_target_pairs={{0,8},{1,9},{2,10},{3,11},{4,12},{5,13},{6,14},{7,15},{8,0},{9,1},... | collective-permute-start | bytes 49160 | tf_op jit(solution)/shard_map/ppermute | solution.py:443
  53.4 2.2 %shard_map.40 = (f32[512,512]{1,0:T(8,128)S(1)}, f32[512,512]{1,0:T(8,128)S(1)}) custom-call(f32[64,512]{1,0:T(8,128)S(1)} %pad_maximum_fusion.coeffs_ref, f32[1,512]{1,0:T(1,128)S(1)} %bitcast.4), custom_call_target="tpu_custom_call" | custom-call | flops 1610612736 | bytes 2097152 | tf_op jit(solution)/shard_map/pallas_call | solution.py:194
  55.6 0.0 collective-permute-done.21
  55.6 0.6 collective-permute-done.20
  56.2 0.0 collective-permute-done.19
  56.2 31.0 %shard_map.41 = bf16[1920,512]{1,0:T(8,128)(2,1)} custom-call(f32[64,512]{1,0:T(8,128)S(1)} %pad_maximum_fusion.coeffs_ref, f32[64,64]{1,0:T(8,128)S(1)} %add_add_fusion.2.gram_ref, f32[1,512]{1,0:T(1,128)S(1)} %bitcast.5, f32[512,512]{1,0:T(8,128)S(1)} %get-tuple-element.33.upper, f32[512,512]{1,0:T(8,128)S(1)} %get-tuple-element.34.square_ref, ...), custom_call_target="tpu_custom_call" | custom-call | tf_op jit(solution)/shard_map/pallas_call | solution.py:416
  (11 shorter events, 0.1 us)
Async XLA Ops:
  0.0 1.0 %copy-start.2 = (f32[8,15360]{1,0:T(8,128)S(1)}, f32[8,15360]{1,0:T(8,128)}, u32[]{:S(2)}) copy-start(f32[8,15360]{1,0:T(8,128)} %snaps_ref.1) | copy-start | bytes 1474564
  1.1 8.9 %collective-permute-start = (f32[8,1920]{1,0:T(8,128)S(1)}, f32[8,1920]{1,0:T(8,128)S(1)}, u32[]{:S(2)}, u32[]{:S(2)}) collective-permute-start(f32[8,1920]{1,0:T(8,128)S(1)} %get-tuple-element.21), channel_id=1, source_target_pairs={{0,4},{4,0},{8,12},{12,8},{16,20},{20,16},{24,28},{28,24},{1,5},{5... | collective-permute-start | bytes 184328 | tf_op jit(solution)/shard_map/ppermute | solution.py:487
  4.1 9.5 %collective-permute-start.1 = (f32[8,1920]{1,0:T(8,128)S(1)}, f32[8,1920]{1,0:T(8,128)S(1)}, u32[]{:S(2)}, u32[]{:S(2)}) collective-permute-start(f32[8,1920]{1,0:T(8,128)S(1)} %get-tuple-element.22), channel_id=1, source_target_pairs={{0,8},{4,12},{8,0},{12,4},{16,24},{20,28},{24,16},{28,20},{1,9},{5... | collective-permute-start | bytes 184328 | tf_op jit(solution)/shard_map/ppermute | solution.py:487
  5.7 10.8 %collective-permute-start.2 = (f32[8,1920]{1,0:T(8,128)S(1)}, f32[8,1920]{1,0:T(8,128)S(1)}, u32[]{:S(2)}, u32[]{:S(2)}) collective-permute-start(f32[8,1920]{1,0:T(8,128)S(1)} %get-tuple-element.23), channel_id=1, source_target_pairs={{0,12},{4,8},{8,4},{12,0},{16,28},{20,24},{24,20},{28,16},{1,13},{... | collective-permute-start | bytes 184328 | tf_op jit(solution)/shard_map/ppermute | solution.py:487
  5.7 10.8 %collective-permute-start.3 = (f32[8,1920]{1,0:T(8,128)S(1)}, f32[8,1920]{1,0:T(8,128)S(1)}, u32[]{:S(2)}, u32[]{:S(2)}) collective-permute-start(f32[8,1920]{1,0:T(8,128)S(1)} %get-tuple-element.24), channel_id=1, source_target_pairs={{0,16},{4,20},{8,24},{12,28},{16,0},{20,4},{24,8},{28,12},{1,17},{... | collective-permute-start | bytes 184328 | tf_op jit(solution)/shard_map/ppermute | solution.py:487
  8.7 9.7 %collective-permute-start.4 = (f32[8,1920]{1,0:T(8,128)S(1)}, f32[8,1920]{1,0:T(8,128)S(1)}, u32[]{:S(2)}, u32[]{:S(2)}) collective-permute-start(f32[8,1920]{1,0:T(8,128)S(1)} %get-tuple-element.25), channel_id=1, source_target_pairs={{0,20},{4,16},{8,28},{12,24},{16,4},{20,0},{24,12},{28,8},{1,21},{... | collective-permute-start | bytes 184328 | tf_op jit(solution)/shard_map/ppermute | solution.py:487
  10.0 8.4 %collective-permute-start.5 = (f32[8,1920]{1,0:T(8,128)S(1)}, f32[8,1920]{1,0:T(8,128)S(1)}, u32[]{:S(2)}, u32[]{:S(2)}) collective-permute-start(f32[8,1920]{1,0:T(8,128)S(1)} %get-tuple-element.26), channel_id=1, source_target_pairs={{0,24},{4,28},{8,16},{12,20},{16,8},{20,12},{24,0},{28,4},{1,25},{... | collective-permute-start | bytes 184328 | tf_op jit(solution)/shard_map/ppermute | solution.py:487
  13.6 7.0 %collective-permute-start.6 = (f32[8,1920]{1,0:T(8,128)S(1)}, f32[8,1920]{1,0:T(8,128)S(1)}, u32[]{:S(2)}, u32[]{:S(2)}) collective-permute-start(f32[8,1920]{1,0:T(8,128)S(1)} %get-tuple-element.27), channel_id=1, source_target_pairs={{0,28},{4,24},{8,20},{12,16},{16,12},{20,8},{24,4},{28,0},{1,29},{... | collective-permute-start | bytes 184328 | tf_op jit(solution)/shard_map/ppermute | solution.py:487
  13.6 2.1 %copy-start = (f32[1920,512]{1,0:T(8,128)S(1)}, f32[1920,512]{1,0:T(8,128)}, u32[]{:S(2)}) copy-start(f32[1920,512]{1,0:T(8,128)} %basis_hbm.1) | copy-start | bytes 11796484
  15.7 24.2 %copy-start.1 = (f32[1920,512]{1,0:T(8,128)S(1)}, f32[1920,512]{1,0:T(8,128)}, u32[]{:S(2)}) copy-start(f32[1920,512]{1,0:T(8,128)} %basis_hbm.1) | copy-start | bytes 11796484
  21.4 21.1 %copy-start.3 = (f32[512]{0:T(512)S(1)}, f32[512]{0:T(512)}, u32[]{:S(2)}) copy-start(f32[512]{0:T(512)} %param.5) | copy-start | bytes 6148
  21.4 1.3 %collective-permute-start.7 = (f32[32,512]{1,0:T(8,128)S(1)}, f32[32,512]{1,0:T(8,128)S(1)}, u32[]{:S(2)}, u32[]{:S(2)}) collective-permute-start(f32[32,512]{1,0:T(8,128)S(1)} %slice_select_fusion), channel_id=1, source_target_pairs={{0,1},{1,0},{2,3},{3,2},{4,5},{5,4},{6,7},{7,6},{8,9},{9,8},{10,11... | collective-permute-start | bytes 196616 | tf_op jit(solution)/shard_map/ppermute | solution.py:443
  22.8 5.3 %collective-permute-start.10 = (f32[32,512]{1,0:T(8,128)S(1)}, f32[32,512]{1,0:T(8,128)S(1)}, u32[]{:S(2)}, u32[]{:S(2)}) collective-permute-start(f32[32,512]{1,0:T(8,128)S(1)} %select_add_fusion), channel_id=1, source_target_pairs={{0,6},{1,7},{2,4},{3,5},{4,2},{5,3},{6,0},{7,1},{8,14},{9,15},{10,... | collective-permute-start | bytes 196616 | tf_op jit(solution)/shard_map/ppermute | solution.py:443
  24.3 5.0 %collective-permute-start.9 = (f32[32,512]{1,0:T(8,128)S(1)}, f32[32,512]{1,0:T(8,128)S(1)}, u32[]{:S(2)}, u32[]{:S(2)}) collective-permute-start(f32[32,512]{1,0:T(8,128)S(1)} %select_add_fusion), channel_id=1, source_target_pairs={{0,4},{1,5},{2,6},{3,7},{4,0},{5,1},{6,2},{7,3},{8,12},{9,13},{10,... | collective-permute-start | bytes 196616 | tf_op jit(solution)/shard_map/ppermute | solution.py:443
  25.8 4.3 %collective-permute-start.8 = (f32[32,512]{1,0:T(8,128)S(1)}, f32[32,512]{1,0:T(8,128)S(1)}, u32[]{:S(2)}, u32[]{:S(2)}) collective-permute-start(f32[32,512]{1,0:T(8,128)S(1)} %select_add_fusion), channel_id=1, source_target_pairs={{0,2},{1,3},{2,0},{3,1},{4,6},{5,7},{6,4},{7,5},{8,10},{9,11},{10,... | collective-permute-start | bytes 196616 | tf_op jit(solution)/shard_map/ppermute | solution.py:443
  30.1 6.7 %collective-permute-start.13 = (f32[32,512]{1,0:T(8,128)S(1)}, f32[32,512]{1,0:T(8,128)S(1)}, u32[]{:S(2)}, u32[]{:S(2)}) collective-permute-start(f32[32,512]{1,0:T(8,128)S(1)} %add_add_fusion.1), channel_id=1, source_target_pairs={{0,24},{1,25},{2,26},{3,27},{4,28},{5,29},{6,30},{7,31},{8,16},{9,... | collective-permute-start | bytes 196616 | tf_op jit(solution)/shard_map/ppermute | solution.py:443
  31.2 7.4 %collective-permute-start.12 = (f32[32,512]{1,0:T(8,128)S(1)}, f32[32,512]{1,0:T(8,128)S(1)}, u32[]{:S(2)}, u32[]{:S(2)}) collective-permute-start(f32[32,512]{1,0:T(8,128)S(1)} %add_add_fusion.1), channel_id=1, source_target_pairs={{0,16},{1,17},{2,18},{3,19},{4,20},{5,21},{6,22},{7,23},{8,24},{9,... | collective-permute-start | bytes 196616 | tf_op jit(solution)/shard_map/ppermute | solution.py:443
  32.6 6.0 %collective-permute-start.11 = (f32[32,512]{1,0:T(8,128)S(1)}, f32[32,512]{1,0:T(8,128)S(1)}, u32[]{:S(2)}, u32[]{:S(2)}) collective-permute-start(f32[32,512]{1,0:T(8,128)S(1)} %add_add_fusion.1), channel_id=1, source_target_pairs={{0,8},{1,9},{2,10},{3,11},{4,12},{5,13},{6,14},{7,15},{8,0},{9,1},... | collective-permute-start | bytes 196616 | tf_op jit(solution)/shard_map/ppermute | solution.py:443
  38.6 1.3 %collective-permute-start.14 = (f32[32,512]{1,0:T(8,128)S(1)}, f32[32,512]{1,0:T(8,128)S(1)}, u32[]{:S(2)}, u32[]{:S(2)}) collective-permute-start(f32[32,512]{1,0:T(8,128)S(1)} %add_add_fusion), channel_id=1, source_target_pairs={{0,1},{1,0},{2,3},{3,2},{4,5},{5,4},{6,7},{7,6},{8,9},{9,8},{10,11... | collective-permute-start | bytes 196616 | tf_op jit(solution)/shard_map/ppermute | solution.py:443
  42.3 1.3 %collective-permute-start.15 = (f32[64,64]{1,0:T(8,128)S(1)}, f32[64,64]{1,0:T(8,128)S(1)}, u32[]{:S(2)}, u32[]{:S(2)}) collective-permute-start(f32[64,64]{1,0:T(8,128)S(1)} %convolution_multiply_fusion), channel_id=1, source_target_pairs={{0,1},{1,0},{2,3},{3,2},{4,5},{5,4},{6,7},{7,6},{8,9},{9,8},{10,11... | collective-permute-start | bytes 49160 | tf_op jit(solution)/shard_map/ppermute | solution.py:443
  43.5 4.8 %collective-permute-start.18 = (f32[64,64]{1,0:T(8,128)S(1)}, f32[64,64]{1,0:T(8,128)S(1)}, u32[]{:S(2)}, u32[]{:S(2)}) collective-permute-start(f32[64,64]{1,0:T(8,128)S(1)} %add.54), channel_id=1, source_target_pairs={{0,6},{1,7},{2,4},{3,5},{4,2},{5,3},{6,0},{7,1},{8,14},{9,15},{10,... | collective-permute-start | bytes 49160 | tf_op jit(solution)/shard_map/ppermute | solution.py:443
  44.9 3.9 %collective-permute-start.17 = (f32[64,64]{1,0:T(8,128)S(1)}, f32[64,64]{1,0:T(8,128)S(1)}, u32[]{:S(2)}, u32[]{:S(2)}) collective-permute-start(f32[64,64]{1,0:T(8,128)S(1)} %add.54), channel_id=1, source_target_pairs={{0,4},{1,5},{2,6},{3,7},{4,0},{5,1},{6,2},{7,3},{8,12},{9,13},{10,... | collective-permute-start | bytes 49160 | tf_op jit(solution)/shard_map/ppermute | solution.py:443
  45.0 3.9 %collective-permute-start.16 = (f32[64,64]{1,0:T(8,128)S(1)}, f32[64,64]{1,0:T(8,128)S(1)}, u32[]{:S(2)}, u32[]{:S(2)}) collective-permute-start(f32[64,64]{1,0:T(8,128)S(1)} %add.54), channel_id=1, source_target_pairs={{0,2},{1,3},{2,0},{3,1},{4,6},{5,7},{6,4},{7,5},{8,10},{9,11},{10,... | collective-permute-start | bytes 49160 | tf_op jit(solution)/shard_map/ppermute | solution.py:443
  49.0 6.7 %collective-permute-start.21 = (f32[64,64]{1,0:T(8,128)S(1)}, f32[64,64]{1,0:T(8,128)S(1)}, u32[]{:S(2)}, u32[]{:S(2)}) collective-permute-start(f32[64,64]{1,0:T(8,128)S(1)} %add_add_fusion.3), channel_id=1, source_target_pairs={{0,24},{1,25},{2,26},{3,27},{4,28},{5,29},{6,30},{7,31},{8,16},{9,... | collective-permute-start | bytes 49160 | tf_op jit(solution)/shard_map/ppermute | solution.py:443
  51.4 4.8 %collective-permute-start.20 = (f32[64,64]{1,0:T(8,128)S(1)}, f32[64,64]{1,0:T(8,128)S(1)}, u32[]{:S(2)}, u32[]{:S(2)}) collective-permute-start(f32[64,64]{1,0:T(8,128)S(1)} %add_add_fusion.3), channel_id=1, source_target_pairs={{0,16},{1,17},{2,18},{3,19},{4,20},{5,21},{6,22},{7,23},{8,24},{9,... | collective-permute-start | bytes 49160 | tf_op jit(solution)/shard_map/ppermute | solution.py:443
  51.4 4.8 %collective-permute-start.19 = (f32[64,64]{1,0:T(8,128)S(1)}, f32[64,64]{1,0:T(8,128)S(1)}, u32[]{:S(2)}, u32[]{:S(2)}) collective-permute-start(f32[64,64]{1,0:T(8,128)S(1)} %add_add_fusion.3), channel_id=1, source_target_pairs={{0,8},{1,9},{2,10},{3,11},{4,12},{5,13},{6,14},{7,15},{8,0},{9,1},... | collective-permute-start | bytes 49160 | tf_op jit(solution)/shard_map/ppermute | solution.py:443

commit v6 on v5

--- a/solution.py
+++ b/solution.py
@@ -289,6 +289,27 @@
     )(*blocks, basis_top, basis_low)
 
 
+def residual_kernel(weight, coeffs_ref, snaps_ref, top_ref, low_ref, out_ref):
+    snaps = snaps_ref.shape[0]
+    top, low = split(coeffs_ref[...], 2)
+    value = dot(jnp.concatenate([top, low], axis=0), top_ref[...], NT, None)
+    value = value[:snaps] + (value[snaps:] + dot(top, low_ref[...], NT, None))
+    top, low = split(snaps_ref[...] - value, 2)
+    value = dot(jnp.concatenate([top, low], axis=0), top, NT, None)
+    out_ref[...] = (value[:snaps] + (value[snaps:] + value[snaps:].T)) * weight
+
+
+def residual_gram(coeffs, snap_rows, basis_top, basis_low, weight):
+    snaps = coeffs.shape[0]
+    spec = pl.BlockSpec(memory_space=pltpu.VMEM)
+    return pl.pallas_call(
+        functools.partial(residual_kernel, weight),
+        out_shape=jax.ShapeDtypeStruct((snaps, snaps), jnp.float32),
+        in_specs=[spec] * 4, out_specs=spec,
+        compiler_params=pltpu.CompilerParams(vmem_limit_bytes=VMEM),
+    )(coeffs, snap_rows, basis_top, basis_low)
+
+
 def rotation(coeffs_ref, gram_ref, upper, square_ref, inverse, second, work):
     coeffs = coeffs_ref[...]
     mid = coeffs.shape[1] // 2
@@ -426,15 +447,6 @@
     )(coeffs, gram_res, squares, upper, square, snap_rows, basis_top, basis_low)
 
 
-HIGH = lax.Precision.HIGH
-
-
-def mat(left, right, contract, precision=HIGH):
-    return lax.dot_general(
-        left, right, (contract, ((), ())), precision=precision, preferred_element_type=jnp.float32
-    )
-
-
 AXES = ("tile", "slab")
 
 
@@ -483,10 +495,9 @@
     if count > 8 or count & (count - 1) or snapshots.shape[0] % 8 or snapshots.shape[1] % (count * LANES):
         return [lax.all_to_all(snapshots, name, split_axis=1, concat_axis=0, tiled=True)]
     blocks = list(deal(snapshots, name))
-    return [
-        lax.ppermute(block, name, [(i, i ^ mask) for i in range(count)]) if mask else block
-        for mask, block in enumerate(blocks)
-    ]
+    for mask in range(1, count):
+        blocks[mask] = lax.ppermute(blocks[mask], name, [(i, i ^ mask) for i in range(count)])
+    return blocks
 
 
 def local(snapshots, old_basis, sing_values):
@@ -496,8 +507,7 @@
     weight_cell = 1.0 / cell_count
     part, snap_rows = local_coeffs(blocks, basis_top, basis_low, weight_cell)
     coeffs = sum_all_halved(part)
-    resid = snap_rows - mat(coeffs, old_basis, ((1,), (1,)))
-    gram_part = mat(resid, resid, ((1,), (1,))) * weight_cell
+    gram_part = residual_gram(coeffs, snap_rows, basis_top, basis_low, weight_cell)
     squares = (sing_values * sing_values)[None, :]
     gram_res = sum_all(gram_part)
     upper, square = opening(lax.optimization_barrier((coeffs, gram_part))[0], squares)

time: 87.6 us -> 83.4 us (0.952)
  matrix products: 2.3 us -> 0 us
  Pallas kernels: 34.8 us -> 32.9 us
    pallas_call x1, Pallas kernels: 31 us -> 27.4 us  [updated_basis(): pl.pallas_call(update_kernel, out_shape=jax.ShapeDtypeStruct((rows, modes...]
    dot_general x2 -> x0, matrix products: 2.3 us -> none  [mat(): lax.dot_general(left, right, (contract, ((), ())), precision=precision, p...]
    pallas_call x0 -> x1, Pallas kernels: none -> 1.63 us  [residual_gram(): pl.pallas_call(functools.partial(residual_kernel, weight), out_shape=jax....]
    unnamed x8 -> x6, local copies, waits for them, and re-layouts: 3.15 us -> 3.15 us
  transfers between devices with their start and end apart: 22 -> 22, of which waited for: 14 -> 14; matrix products, arithmetic and copies ran while one was open for 0% -> 0% of each run, Pallas kernels for 3% -> 4%
where the time goes in v6:
time: 83.4 us; the launch traced here: 83.2 us
  Pallas kernels  32.9 us (39%)
  starting transfers between devices  28.8 us (35%)
  waiting for transfers between devices  17.9 us (21%)
  local copies, waits for them, and re-layouts  3.15 us (4%)
    pallas_call x1, Pallas kernels, updated_basis(): pl.pallas_call(update_kernel, out_shape=jax.ShapeDtypeStruct((rows, modes...  27.4 us
    ppermute x15, starting transfers between devices, exchange(): return lax.ppermute(part, AXES, [(i, i ^ mask) for i in range(count)])  16.3 us
    ppermute x15, waiting for transfers between devices, exchange(): return lax.ppermute(part, AXES, [(i, i ^ mask) for i in range(count)])  13.8 us
    ppermute x7, starting transfers between devices, exchange_rows(): lax.ppermute(blocks[mask], name, [(i, i ^ mask) for i in range(count)])  12.5 us
    ppermute x7, waiting for transfers between devices, exchange_rows(): lax.ppermute(blocks[mask], name, [(i, i ^ mask) for i in range(count)])  4.07 us
    unnamed x6, local copies, waits for them, and re-layouts  3.15 us
    pallas_call x1, Pallas kernels, opening(): pl.pallas_call(opening_kernel, out_shape=(shape, shape), in_specs=[spec]...  2.18 us
  transfers between devices with their start and end apart: 22, of which 14 were waited for; matrix products, arithmetic and copies ran while one was open for 0% of the time, Pallas kernels for 4%

profile of v6, /device:TPU:0, one launch (start us, length us, event | category | flops | bytes accessed | tf_op | source)
XLA Modules:
  0.0 83.2 jit_solution(16538827234069020317)
XLA Ops:
  0.0 0.0 copy-start.1
  0.0 1.0 %copy-done.1 = f32[8,15360]{1,0:T(8,128)S(1)} copy-done((f32[8,15360]{1,0:T(8,128)S(1)}, f32[8,15360]{1,0:T(8,128)}, u32[]{:S(2)}) %copy-start.1) | copy-done | bytes 491544
  1.1 3.1 %collective-permute-start = (f32[8,1920]{1,0:T(8,128)S(1)}, f32[8,1920]{1,0:T(8,128)S(1)}, u32[]{:S(2)}, u32[]{:S(2)}) collective-permute-start(f32[8,1920]{1,0:T(8,128)S(1)} %get-tuple-element.21), channel_id=1, source_target_pairs={{0,4},{4,0},{8,12},{12,8},{16,20},{20,16},{24,28},{28,24},{1,5},{5... | collective-permute-start | bytes 184328 | tf_op jit(solution)/shard_map/ppermute | solution.py:499
  4.1 1.6 %collective-permute-start.1 = (f32[8,1920]{1,0:T(8,128)S(1)}, f32[8,1920]{1,0:T(8,128)S(1)}, u32[]{:S(2)}, u32[]{:S(2)}) collective-permute-start(f32[8,1920]{1,0:T(8,128)S(1)} %get-tuple-element.22), channel_id=1, source_target_pairs={{0,8},{4,12},{8,0},{12,4},{16,24},{20,28},{24,16},{28,20},{1,9},{5... | collective-permute-start | bytes 184328 | tf_op jit(solution)/shard_map/ppermute | solution.py:499
  5.7 0.0 collective-permute-start.2
  5.7 3.0 %collective-permute-start.3 = (f32[8,1920]{1,0:T(8,128)S(1)}, f32[8,1920]{1,0:T(8,128)S(1)}, u32[]{:S(2)}, u32[]{:S(2)}) collective-permute-start(f32[8,1920]{1,0:T(8,128)S(1)} %get-tuple-element.24), channel_id=1, source_target_pairs={{0,16},{4,20},{8,24},{12,28},{16,0},{20,4},{24,8},{28,12},{1,17},{... | collective-permute-start | bytes 184328 | tf_op jit(solution)/shard_map/ppermute | solution.py:499
  8.7 1.3 %collective-permute-start.4 = (f32[8,1920]{1,0:T(8,128)S(1)}, f32[8,1920]{1,0:T(8,128)S(1)}, u32[]{:S(2)}, u32[]{:S(2)}) collective-permute-start(f32[8,1920]{1,0:T(8,128)S(1)} %get-tuple-element.25), channel_id=1, source_target_pairs={{0,20},{4,16},{8,28},{12,24},{16,4},{20,0},{24,12},{28,8},{1,21},{... | collective-permute-start | bytes 184328 | tf_op jit(solution)/shard_map/ppermute | solution.py:499
  10.0 0.0 collective-permute-done.refs_1_
  10.0 3.6 %collective-permute-start.5 = (f32[8,1920]{1,0:T(8,128)S(1)}, f32[8,1920]{1,0:T(8,128)S(1)}, u32[]{:S(2)}, u32[]{:S(2)}) collective-permute-start(f32[8,1920]{1,0:T(8,128)S(1)} %get-tuple-element.26), channel_id=1, source_target_pairs={{0,24},{4,28},{8,16},{12,20},{16,8},{20,12},{24,0},{28,4},{1,25},{... | collective-permute-start | bytes 184328 | tf_op jit(solution)/shard_map/ppermute | solution.py:499
  13.6 0.0 collective-permute-done.1.refs_2_
  13.6 0.0 collective-permute-start.6
  13.6 0.0 copy-start
  13.6 2.1 %copy-done = f32[1920,512]{1,0:T(8,128)S(1)} copy-done((f32[1920,512]{1,0:T(8,128)S(1)}, f32[1920,512]{1,0:T(8,128)}, u32[]{:S(2)}) %copy-start) | copy-done | bytes 3932184
  15.7 0.8 shard_map.38
  16.5 0.0 collective-permute-done.2.refs_3_
  16.5 0.0 collective-permute-done.3.refs_4_
  16.6 1.8 %collective-permute-done.4.refs_5_ = f32[8,1920]{1,0:T(8,128)S(1)} collective-permute-done((f32[8,1920]{1,0:T(8,128)S(1)}, f32[8,1920]{1,0:T(8,128)S(1)}, u32[]{:S(2)}, u32[]{:S(2)}) %collective-permute-start.4) | collective-permute-done | bytes 61472 | tf_op jit(solution)/shard_map/ppermute | solution.py:499
  18.4 0.0 collective-permute-done.5.refs_6_
  18.4 2.2 %collective-permute-done.6.refs_7_ = f32[8,1920]{1,0:T(8,128)S(1)} collective-permute-done((f32[8,1920]{1,0:T(8,128)S(1)}, f32[8,1920]{1,0:T(8,128)S(1)}, u32[]{:S(2)}, u32[]{:S(2)}) %collective-permute-start.6) | collective-permute-done | bytes 61472 | tf_op jit(solution)/shard_map/ppermute | solution.py:499
  20.6 0.8 shard_map.39
  21.4 0.1 collective-permute-start.7
  21.5 1.2 %collective-permute-done.7 = f32[32,512]{1,0:T(8,128)S(1)} collective-permute-done((f32[32,512]{1,0:T(8,128)S(1)}, f32[32,512]{1,0:T(8,128)S(1)}, u32[]{:S(2)}, u32[]{:S(2)}) %collective-permute-start.7) | collective-permute-done | bytes 65568 | tf_op jit(solution)/shard_map/ppermute | solution.py:455
  22.7 1.5 %collective-permute-start.10 = (f32[32,512]{1,0:T(8,128)S(1)}, f32[32,512]{1,0:T(8,128)S(1)}, u32[]{:S(2)}, u32[]{:S(2)}) collective-permute-start(f32[32,512]{1,0:T(8,128)S(1)} %select_add_fusion), channel_id=1, source_target_pairs={{0,6},{1,7},{2,4},{3,5},{4,2},{5,3},{6,0},{7,1},{8,14},{9,15},{10,... | collective-permute-start | bytes 196616 | tf_op jit(solution)/shard_map/ppermute | solution.py:455
  24.2 1.5 %collective-permute-start.9 = (f32[32,512]{1,0:T(8,128)S(1)}, f32[32,512]{1,0:T(8,128)S(1)}, u32[]{:S(2)}, u32[]{:S(2)}) collective-permute-start(f32[32,512]{1,0:T(8,128)S(1)} %select_add_fusion), channel_id=1, source_target_pairs={{0,4},{1,5},{2,6},{3,7},{4,0},{5,1},{6,2},{7,3},{8,12},{9,13},{10,... | collective-permute-start | bytes 196616 | tf_op jit(solution)/shard_map/ppermute | solution.py:455
  25.8 0.5 collective-permute-start.8
  26.3 1.8 %collective-permute-done.10 = f32[32,512]{1,0:T(8,128)S(1)} collective-permute-done((f32[32,512]{1,0:T(8,128)S(1)}, f32[32,512]{1,0:T(8,128)S(1)}, u32[]{:S(2)}, u32[]{:S(2)}) %collective-permute-start.10) | collective-permute-done | bytes 65568 | tf_op jit(solution)/shard_map/ppermute | solution.py:455
  28.1 1.2 %collective-permute-done.9 = f32[32,512]{1,0:T(8,128)S(1)} collective-permute-done((f32[32,512]{1,0:T(8,128)S(1)}, f32[32,512]{1,0:T(8,128)S(1)}, u32[]{:S(2)}, u32[]{:S(2)}) %collective-permute-start.9) | collective-permute-done | bytes 65568 | tf_op jit(solution)/shard_map/ppermute | solution.py:455
  29.3 0.8 collective-permute-done.8
  30.1 1.2 %collective-permute-start.13 = (f32[32,512]{1,0:T(8,128)S(1)}, f32[32,512]{1,0:T(8,128)S(1)}, u32[]{:S(2)}, u32[]{:S(2)}) collective-permute-start(f32[32,512]{1,0:T(8,128)S(1)} %add_add_fusion.1), channel_id=1, source_target_pairs={{0,24},{1,25},{2,26},{3,27},{4,28},{5,29},{6,30},{7,31},{8,16},{9,... | collective-permute-start | bytes 196616 | tf_op jit(solution)/shard_map/ppermute | solution.py:455
  31.2 1.4 %collective-permute-start.12 = (f32[32,512]{1,0:T(8,128)S(1)}, f32[32,512]{1,0:T(8,128)S(1)}, u32[]{:S(2)}, u32[]{:S(2)}) collective-permute-start(f32[32,512]{1,0:T(8,128)S(1)} %add_add_fusion.1), channel_id=1, source_target_pairs={{0,16},{1,17},{2,18},{3,19},{4,20},{5,21},{6,22},{7,23},{8,24},{9,... | collective-permute-start | bytes 196616 | tf_op jit(solution)/shard_map/ppermute | solution.py:455
  32.6 1.9 %collective-permute-start.11 = (f32[32,512]{1,0:T(8,128)S(1)}, f32[32,512]{1,0:T(8,128)S(1)}, u32[]{:S(2)}, u32[]{:S(2)}) collective-permute-start(f32[32,512]{1,0:T(8,128)S(1)} %add_add_fusion.1), channel_id=1, source_target_pairs={{0,8},{1,9},{2,10},{3,11},{4,12},{5,13},{6,14},{7,15},{8,0},{9,1},... | collective-permute-start | bytes 196616 | tf_op jit(solution)/shard_map/ppermute | solution.py:455
  34.5 2.3 %collective-permute-done.13 = f32[32,512]{1,0:T(8,128)S(1)} collective-permute-done((f32[32,512]{1,0:T(8,128)S(1)}, f32[32,512]{1,0:T(8,128)S(1)}, u32[]{:S(2)}, u32[]{:S(2)}) %collective-permute-start.13) | collective-permute-done | bytes 65568 | tf_op jit(solution)/shard_map/ppermute | solution.py:455
  36.8 1.8 %collective-permute-done.12 = f32[32,512]{1,0:T(8,128)S(1)} collective-permute-done((f32[32,512]{1,0:T(8,128)S(1)}, f32[32,512]{1,0:T(8,128)S(1)}, u32[]{:S(2)}, u32[]{:S(2)}) %collective-permute-start.12) | collective-permute-done | bytes 65568 | tf_op jit(solution)/shard_map/ppermute | solution.py:455
  38.6 0.0 collective-permute-done.11
  38.6 0.1 collective-permute-start.14
  38.7 1.2 %collective-permute-done.14 = f32[32,512]{1,0:T(8,128)S(1)} collective-permute-done((f32[32,512]{1,0:T(8,128)S(1)}, f32[32,512]{1,0:T(8,128)S(1)}, u32[]{:S(2)}, u32[]{:S(2)}) %collective-permute-start.14) | collective-permute-done | bytes 65568 | tf_op jit(solution)/shard_map/ppermute | solution.py:455
  40.0 0.0 copy-start.2
  40.0 1.6 %shard_map.40 = f32[64,64]{1,0:T(8,128)S(1)} custom-call(f32[64,512]{1,0:T(8,128)S(1)} %pad_maximum_fusion.coeffs_ref, f32[64,1920]{1,0:T(8,128)S(1)} %get-tuple-element.31.snaps_ref, bf16[1920,512]{1,0:T(8,128)(2,1)S(1)} %get-tuple-element.28.refs_8_.top_ref, bf16[1920,512]{1,0:T(8,128)(2,1)S(1)} %get-tuple-element.29.refs_9_.low_ref), custom_call_target="tpu_custom_call" | custom-call | tf_op jit(solution)/shard_map/pallas_call | solution.py:305
  41.6 0.2 collective-permute-start.15
  41.8 1.0 %collective-permute-done.15 = f32[64,64]{1,0:T(8,128)S(1)} collective-permute-done((f32[64,64]{1,0:T(8,128)S(1)}, f32[64,64]{1,0:T(8,128)S(1)}, u32[]{:S(2)}, u32[]{:S(2)}) %collective-permute-start.15) | collective-permute-done | bytes 16416 | tf_op jit(solution)/shard_map/ppermute | solution.py:455
  42.9 1.3 %collective-permute-start.18 = (f32[64,64]{1,0:T(8,128)S(1)}, f32[64,64]{1,0:T(8,128)S(1)}, u32[]{:S(2)}, u32[]{:S(2)}) collective-permute-start(f32[64,64]{1,0:T(8,128)S(1)} %add.54), channel_id=1, source_target_pairs={{0,6},{1,7},{2,4},{3,5},{4,2},{5,3},{6,0},{7,1},{8,14},{9,15},{10,... | collective-permute-start | bytes 49160 | tf_op jit(solution)/shard_map/ppermute | solution.py:455
  44.2 0.2 collective-permute-start.17
  44.4 2.0 %collective-permute-start.16 = (f32[64,64]{1,0:T(8,128)S(1)}, f32[64,64]{1,0:T(8,128)S(1)}, u32[]{:S(2)}, u32[]{:S(2)}) collective-permute-start(f32[64,64]{1,0:T(8,128)S(1)} %add.54), channel_id=1, source_target_pairs={{0,2},{1,3},{2,0},{3,1},{4,6},{5,7},{6,4},{7,5},{8,10},{9,11},{10,... | collective-permute-start | bytes 49160 | tf_op jit(solution)/shard_map/ppermute | solution.py:455
  46.4 0.0 copy-done.2
  46.4 1.3 %collective-permute-done.18 = f32[64,64]{1,0:T(8,128)S(1)} collective-permute-done((f32[64,64]{1,0:T(8,128)S(1)}, f32[64,64]{1,0:T(8,128)S(1)}, u32[]{:S(2)}, u32[]{:S(2)}) %collective-permute-start.18) | collective-permute-done | bytes 16416 | tf_op jit(solution)/shard_map/ppermute | solution.py:455
  47.7 0.4 collective-permute-done.17
  48.1 0.2 collective-permute-done.16
  48.3 2.4 %collective-permute-start.21 = (f32[64,64]{1,0:T(8,128)S(1)}, f32[64,64]{1,0:T(8,128)S(1)}, u32[]{:S(2)}, u32[]{:S(2)}) collective-permute-start(f32[64,64]{1,0:T(8,128)S(1)} %add_add_fusion.3), channel_id=1, source_target_pairs={{0,24},{1,25},{2,26},{3,27},{4,28},{5,29},{6,30},{7,31},{8,16},{9,... | collective-permute-start | bytes 49160 | tf_op jit(solution)/shard_map/ppermute | solution.py:455
  50.7 0.0 collective-permute-start.20
  50.7 2.0 %collective-permute-start.19 = (f32[64,64]{1,0:T(8,128)S(1)}, f32[64,64]{1,0:T(8,128)S(1)}, u32[]{:S(2)}, u32[]{:S(2)}) collective-permute-start(f32[64,64]{1,0:T(8,128)S(1)} %add_add_fusion.3), channel_id=1, source_target_pairs={{0,8},{1,9},{2,10},{3,11},{4,12},{5,13},{6,14},{7,15},{8,0},{9,1},... | collective-permute-start | bytes 49160 | tf_op jit(solution)/shard_map/ppermute | solution.py:455
  52.8 2.2 %shard_map.41 = (f32[512,512]{1,0:T(8,128)S(1)}, f32[512,512]{1,0:T(8,128)S(1)}) custom-call(f32[64,512]{1,0:T(8,128)S(1)} %pad_maximum_fusion.coeffs_ref, f32[1,512]{1,0:T(1,128)S(1)} %bitcast.1), custom_call_target="tpu_custom_call" | custom-call | flops 1610612736 | bytes 2097152 | tf_op jit(solution)/shard_map/pallas_call | solution.py:194
  55.0 0.0 collective-permute-done.21
  55.0 0.6 collective-permute-done.20
  55.5 0.0 collective-permute-done.19
  55.6 27.4 %shard_map.42 = bf16[1920,512]{1,0:T(8,128)(2,1)} custom-call(f32[64,512]{1,0:T(8,128)S(1)} %pad_maximum_fusion.coeffs_ref, f32[64,64]{1,0:T(8,128)S(1)} %add_add_fusion.2.gram_ref, f32[1,512]{1,0:T(1,128)S(1)} %bitcast.2, f32[512,512]{1,0:T(8,128)S(1)} %get-tuple-element.33.upper, f32[512,512]{1,0:T(8,128)S(1)} %get-tuple-element.34.square_ref, ...), custom_call_target="tpu_custom_call" | custom-call | tf_op jit(solution)/shard_map/pallas_call | solution.py:437
  (11 shorter events, 0.1 us)
Async XLA Ops:
  0.0 1.0 %copy-start.1 = (f32[8,15360]{1,0:T(8,128)S(1)}, f32[8,15360]{1,0:T(8,128)}, u32[]{:S(2)}) copy-start(f32[8,15360]{1,0:T(8,128)} %snaps_ref.1) | copy-start | bytes 1474564
  1.1 8.9 %collective-permute-start = (f32[8,1920]{1,0:T(8,128)S(1)}, f32[8,1920]{1,0:T(8,128)S(1)}, u32[]{:S(2)}, u32[]{:S(2)}) collective-permute-start(f32[8,1920]{1,0:T(8,128)S(1)} %get-tuple-element.21), channel_id=1, source_target_pairs={{0,4},{4,0},{8,12},{12,8},{16,20},{20,16},{24,28},{28,24},{1,5},{5... | collective-permute-start | bytes 184328 | tf_op jit(solution)/shard_map/ppermute | solution.py:499
  4.1 9.5 %collective-permute-start.1 = (f32[8,1920]{1,0:T(8,128)S(1)}, f32[8,1920]{1,0:T(8,128)S(1)}, u32[]{:S(2)}, u32[]{:S(2)}) collective-permute-start(f32[8,1920]{1,0:T(8,128)S(1)} %get-tuple-element.22), channel_id=1, source_target_pairs={{0,8},{4,12},{8,0},{12,4},{16,24},{20,28},{24,16},{28,20},{1,9},{5... | collective-permute-start | bytes 184328 | tf_op jit(solution)/shard_map/ppermute | solution.py:499
  5.7 10.8 %collective-permute-start.2 = (f32[8,1920]{1,0:T(8,128)S(1)}, f32[8,1920]{1,0:T(8,128)S(1)}, u32[]{:S(2)}, u32[]{:S(2)}) collective-permute-start(f32[8,1920]{1,0:T(8,128)S(1)} %get-tuple-element.23), channel_id=1, source_target_pairs={{0,12},{4,8},{8,4},{12,0},{16,28},{20,24},{24,20},{28,16},{1,13},{... | collective-permute-start | bytes 184328 | tf_op jit(solution)/shard_map/ppermute | solution.py:499
  5.7 10.8 %collective-permute-start.3 = (f32[8,1920]{1,0:T(8,128)S(1)}, f32[8,1920]{1,0:T(8,128)S(1)}, u32[]{:S(2)}, u32[]{:S(2)}) collective-permute-start(f32[8,1920]{1,0:T(8,128)S(1)} %get-tuple-element.24), channel_id=1, source_target_pairs={{0,16},{4,20},{8,24},{12,28},{16,0},{20,4},{24,8},{28,12},{1,17},{... | collective-permute-start | bytes 184328 | tf_op jit(solution)/shard_map/ppermute | solution.py:499
  8.7 9.7 %collective-permute-start.4 = (f32[8,1920]{1,0:T(8,128)S(1)}, f32[8,1920]{1,0:T(8,128)S(1)}, u32[]{:S(2)}, u32[]{:S(2)}) collective-permute-start(f32[8,1920]{1,0:T(8,128)S(1)} %get-tuple-element.25), channel_id=1, source_target_pairs={{0,20},{4,16},{8,28},{12,24},{16,4},{20,0},{24,12},{28,8},{1,21},{... | collective-permute-start | bytes 184328 | tf_op jit(solution)/shard_map/ppermute | solution.py:499
  10.0 8.4 %collective-permute-start.5 = (f32[8,1920]{1,0:T(8,128)S(1)}, f32[8,1920]{1,0:T(8,128)S(1)}, u32[]{:S(2)}, u32[]{:S(2)}) collective-permute-start(f32[8,1920]{1,0:T(8,128)S(1)} %get-tuple-element.26), channel_id=1, source_target_pairs={{0,24},{4,28},{8,16},{12,20},{16,8},{20,12},{24,0},{28,4},{1,25},{... | collective-permute-start | bytes 184328 | tf_op jit(solution)/shard_map/ppermute | solution.py:499
  13.6 7.0 %collective-permute-start.6 = (f32[8,1920]{1,0:T(8,128)S(1)}, f32[8,1920]{1,0:T(8,128)S(1)}, u32[]{:S(2)}, u32[]{:S(2)}) collective-permute-start(f32[8,1920]{1,0:T(8,128)S(1)} %get-tuple-element.27), channel_id=1, source_target_pairs={{0,28},{4,24},{8,20},{12,16},{16,12},{20,8},{24,4},{28,0},{1,29},{... | collective-permute-start | bytes 184328 | tf_op jit(solution)/shard_map/ppermute | solution.py:499
  13.6 2.1 %copy-start = (f32[1920,512]{1,0:T(8,128)S(1)}, f32[1920,512]{1,0:T(8,128)}, u32[]{:S(2)}) copy-start(f32[1920,512]{1,0:T(8,128)} %basis_hbm.1) | copy-start | bytes 11796484
  21.4 1.3 %collective-permute-start.7 = (f32[32,512]{1,0:T(8,128)S(1)}, f32[32,512]{1,0:T(8,128)S(1)}, u32[]{:S(2)}, u32[]{:S(2)}) collective-permute-start(f32[32,512]{1,0:T(8,128)S(1)} %slice_select_fusion), channel_id=1, source_target_pairs={{0,1},{1,0},{2,3},{3,2},{4,5},{5,4},{6,7},{7,6},{8,9},{9,8},{10,11... | collective-permute-start | bytes 196616 | tf_op jit(solution)/shard_map/ppermute | solution.py:455
  22.7 5.3 %collective-permute-start.10 = (f32[32,512]{1,0:T(8,128)S(1)}, f32[32,512]{1,0:T(8,128)S(1)}, u32[]{:S(2)}, u32[]{:S(2)}) collective-permute-start(f32[32,512]{1,0:T(8,128)S(1)} %select_add_fusion), channel_id=1, source_target_pairs={{0,6},{1,7},{2,4},{3,5},{4,2},{5,3},{6,0},{7,1},{8,14},{9,15},{10,... | collective-permute-start | bytes 196616 | tf_op jit(solution)/shard_map/ppermute | solution.py:455
  24.2 5.0 %collective-permute-start.9 = (f32[32,512]{1,0:T(8,128)S(1)}, f32[32,512]{1,0:T(8,128)S(1)}, u32[]{:S(2)}, u32[]{:S(2)}) collective-permute-start(f32[32,512]{1,0:T(8,128)S(1)} %select_add_fusion), channel_id=1, source_target_pairs={{0,4},{1,5},{2,6},{3,7},{4,0},{5,1},{6,2},{7,3},{8,12},{9,13},{10,... | collective-permute-start | bytes 196616 | tf_op jit(solution)/shard_map/ppermute | solution.py:455
  25.8 4.3 %collective-permute-start.8 = (f32[32,512]{1,0:T(8,128)S(1)}, f32[32,512]{1,0:T(8,128)S(1)}, u32[]{:S(2)}, u32[]{:S(2)}) collective-permute-start(f32[32,512]{1,0:T(8,128)S(1)} %select_add_fusion), channel_id=1, source_target_pairs={{0,2},{1,3},{2,0},{3,1},{4,6},{5,7},{6,4},{7,5},{8,10},{9,11},{10,... | collective-permute-start | bytes 196616 | tf_op jit(solution)/shard_map/ppermute | solution.py:455
  30.1 6.7 %collective-permute-start.13 = (f32[32,512]{1,0:T(8,128)S(1)}, f32[32,512]{1,0:T(8,128)S(1)}, u32[]{:S(2)}, u32[]{:S(2)}) collective-permute-start(f32[32,512]{1,0:T(8,128)S(1)} %add_add_fusion.1), channel_id=1, source_target_pairs={{0,24},{1,25},{2,26},{3,27},{4,28},{5,29},{6,30},{7,31},{8,16},{9,... | collective-permute-start | bytes 196616 | tf_op jit(solution)/shard_map/ppermute | solution.py:455
  31.2 7.4 %collective-permute-start.12 = (f32[32,512]{1,0:T(8,128)S(1)}, f32[32,512]{1,0:T(8,128)S(1)}, u32[]{:S(2)}, u32[]{:S(2)}) collective-permute-start(f32[32,512]{1,0:T(8,128)S(1)} %add_add_fusion.1), channel_id=1, source_target_pairs={{0,16},{1,17},{2,18},{3,19},{4,20},{5,21},{6,22},{7,23},{8,24},{9,... | collective-permute-start | bytes 196616 | tf_op jit(solution)/shard_map/ppermute | solution.py:455
  32.6 6.0 %collective-permute-start.11 = (f32[32,512]{1,0:T(8,128)S(1)}, f32[32,512]{1,0:T(8,128)S(1)}, u32[]{:S(2)}, u32[]{:S(2)}) collective-permute-start(f32[32,512]{1,0:T(8,128)S(1)} %add_add_fusion.1), channel_id=1, source_target_pairs={{0,8},{1,9},{2,10},{3,11},{4,12},{5,13},{6,14},{7,15},{8,0},{9,1},... | collective-permute-start | bytes 196616 | tf_op jit(solution)/shard_map/ppermute | solution.py:455
  38.6 1.3 %collective-permute-start.14 = (f32[32,512]{1,0:T(8,128)S(1)}, f32[32,512]{1,0:T(8,128)S(1)}, u32[]{:S(2)}, u32[]{:S(2)}) collective-permute-start(f32[32,512]{1,0:T(8,128)S(1)} %add_add_fusion), channel_id=1, source_target_pairs={{0,1},{1,0},{2,3},{3,2},{4,5},{5,4},{6,7},{7,6},{8,9},{9,8},{10,11... | collective-permute-start | bytes 196616 | tf_op jit(solution)/shard_map/ppermute | solution.py:455
  40.0 6.4 %copy-start.2 = (f32[512]{0:T(512)S(1)}, f32[512]{0:T(512)}, u32[]{:S(2)}) copy-start(f32[512]{0:T(512)} %param.5) | copy-start | bytes 6148
  41.6 1.3 %collective-permute-start.15 = (f32[64,64]{1,0:T(8,128)S(1)}, f32[64,64]{1,0:T(8,128)S(1)}, u32[]{:S(2)}, u32[]{:S(2)}) collective-permute-start(f32[64,64]{1,0:T(8,128)S(1)} %shard_map.40), channel_id=1, source_target_pairs={{0,1},{1,0},{2,3},{3,2},{4,5},{5,4},{6,7},{7,6},{8,9},{9,8},{10,11... | collective-permute-start | bytes 49160 | tf_op jit(solution)/shard_map/ppermute | solution.py:455
  42.9 4.8 %collective-permute-start.18 = (f32[64,64]{1,0:T(8,128)S(1)}, f32[64,64]{1,0:T(8,128)S(1)}, u32[]{:S(2)}, u32[]{:S(2)}) collective-permute-start(f32[64,64]{1,0:T(8,128)S(1)} %add.54), channel_id=1, source_target_pairs={{0,6},{1,7},{2,4},{3,5},{4,2},{5,3},{6,0},{7,1},{8,14},{9,15},{10,... | collective-permute-start | bytes 49160 | tf_op jit(solution)/shard_map/ppermute | solution.py:455
  44.2 3.9 %collective-permute-start.17 = (f32[64,64]{1,0:T(8,128)S(1)}, f32[64,64]{1,0:T(8,128)S(1)}, u32[]{:S(2)}, u32[]{:S(2)}) collective-permute-start(f32[64,64]{1,0:T(8,128)S(1)} %add.54), channel_id=1, source_target_pairs={{0,4},{1,5},{2,6},{3,7},{4,0},{5,1},{6,2},{7,3},{8,12},{9,13},{10,... | collective-permute-start | bytes 49160 | tf_op jit(solution)/shard_map/ppermute | solution.py:455
  44.4 3.9 %collective-permute-start.16 = (f32[64,64]{1,0:T(8,128)S(1)}, f32[64,64]{1,0:T(8,128)S(1)}, u32[]{:S(2)}, u32[]{:S(2)}) collective-permute-start(f32[64,64]{1,0:T(8,128)S(1)} %add.54), channel_id=1, source_target_pairs={{0,2},{1,3},{2,0},{3,1},{4,6},{5,7},{6,4},{7,5},{8,10},{9,11},{10,... | collective-permute-start | bytes 49160 | tf_op jit(solution)/shard_map/ppermute | solution.py:455
  48.3 6.6 %collective-permute-start.21 = (f32[64,64]{1,0:T(8,128)S(1)}, f32[64,64]{1,0:T(8,128)S(1)}, u32[]{:S(2)}, u32[]{:S(2)}) collective-permute-start(f32[64,64]{1,0:T(8,128)S(1)} %add_add_fusion.3), channel_id=1, source_target_pairs={{0,24},{1,25},{2,26},{3,27},{4,28},{5,29},{6,30},{7,31},{8,16},{9,... | collective-permute-start | bytes 49160 | tf_op jit(solution)/shard_map/ppermute | solution.py:455
  50.7 4.8 %collective-permute-start.20 = (f32[64,64]{1,0:T(8,128)S(1)}, f32[64,64]{1,0:T(8,128)S(1)}, u32[]{:S(2)}, u32[]{:S(2)}) collective-permute-start(f32[64,64]{1,0:T(8,128)S(1)} %add_add_fusion.3), channel_id=1, source_target_pairs={{0,16},{1,17},{2,18},{3,19},{4,20},{5,21},{6,22},{7,23},{8,24},{9,... | collective-permute-start | bytes 49160 | tf_op jit(solution)/shard_map/ppermute | solution.py:455
  50.7 4.8 %collective-permute-start.19 = (f32[64,64]{1,0:T(8,128)S(1)}, f32[64,64]{1,0:T(8,128)S(1)}, u32[]{:S(2)}, u32[]{:S(2)}) collective-permute-start(f32[64,64]{1,0:T(8,128)S(1)} %add_add_fusion.3), channel_id=1, source_target_pairs={{0,8},{1,9},{2,10},{3,11},{4,12},{5,13},{6,14},{7,15},{8,0},{9,1},... | collective-permute-start | bytes 49160 | tf_op jit(solution)/shard_map/ppermute | solution.py:455

commit v7 on v6

--- a/solution.py
+++ b/solution.py
@@ -200,35 +200,20 @@
     )(coeffs, squares)
 
 
-def pieces_kernel(basis_hbm, top, low, held, loaded):
-    chunk = held.shape[1]
-    count = basis_hbm.shape[0] // chunk
-    copies = [
-        pltpu.make_async_copy(
-            basis_hbm.at[pl.ds(index * chunk, chunk), :], held.at[index % 2], loaded.at[index % 2]
-        )
-        for index in range(count)
-    ]
-    copies[0].start()
-    for index in range(count):
-        if index + 1 < count:
-            copies[index + 1].start()
-        copies[index].wait()
-        here = pl.ds(index * chunk, chunk)
-        top[here, :], low[here, :] = split(held[index % 2], 2)
+def pieces_kernel(basis_ref, top, low):
+    rows = basis_ref.shape[0]
+    chunk = chunk_of(rows)
+    for start in range(0, rows, chunk):
+        here = pl.ds(start, chunk)
+        top[here, :], low[here, :] = split(basis_ref[here, :], 2)
 
 
 def basis_pieces(old_basis):
     rows, modes = old_basis.shape
-    chunk = chunk_of(rows)
     spec = pl.BlockSpec(memory_space=pltpu.VMEM)
     shape = jax.ShapeDtypeStruct((rows, modes), jnp.bfloat16)
     return pl.pallas_call(
-        pieces_kernel, out_shape=(shape, shape),
-        in_specs=[pl.BlockSpec(memory_space=pltpu.HBM)], out_specs=(spec, spec),
-        scratch_shapes=[
-            pltpu.VMEM((2, chunk, modes), jnp.float32), pltpu.SemaphoreType.DMA((2,))
-        ],
+        pieces_kernel, out_shape=(shape, shape), in_specs=[spec], out_specs=(spec, spec),
         compiler_params=pltpu.CompilerParams(vmem_limit_bytes=VMEM),
         cost_estimate=pl.CostEstimate(
             flops=1000 * rows * modes, bytes_accessed=8 * rows * modes, transcendentals=0

time: 83.4 us -> 83.4 us (level)
  transfers between devices with their start and end apart: 22 -> 22, of which waited for: 14 -> 14; matrix products, arithmetic and copies ran while one was open for 0% -> 0% of each run, Pallas kernels for 4% -> 3%
where the time goes in v7:
time: 83.4 us; the launch traced here: 83.2 us
  Pallas kernels  32.6 us (39%)
  starting transfers between devices  28.8 us (35%)
  waiting for transfers between devices  18.2 us (22%)
  local copies, waits for them, and re-layouts  3.15 us (4%)
    pallas_call x1, Pallas kernels, updated_basis(): pl.pallas_call(update_kernel, out_shape=jax.ShapeDtypeStruct((rows, modes...  27.4 us
    ppermute x15, starting transfers between devices, exchange(): return lax.ppermute(part, AXES, [(i, i ^ mask) for i in range(count)])  16.3 us
    ppermute x15, waiting for transfers between devices, exchange(): return lax.ppermute(part, AXES, [(i, i ^ mask) for i in range(count)])  13.8 us
    ppermute x7, starting transfers between devices, exchange_rows(): lax.ppermute(blocks[mask], name, [(i, i ^ mask) for i in range(count)])  12.5 us
    ppermute x7, waiting for transfers between devices, exchange_rows(): lax.ppermute(blocks[mask], name, [(i, i ^ mask) for i in range(count)])  4.34 us
    unnamed x6, local copies, waits for them, and re-layouts  3.15 us
    pallas_call x1, Pallas kernels, opening(): pl.pallas_call(opening_kernel, out_shape=(shape, shape), in_specs=[spec]...  2.18 us
  transfers between devices with their start and end apart: 22, of which 14 were waited for; matrix products, arithmetic and copies ran while one was open for 0% of the time, Pallas kernels for 3%

profile of v7, /device:TPU:0, one launch (start us, length us, event | category | flops | bytes accessed | tf_op | source)
XLA Modules:
  0.0 83.2 jit_solution(1351728721725872212)
XLA Ops:
  0.0 0.0 copy-start.1
  0.0 1.0 %copy-done.1 = f32[8,15360]{1,0:T(8,128)S(1)} copy-done((f32[8,15360]{1,0:T(8,128)S(1)}, f32[8,15360]{1,0:T(8,128)}, u32[]{:S(2)}) %copy-start.1) | copy-done | bytes 491544
  1.1 3.1 %collective-permute-start = (f32[8,1920]{1,0:T(8,128)S(1)}, f32[8,1920]{1,0:T(8,128)S(1)}, u32[]{:S(2)}, u32[]{:S(2)}) collective-permute-start(f32[8,1920]{1,0:T(8,128)S(1)} %get-tuple-element.21), channel_id=1, source_target_pairs={{0,4},{4,0},{8,12},{12,8},{16,20},{20,16},{24,28},{28,24},{1,5},{5... | collective-permute-start | bytes 184328 | tf_op jit(solution)/shard_map/ppermute | solution.py:484
  4.1 1.6 %collective-permute-start.1 = (f32[8,1920]{1,0:T(8,128)S(1)}, f32[8,1920]{1,0:T(8,128)S(1)}, u32[]{:S(2)}, u32[]{:S(2)}) collective-permute-start(f32[8,1920]{1,0:T(8,128)S(1)} %get-tuple-element.22), channel_id=1, source_target_pairs={{0,8},{4,12},{8,0},{12,4},{16,24},{20,28},{24,16},{28,20},{1,9},{5... | collective-permute-start | bytes 184328 | tf_op jit(solution)/shard_map/ppermute | solution.py:484
  5.7 0.0 collective-permute-start.2
  5.7 3.0 %collective-permute-start.3 = (f32[8,1920]{1,0:T(8,128)S(1)}, f32[8,1920]{1,0:T(8,128)S(1)}, u32[]{:S(2)}, u32[]{:S(2)}) collective-permute-start(f32[8,1920]{1,0:T(8,128)S(1)} %get-tuple-element.24), channel_id=1, source_target_pairs={{0,16},{4,20},{8,24},{12,28},{16,0},{20,4},{24,8},{28,12},{1,17},{... | collective-permute-start | bytes 184328 | tf_op jit(solution)/shard_map/ppermute | solution.py:484
  8.7 1.3 %collective-permute-start.4 = (f32[8,1920]{1,0:T(8,128)S(1)}, f32[8,1920]{1,0:T(8,128)S(1)}, u32[]{:S(2)}, u32[]{:S(2)}) collective-permute-start(f32[8,1920]{1,0:T(8,128)S(1)} %get-tuple-element.25), channel_id=1, source_target_pairs={{0,20},{4,16},{8,28},{12,24},{16,4},{20,0},{24,12},{28,8},{1,21},{... | collective-permute-start | bytes 184328 | tf_op jit(solution)/shard_map/ppermute | solution.py:484
  10.0 0.0 collective-permute-done.refs_1_
  10.0 3.6 %collective-permute-start.5 = (f32[8,1920]{1,0:T(8,128)S(1)}, f32[8,1920]{1,0:T(8,128)S(1)}, u32[]{:S(2)}, u32[]{:S(2)}) collective-permute-start(f32[8,1920]{1,0:T(8,128)S(1)} %get-tuple-element.26), channel_id=1, source_target_pairs={{0,24},{4,28},{8,16},{12,20},{16,8},{20,12},{24,0},{28,4},{1,25},{... | collective-permute-start | bytes 184328 | tf_op jit(solution)/shard_map/ppermute | solution.py:484
  13.6 0.0 collective-permute-done.1.refs_2_
  13.6 0.0 collective-permute-start.6
  13.6 0.0 copy-start
  13.6 2.1 %copy-done = f32[1920,512]{1,0:T(8,128)S(1)} copy-done((f32[1920,512]{1,0:T(8,128)S(1)}, f32[1920,512]{1,0:T(8,128)}, u32[]{:S(2)}) %copy-start) | copy-done | bytes 3932184
  15.7 0.5 shard_map.38
  16.3 0.0 collective-permute-done.2.refs_3_
  16.3 0.0 collective-permute-done.3.refs_4_
  16.3 2.1 %collective-permute-done.4.refs_5_ = f32[8,1920]{1,0:T(8,128)S(1)} collective-permute-done((f32[8,1920]{1,0:T(8,128)S(1)}, f32[8,1920]{1,0:T(8,128)S(1)}, u32[]{:S(2)}, u32[]{:S(2)}) %collective-permute-start.4) | collective-permute-done | bytes 61472 | tf_op jit(solution)/shard_map/ppermute | solution.py:484
  18.4 0.0 collective-permute-done.5.refs_6_
  18.4 2.2 %collective-permute-done.6.refs_7_ = f32[8,1920]{1,0:T(8,128)S(1)} collective-permute-done((f32[8,1920]{1,0:T(8,128)S(1)}, f32[8,1920]{1,0:T(8,128)S(1)}, u32[]{:S(2)}, u32[]{:S(2)}) %collective-permute-start.6) | collective-permute-done | bytes 61472 | tf_op jit(solution)/shard_map/ppermute | solution.py:484
  20.6 0.8 shard_map.39
  21.4 0.1 collective-permute-start.7
  21.5 1.2 %collective-permute-done.7 = f32[32,512]{1,0:T(8,128)S(1)} collective-permute-done((f32[32,512]{1,0:T(8,128)S(1)}, f32[32,512]{1,0:T(8,128)S(1)}, u32[]{:S(2)}, u32[]{:S(2)}) %collective-permute-start.7) | collective-permute-done | bytes 65568 | tf_op jit(solution)/shard_map/ppermute | solution.py:440
  22.7 1.5 %collective-permute-start.10 = (f32[32,512]{1,0:T(8,128)S(1)}, f32[32,512]{1,0:T(8,128)S(1)}, u32[]{:S(2)}, u32[]{:S(2)}) collective-permute-start(f32[32,512]{1,0:T(8,128)S(1)} %select_add_fusion), channel_id=1, source_target_pairs={{0,6},{1,7},{2,4},{3,5},{4,2},{5,3},{6,0},{7,1},{8,14},{9,15},{10,... | collective-permute-start | bytes 196616 | tf_op jit(solution)/shard_map/ppermute | solution.py:440
  24.2 1.5 %collective-permute-start.9 = (f32[32,512]{1,0:T(8,128)S(1)}, f32[32,512]{1,0:T(8,128)S(1)}, u32[]{:S(2)}, u32[]{:S(2)}) collective-permute-start(f32[32,512]{1,0:T(8,128)S(1)} %select_add_fusion), channel_id=1, source_target_pairs={{0,4},{1,5},{2,6},{3,7},{4,0},{5,1},{6,2},{7,3},{8,12},{9,13},{10,... | collective-permute-start | bytes 196616 | tf_op jit(solution)/shard_map/ppermute | solution.py:440
  25.8 0.5 collective-permute-start.8
  26.3 1.8 %collective-permute-done.10 = f32[32,512]{1,0:T(8,128)S(1)} collective-permute-done((f32[32,512]{1,0:T(8,128)S(1)}, f32[32,512]{1,0:T(8,128)S(1)}, u32[]{:S(2)}, u32[]{:S(2)}) %collective-permute-start.10) | collective-permute-done | bytes 65568 | tf_op jit(solution)/shard_map/ppermute | solution.py:440
  28.1 1.2 %collective-permute-done.9 = f32[32,512]{1,0:T(8,128)S(1)} collective-permute-done((f32[32,512]{1,0:T(8,128)S(1)}, f32[32,512]{1,0:T(8,128)S(1)}, u32[]{:S(2)}, u32[]{:S(2)}) %collective-permute-start.9) | collective-permute-done | bytes 65568 | tf_op jit(solution)/shard_map/ppermute | solution.py:440
  29.3 0.8 collective-permute-done.8
  30.1 1.2 %collective-permute-start.13 = (f32[32,512]{1,0:T(8,128)S(1)}, f32[32,512]{1,0:T(8,128)S(1)}, u32[]{:S(2)}, u32[]{:S(2)}) collective-permute-start(f32[32,512]{1,0:T(8,128)S(1)} %add_add_fusion.1), channel_id=1, source_target_pairs={{0,24},{1,25},{2,26},{3,27},{4,28},{5,29},{6,30},{7,31},{8,16},{9,... | collective-permute-start | bytes 196616 | tf_op jit(solution)/shard_map/ppermute | solution.py:440
  31.2 1.4 %collective-permute-start.12 = (f32[32,512]{1,0:T(8,128)S(1)}, f32[32,512]{1,0:T(8,128)S(1)}, u32[]{:S(2)}, u32[]{:S(2)}) collective-permute-start(f32[32,512]{1,0:T(8,128)S(1)} %add_add_fusion.1), channel_id=1, source_target_pairs={{0,16},{1,17},{2,18},{3,19},{4,20},{5,21},{6,22},{7,23},{8,24},{9,... | collective-permute-start | bytes 196616 | tf_op jit(solution)/shard_map/ppermute | solution.py:440
  32.6 1.9 %collective-permute-start.11 = (f32[32,512]{1,0:T(8,128)S(1)}, f32[32,512]{1,0:T(8,128)S(1)}, u32[]{:S(2)}, u32[]{:S(2)}) collective-permute-start(f32[32,512]{1,0:T(8,128)S(1)} %add_add_fusion.1), channel_id=1, source_target_pairs={{0,8},{1,9},{2,10},{3,11},{4,12},{5,13},{6,14},{7,15},{8,0},{9,1},... | collective-permute-start | bytes 196616 | tf_op jit(solution)/shard_map/ppermute | solution.py:440
  34.5 2.3 %collective-permute-done.13 = f32[32,512]{1,0:T(8,128)S(1)} collective-permute-done((f32[32,512]{1,0:T(8,128)S(1)}, f32[32,512]{1,0:T(8,128)S(1)}, u32[]{:S(2)}, u32[]{:S(2)}) %collective-permute-start.13) | collective-permute-done | bytes 65568 | tf_op jit(solution)/shard_map/ppermute | solution.py:440
  36.8 1.8 %collective-permute-done.12 = f32[32,512]{1,0:T(8,128)S(1)} collective-permute-done((f32[32,512]{1,0:T(8,128)S(1)}, f32[32,512]{1,0:T(8,128)S(1)}, u32[]{:S(2)}, u32[]{:S(2)}) %collective-permute-start.12) | collective-permute-done | bytes 65568 | tf_op jit(solution)/shard_map/ppermute | solution.py:440
  38.6 0.0 collective-permute-done.11
  38.6 0.1 collective-permute-start.14
  38.7 1.2 %collective-permute-done.14 = f32[32,512]{1,0:T(8,128)S(1)} collective-permute-done((f32[32,512]{1,0:T(8,128)S(1)}, f32[32,512]{1,0:T(8,128)S(1)}, u32[]{:S(2)}, u32[]{:S(2)}) %collective-permute-start.14) | collective-permute-done | bytes 65568 | tf_op jit(solution)/shard_map/ppermute | solution.py:440
  40.0 0.0 copy-start.2
  40.0 1.6 %shard_map.40 = f32[64,64]{1,0:T(8,128)S(1)} custom-call(f32[64,512]{1,0:T(8,128)S(1)} %pad_maximum_fusion.coeffs_ref, f32[64,1920]{1,0:T(8,128)S(1)} %get-tuple-element.31.snaps_ref, bf16[1920,512]{1,0:T(8,128)(2,1)S(1)} %get-tuple-element.28.refs_8_.top_ref, bf16[1920,512]{1,0:T(8,128)(2,1)S(1)} %get-tuple-element.29.refs_9_.low_ref), custom_call_target="tpu_custom_call" | custom-call | tf_op jit(solution)/shard_map/pallas_call | solution.py:290
  41.6 0.2 collective-permute-start.15
  41.8 1.0 %collective-permute-done.15 = f32[64,64]{1,0:T(8,128)S(1)} collective-permute-done((f32[64,64]{1,0:T(8,128)S(1)}, f32[64,64]{1,0:T(8,128)S(1)}, u32[]{:S(2)}, u32[]{:S(2)}) %collective-permute-start.15) | collective-permute-done | bytes 16416 | tf_op jit(solution)/shard_map/ppermute | solution.py:440
  42.9 1.3 %collective-permute-start.18 = (f32[64,64]{1,0:T(8,128)S(1)}, f32[64,64]{1,0:T(8,128)S(1)}, u32[]{:S(2)}, u32[]{:S(2)}) collective-permute-start(f32[64,64]{1,0:T(8,128)S(1)} %add.54), channel_id=1, source_target_pairs={{0,6},{1,7},{2,4},{3,5},{4,2},{5,3},{6,0},{7,1},{8,14},{9,15},{10,... | collective-permute-start | bytes 49160 | tf_op jit(solution)/shard_map/ppermute | solution.py:440
  44.2 0.2 collective-permute-start.17
  44.4 2.0 %collective-permute-start.16 = (f32[64,64]{1,0:T(8,128)S(1)}, f32[64,64]{1,0:T(8,128)S(1)}, u32[]{:S(2)}, u32[]{:S(2)}) collective-permute-start(f32[64,64]{1,0:T(8,128)S(1)} %add.54), channel_id=1, source_target_pairs={{0,2},{1,3},{2,0},{3,1},{4,6},{5,7},{6,4},{7,5},{8,10},{9,11},{10,... | collective-permute-start | bytes 49160 | tf_op jit(solution)/shard_map/ppermute | solution.py:440
  46.4 0.0 copy-done.2
  46.4 1.3 %collective-permute-done.18 = f32[64,64]{1,0:T(8,128)S(1)} collective-permute-done((f32[64,64]{1,0:T(8,128)S(1)}, f32[64,64]{1,0:T(8,128)S(1)}, u32[]{:S(2)}, u32[]{:S(2)}) %collective-permute-start.18) | collective-permute-done | bytes 16416 | tf_op jit(solution)/shard_map/ppermute | solution.py:440
  47.7 0.4 collective-permute-done.17
  48.1 0.2 collective-permute-done.16
  48.3 2.4 %collective-permute-start.21 = (f32[64,64]{1,0:T(8,128)S(1)}, f32[64,64]{1,0:T(8,128)S(1)}, u32[]{:S(2)}, u32[]{:S(2)}) collective-permute-start(f32[64,64]{1,0:T(8,128)S(1)} %add_add_fusion.3), channel_id=1, source_target_pairs={{0,24},{1,25},{2,26},{3,27},{4,28},{5,29},{6,30},{7,31},{8,16},{9,... | collective-permute-start | bytes 49160 | tf_op jit(solution)/shard_map/ppermute | solution.py:440
  50.7 0.0 collective-permute-start.20
  50.7 2.0 %collective-permute-start.19 = (f32[64,64]{1,0:T(8,128)S(1)}, f32[64,64]{1,0:T(8,128)S(1)}, u32[]{:S(2)}, u32[]{:S(2)}) collective-permute-start(f32[64,64]{1,0:T(8,128)S(1)} %add_add_fusion.3), channel_id=1, source_target_pairs={{0,8},{1,9},{2,10},{3,11},{4,12},{5,13},{6,14},{7,15},{8,0},{9,1},... | collective-permute-start | bytes 49160 | tf_op jit(solution)/shard_map/ppermute | solution.py:440
  52.8 2.2 %shard_map.41 = (f32[512,512]{1,0:T(8,128)S(1)}, f32[512,512]{1,0:T(8,128)S(1)}) custom-call(f32[64,512]{1,0:T(8,128)S(1)} %pad_maximum_fusion.coeffs_ref, f32[1,512]{1,0:T(1,128)S(1)} %bitcast.1), custom_call_target="tpu_custom_call" | custom-call | flops 1610612736 | bytes 2097152 | tf_op jit(solution)/shard_map/pallas_call | solution.py:194
  55.0 0.0 collective-permute-done.21
  55.0 0.6 collective-permute-done.20
  55.5 0.0 collective-permute-done.19
  55.6 27.4 %shard_map.42 = bf16[1920,512]{1,0:T(8,128)(2,1)} custom-call(f32[64,512]{1,0:T(8,128)S(1)} %pad_maximum_fusion.coeffs_ref, f32[64,64]{1,0:T(8,128)S(1)} %add_add_fusion.2.gram_ref, f32[1,512]{1,0:T(1,128)S(1)} %bitcast.2, f32[512,512]{1,0:T(8,128)S(1)} %get-tuple-element.33.upper, f32[512,512]{1,0:T(8,128)S(1)} %get-tuple-element.34.square_ref, ...), custom_call_target="tpu_custom_call" | custom-call | tf_op jit(solution)/shard_map/pallas_call | solution.py:422
  (11 shorter events, 0.1 us)
Async XLA Ops:
  0.0 1.0 %copy-start.1 = (f32[8,15360]{1,0:T(8,128)S(1)}, f32[8,15360]{1,0:T(8,128)}, u32[]{:S(2)}) copy-start(f32[8,15360]{1,0:T(8,128)} %snaps_ref.1) | copy-start | bytes 1474564
  1.1 8.9 %collective-permute-start = (f32[8,1920]{1,0:T(8,128)S(1)}, f32[8,1920]{1,0:T(8,128)S(1)}, u32[]{:S(2)}, u32[]{:S(2)}) collective-permute-start(f32[8,1920]{1,0:T(8,128)S(1)} %get-tuple-element.21), channel_id=1, source_target_pairs={{0,4},{4,0},{8,12},{12,8},{16,20},{20,16},{24,28},{28,24},{1,5},{5... | collective-permute-start | bytes 184328 | tf_op jit(solution)/shard_map/ppermute | solution.py:484
  4.1 9.5 %collective-permute-start.1 = (f32[8,1920]{1,0:T(8,128)S(1)}, f32[8,1920]{1,0:T(8,128)S(1)}, u32[]{:S(2)}, u32[]{:S(2)}) collective-permute-start(f32[8,1920]{1,0:T(8,128)S(1)} %get-tuple-element.22), channel_id=1, source_target_pairs={{0,8},{4,12},{8,0},{12,4},{16,24},{20,28},{24,16},{28,20},{1,9},{5... | collective-permute-start | bytes 184328 | tf_op jit(solution)/shard_map/ppermute | solution.py:484
  5.7 10.5 %collective-permute-start.2 = (f32[8,1920]{1,0:T(8,128)S(1)}, f32[8,1920]{1,0:T(8,128)S(1)}, u32[]{:S(2)}, u32[]{:S(2)}) collective-permute-start(f32[8,1920]{1,0:T(8,128)S(1)} %get-tuple-element.23), channel_id=1, source_target_pairs={{0,12},{4,8},{8,4},{12,0},{16,28},{20,24},{24,20},{28,16},{1,13},{... | collective-permute-start | bytes 184328 | tf_op jit(solution)/shard_map/ppermute | solution.py:484
  5.7 10.6 %collective-permute-start.3 = (f32[8,1920]{1,0:T(8,128)S(1)}, f32[8,1920]{1,0:T(8,128)S(1)}, u32[]{:S(2)}, u32[]{:S(2)}) collective-permute-start(f32[8,1920]{1,0:T(8,128)S(1)} %get-tuple-element.24), channel_id=1, source_target_pairs={{0,16},{4,20},{8,24},{12,28},{16,0},{20,4},{24,8},{28,12},{1,17},{... | collective-permute-start | bytes 184328 | tf_op jit(solution)/shard_map/ppermute | solution.py:484
  8.7 9.7 %collective-permute-start.4 = (f32[8,1920]{1,0:T(8,128)S(1)}, f32[8,1920]{1,0:T(8,128)S(1)}, u32[]{:S(2)}, u32[]{:S(2)}) collective-permute-start(f32[8,1920]{1,0:T(8,128)S(1)} %get-tuple-element.25), channel_id=1, source_target_pairs={{0,20},{4,16},{8,28},{12,24},{16,4},{20,0},{24,12},{28,8},{1,21},{... | collective-permute-start | bytes 184328 | tf_op jit(solution)/shard_map/ppermute | solution.py:484
  10.0 8.4 %collective-permute-start.5 = (f32[8,1920]{1,0:T(8,128)S(1)}, f32[8,1920]{1,0:T(8,128)S(1)}, u32[]{:S(2)}, u32[]{:S(2)}) collective-permute-start(f32[8,1920]{1,0:T(8,128)S(1)} %get-tuple-element.26), channel_id=1, source_target_pairs={{0,24},{4,28},{8,16},{12,20},{16,8},{20,12},{24,0},{28,4},{1,25},{... | collective-permute-start | bytes 184328 | tf_op jit(solution)/shard_map/ppermute | solution.py:484
  13.6 7.0 %collective-permute-start.6 = (f32[8,1920]{1,0:T(8,128)S(1)}, f32[8,1920]{1,0:T(8,128)S(1)}, u32[]{:S(2)}, u32[]{:S(2)}) collective-permute-start(f32[8,1920]{1,0:T(8,128)S(1)} %get-tuple-element.27), channel_id=1, source_target_pairs={{0,28},{4,24},{8,20},{12,16},{16,12},{20,8},{24,4},{28,0},{1,29},{... | collective-permute-start | bytes 184328 | tf_op jit(solution)/shard_map/ppermute | solution.py:484
  13.6 2.1 %copy-start = (f32[1920,512]{1,0:T(8,128)S(1)}, f32[1920,512]{1,0:T(8,128)}, u32[]{:S(2)}) copy-start(f32[1920,512]{1,0:T(8,128)} %basis_ref.1) | copy-start | bytes 11796484
  21.4 1.3 %collective-permute-start.7 = (f32[32,512]{1,0:T(8,128)S(1)}, f32[32,512]{1,0:T(8,128)S(1)}, u32[]{:S(2)}, u32[]{:S(2)}) collective-permute-start(f32[32,512]{1,0:T(8,128)S(1)} %slice_select_fusion), channel_id=1, source_target_pairs={{0,1},{1,0},{2,3},{3,2},{4,5},{5,4},{6,7},{7,6},{8,9},{9,8},{10,11... | collective-permute-start | bytes 196616 | tf_op jit(solution)/shard_map/ppermute | solution.py:440
  22.7 5.3 %collective-permute-start.10 = (f32[32,512]{1,0:T(8,128)S(1)}, f32[32,512]{1,0:T(8,128)S(1)}, u32[]{:S(2)}, u32[]{:S(2)}) collective-permute-start(f32[32,512]{1,0:T(8,128)S(1)} %select_add_fusion), channel_id=1, source_target_pairs={{0,6},{1,7},{2,4},{3,5},{4,2},{5,3},{6,0},{7,1},{8,14},{9,15},{10,... | collective-permute-start | bytes 196616 | tf_op jit(solution)/shard_map/ppermute | solution.py:440
  24.2 5.0 %collective-permute-start.9 = (f32[32,512]{1,0:T(8,128)S(1)}, f32[32,512]{1,0:T(8,128)S(1)}, u32[]{:S(2)}, u32[]{:S(2)}) collective-permute-start(f32[32,512]{1,0:T(8,128)S(1)} %select_add_fusion), channel_id=1, source_target_pairs={{0,4},{1,5},{2,6},{3,7},{4,0},{5,1},{6,2},{7,3},{8,12},{9,13},{10,... | collective-permute-start | bytes 196616 | tf_op jit(solution)/shard_map/ppermute | solution.py:440
  25.8 4.3 %collective-permute-start.8 = (f32[32,512]{1,0:T(8,128)S(1)}, f32[32,512]{1,0:T(8,128)S(1)}, u32[]{:S(2)}, u32[]{:S(2)}) collective-permute-start(f32[32,512]{1,0:T(8,128)S(1)} %select_add_fusion), channel_id=1, source_target_pairs={{0,2},{1,3},{2,0},{3,1},{4,6},{5,7},{6,4},{7,5},{8,10},{9,11},{10,... | collective-permute-start | bytes 196616 | tf_op jit(solution)/shard_map/ppermute | solution.py:440
  30.1 6.7 %collective-permute-start.13 = (f32[32,512]{1,0:T(8,128)S(1)}, f32[32,512]{1,0:T(8,128)S(1)}, u32[]{:S(2)}, u32[]{:S(2)}) collective-permute-start(f32[32,512]{1,0:T(8,128)S(1)} %add_add_fusion.1), channel_id=1, source_target_pairs={{0,24},{1,25},{2,26},{3,27},{4,28},{5,29},{6,30},{7,31},{8,16},{9,... | collective-permute-start | bytes 196616 | tf_op jit(solution)/shard_map/ppermute | solution.py:440
  31.2 7.4 %collective-permute-start.12 = (f32[32,512]{1,0:T(8,128)S(1)}, f32[32,512]{1,0:T(8,128)S(1)}, u32[]{:S(2)}, u32[]{:S(2)}) collective-permute-start(f32[32,512]{1,0:T(8,128)S(1)} %add_add_fusion.1), channel_id=1, source_target_pairs={{0,16},{1,17},{2,18},{3,19},{4,20},{5,21},{6,22},{7,23},{8,24},{9,... | collective-permute-start | bytes 196616 | tf_op jit(solution)/shard_map/ppermute | solution.py:440
  32.6 6.0 %collective-permute-start.11 = (f32[32,512]{1,0:T(8,128)S(1)}, f32[32,512]{1,0:T(8,128)S(1)}, u32[]{:S(2)}, u32[]{:S(2)}) collective-permute-start(f32[32,512]{1,0:T(8,128)S(1)} %add_add_fusion.1), channel_id=1, source_target_pairs={{0,8},{1,9},{2,10},{3,11},{4,12},{5,13},{6,14},{7,15},{8,0},{9,1},... | collective-permute-start | bytes 196616 | tf_op jit(solution)/shard_map/ppermute | solution.py:440
  38.6 1.3 %collective-permute-start.14 = (f32[32,512]{1,0:T(8,128)S(1)}, f32[32,512]{1,0:T(8,128)S(1)}, u32[]{:S(2)}, u32[]{:S(2)}) collective-permute-start(f32[32,512]{1,0:T(8,128)S(1)} %add_add_fusion), channel_id=1, source_target_pairs={{0,1},{1,0},{2,3},{3,2},{4,5},{5,4},{6,7},{7,6},{8,9},{9,8},{10,11... | collective-permute-start | bytes 196616 | tf_op jit(solution)/shard_map/ppermute | solution.py:440
  40.0 6.4 %copy-start.2 = (f32[512]{0:T(512)S(1)}, f32[512]{0:T(512)}, u32[]{:S(2)}) copy-start(f32[512]{0:T(512)} %param.5) | copy-start | bytes 6148
  41.6 1.3 %collective-permute-start.15 = (f32[64,64]{1,0:T(8,128)S(1)}, f32[64,64]{1,0:T(8,128)S(1)}, u32[]{:S(2)}, u32[]{:S(2)}) collective-permute-start(f32[64,64]{1,0:T(8,128)S(1)} %shard_map.40), channel_id=1, source_target_pairs={{0,1},{1,0},{2,3},{3,2},{4,5},{5,4},{6,7},{7,6},{8,9},{9,8},{10,11... | collective-permute-start | bytes 49160 | tf_op jit(solution)/shard_map/ppermute | solution.py:440
  42.9 4.8 %collective-permute-start.18 = (f32[64,64]{1,0:T(8,128)S(1)}, f32[64,64]{1,0:T(8,128)S(1)}, u32[]{:S(2)}, u32[]{:S(2)}) collective-permute-start(f32[64,64]{1,0:T(8,128)S(1)} %add.54), channel_id=1, source_target_pairs={{0,6},{1,7},{2,4},{3,5},{4,2},{5,3},{6,0},{7,1},{8,14},{9,15},{10,... | collective-permute-start | bytes 49160 | tf_op jit(solution)/shard_map/ppermute | solution.py:440
  44.2 3.9 %collective-permute-start.17 = (f32[64,64]{1,0:T(8,128)S(1)}, f32[64,64]{1,0:T(8,128)S(1)}, u32[]{:S(2)}, u32[]{:S(2)}) collective-permute-start(f32[64,64]{1,0:T(8,128)S(1)} %add.54), channel_id=1, source_target_pairs={{0,4},{1,5},{2,6},{3,7},{4,0},{5,1},{6,2},{7,3},{8,12},{9,13},{10,... | collective-permute-start | bytes 49160 | tf_op jit(solution)/shard_map/ppermute | solution.py:440
  44.4 3.9 %collective-permute-start.16 = (f32[64,64]{1,0:T(8,128)S(1)}, f32[64,64]{1,0:T(8,128)S(1)}, u32[]{:S(2)}, u32[]{:S(2)}) collective-permute-start(f32[64,64]{1,0:T(8,128)S(1)} %add.54), channel_id=1, source_target_pairs={{0,2},{1,3},{2,0},{3,1},{4,6},{5,7},{6,4},{7,5},{8,10},{9,11},{10,... | collective-permute-start | bytes 49160 | tf_op jit(solution)/shard_map/ppermute | solution.py:440
  48.3 6.6 %collective-permute-start.21 = (f32[64,64]{1,0:T(8,128)S(1)}, f32[64,64]{1,0:T(8,128)S(1)}, u32[]{:S(2)}, u32[]{:S(2)}) collective-permute-start(f32[64,64]{1,0:T(8,128)S(1)} %add_add_fusion.3), channel_id=1, source_target_pairs={{0,24},{1,25},{2,26},{3,27},{4,28},{5,29},{6,30},{7,31},{8,16},{9,... | collective-permute-start | bytes 49160 | tf_op jit(solution)/shard_map/ppermute | solution.py:440
  50.7 4.8 %collective-permute-start.20 = (f32[64,64]{1,0:T(8,128)S(1)}, f32[64,64]{1,0:T(8,128)S(1)}, u32[]{:S(2)}, u32[]{:S(2)}) collective-permute-start(f32[64,64]{1,0:T(8,128)S(1)} %add_add_fusion.3), channel_id=1, source_target_pairs={{0,16},{1,17},{2,18},{3,19},{4,20},{5,21},{6,22},{7,23},{8,24},{9,... | collective-permute-start | bytes 49160 | tf_op jit(solution)/shard_map/ppermute | solution.py:440
  50.7 4.8 %collective-permute-start.19 = (f32[64,64]{1,0:T(8,128)S(1)}, f32[64,64]{1,0:T(8,128)S(1)}, u32[]{:S(2)}, u32[]{:S(2)}) collective-permute-start(f32[64,64]{1,0:T(8,128)S(1)} %add_add_fusion.3), channel_id=1, source_target_pairs={{0,8},{1,9},{2,10},{3,11},{4,12},{5,13},{6,14},{7,15},{8,0},{9,1},... | collective-permute-start | bytes 49160 | tf_op jit(solution)/shard_map/ppermute | solution.py:440
